TPU v7x, 512 devices: a whole 4x8x8 slice. The times are simulated.
512 devices in a mesh: tok: 64 (over y, z), tp: 8 (over x, core).
Axes of the slice: x: 4, y: 8, z: 8, core: 2. Of those that a mesh axis runs over, the one named last changes fastest.
Arguments:
- hidden: bfloat16 [6144, 8192], P('tok'), may hold values from -2600 to 2600
- norm_gain: float32 [8192], replicated, may hold values from 0.5 to 1.5
- w_query: bfloat16 [8192, 4096], P('tok', 'tp'), may hold values from -1 to 1
- w_key: bfloat16 [8192, 1024], P('tok', 'tp'), may hold values from -1 to 1
- w_value: bfloat16 [8192, 1024], P('tok', 'tp'), may hold values from -0.0625 to 0.0625
- doc_ids: int32 [6144], P('tok'), may hold values from 0 to 3, as said below
Outputs:
- attended: bfloat16 [6144, 4096], P('tok', 'tp')
- out_scale: float32 [4096], P('tp')
- folded_gain: float32 [8192], P(('tok', 'tp'))
- codes_query: float32 [8192, 4096], P(('tok', 'tp'))
- codes_key: float32 [8192, 1024], P(('tok', 'tp'))
- codes_value: float32 [8192, 1024], P(('tok', 'tp'))
- scale_query: float32 [4096], P('tp')
- scale_key: float32 [1024], P('tp')
- scale_value: float32 [1024], P('tp')
Inputs may be any that keep to these rules, and one draw needn't show every extreme that they name: doc_ids never falls along the tokens; each of the 4 documents holds 1 to 4608 tokens and one holds exactly 4608.
All inputs are finite; a program needn't handle non-finite values. Where the computation divides by a largest or mean magnitude, that divisor is 1e-20 or more.
Results may differ from a plain program's by a relative error of at most 0.005.
The roundings to bfloat16 on the way count: a program that leaves them out, or rounds other values in their place, can miss the bound.
Values may be sent and summed in bfloat16 or wider, within the bound.
No kernel may reach another device: no remote copies, remote signals or barrier semaphores. Data moves between devices by JAX's collectives and lax.ppermute only.
A program may use at most 64 MiB of HBM per device.

v0:
```python
import functools
import math

import jax
import jax.numpy as jnp
from jax import lax
from jax.sharding import Mesh
from jax.sharding import PartitionSpec as P

HEAD = 128
KVH = 8
QHEADS = 32
TOK = ("tok_0", "tok_1")
TOK_TP = ("tok_0", "tok_1", "tp")


def over_pieces(shard, axis):
    tiles = lax.all_gather(shard, axis)
    return tiles.max(axis=0)


def side_by_side(arrays, axis, dim, along):
    widths = [a.shape[along] for a in arrays]
    both = jnp.concatenate(arrays, axis=along)
    whole = lax.all_gather(both, axis, axis=dim, tiled=True)
    return tuple(jnp.split(whole, [sum(widths[:k]) for k in range(1, len(widths))], axis=along))


def from_everyone(shard, axis):
    copies = jnp.broadcast_to(shard, (lax.axis_size(axis), *shard.shape))
    return lax.all_to_all(copies, axis, split_axis=0, concat_axis=0, tiled=True)


def of_everyone(shard, axis):
    return from_everyone(shard, axis).max(axis=0)


def one_axis_at_a_time(shard, axes):
    return functools.reduce(lax.pmax, axes, shard)


def shortened(shard):

    def short(part):
        return part.astype(jnp.bfloat16) if part.dtype == jnp.float32 else part

    return jax.tree.map(short, shard)


def rotate(states, positions):
    half = states.shape[-1] // 2
    inverse = jnp.exp(
        jnp.arange(half, dtype=jnp.float32) * (-2.0 * math.log(10000.0) / states.shape[-1])
    )
    angles = positions[:, None] * inverse[None, :]
    cosine = jnp.cos(angles)[:, None, :]
    sine = jnp.sin(angles)[:, None, :]
    first = states[..., :half]
    second = states[..., half:]
    return jnp.concatenate(
        [first * cosine - second * sine, second * cosine + first * sine], axis=-1
    )


def smooth_from(input_peak, weight_peak):
    return jnp.sqrt(jnp.maximum(input_peak, 1e-05)) / jnp.sqrt(jnp.maximum(weight_peak, 1e-05))


def on_device(hidden, norm_gain, w_query, w_key, w_value, doc_ids):
    tok_dev = hidden.shape[0]
    row_count = w_query.shape[0]
    tp_count = lax.axis_size("tp")
    tok_index = lax.axis_index(TOK)
    tp_index = lax.axis_index("tp")
    heads_here = w_query.shape[1] // HEAD
    kv_here = w_key.shape[1] // HEAD
    group_size = QHEADS // KVH
    matrices = (w_query, w_key, w_value)
    states = hidden.astype(jnp.float32)
    normed = (
        states
        * lax.rsqrt(jnp.mean(states * states, axis=1, keepdims=True) + 1e-05)
        * norm_gain[None, :]
    ).astype(jnp.bfloat16)
    input_peak = over_pieces(
        jnp.max(jnp.abs(normed), axis=0).astype(jnp.float32).astype(jnp.bfloat16), TOK
    ).astype(jnp.float32)
    gathered = side_by_side((w_query, w_key, w_value), TOK, 0, 1)
    projected = tuple(
        (jnp.dot(normed, matrix, preferred_element_type=jnp.float32) for matrix in gathered)
    )
    local_peak = jnp.max(
        jnp.stack([jnp.max(jnp.abs(matrix), axis=1) for matrix in gathered]), axis=0
    ).astype(jnp.float32)
    row_peak = of_everyone(local_peak.astype(jnp.bfloat16), "tp").astype(local_peak.dtype)
    smooth_all = smooth_from(input_peak, row_peak)
    smoothing_rows = lax.dynamic_slice_in_dim(smooth_all, tok_index * row_count, row_count)
    scales = tuple(
        (
            jnp.maximum(
                jnp.max(jnp.abs(smooth_all[:, None] * matrix.astype(jnp.float32)), axis=0), 1e-05
            )
            / 127.0
            for matrix in gathered
        )
    )
    query_positions = tok_index * tok_dev + jnp.arange(tok_dev, dtype=jnp.int32)
    positions = query_positions.astype(jnp.float32)
    query = (
        rotate(projected[0].reshape(tok_dev, heads_here, HEAD), positions)
        .astype(jnp.bfloat16)
        .reshape(tok_dev, kv_here, group_size, HEAD)
    )
    key = (
        rotate(projected[1].reshape(tok_dev, kv_here, HEAD), positions)
        .astype(jnp.bfloat16)
        .reshape(tok_dev, kv_here * HEAD)
    )
    value = projected[2].astype(jnp.bfloat16)
    score_scale = 1.0 / math.sqrt(HEAD)
    highest = jnp.full((kv_here, group_size, tok_dev), -1e30, jnp.float32)
    key_block, value_block, doc_block = (
        *side_by_side((key, value), TOK, 0, 1),
        lax.all_gather(doc_ids, TOK, axis=0, tiled=True),
    )
    length = key_block.shape[0]
    scores = (
        jnp.einsum(
            "tkgd,skd->kgts",
            query,
            key_block.reshape(length, kv_here, HEAD),
            preferred_element_type=jnp.float32,
        )
        * score_scale
    )
    key_positions = jnp.arange(length, dtype=jnp.int32)
    allowed = (doc_ids[:, None] == doc_block[None, :]) & (
        key_positions[None, :] <= query_positions[:, None]
    )
    scores = jnp.where(allowed, scores, -1e30)
    raised = jnp.maximum(highest, jnp.max(scores, axis=3))
    weights = jnp.where(allowed, jnp.exp(scores - raised[..., None]), 0.0)
    totals = jnp.sum(weights, axis=3)
    accumulated = jnp.einsum(
        "kgts,skd->kgtd",
        weights.astype(jnp.bfloat16),
        value_block.reshape(length, kv_here, HEAD),
        preferred_element_type=jnp.float32,
    )
    highest, totals, accumulated = (raised, totals, accumulated)
    attended = (
        (accumulated / totals[..., None])
        .transpose(2, 0, 1, 3)
        .reshape(tok_dev, heads_here * HEAD)
        .astype(jnp.bfloat16)
    )
    out_scale = one_axis_at_a_time(jnp.max(jnp.abs(attended), axis=0).astype(jnp.float32), TOK)
    sub_rows = row_count // tp_count
    smooth_part = lax.dynamic_slice_in_dim(smoothing_rows, tp_index * sub_rows, sub_rows)
    gain_part = lax.dynamic_slice_in_dim(
        norm_gain, tok_index * row_count + tp_index * sub_rows, sub_rows
    )
    folded_gain = gain_part / smooth_part
    blocks = tuple(
        (
            smoothing_rows[:, None] * matrix.astype(jnp.float32) / column_scale[None, :]
            for matrix, column_scale in zip(matrices, scales)
        )
    )
    codes = jax.tree.map(
        lambda part, own: part.astype(own.dtype),
        lax.all_to_all(shortened(blocks), "tp", split_axis=0, concat_axis=1, tiled=True),
        blocks,
    )
    return (
        attended,
        out_scale,
        folded_gain,
        codes[0],
        codes[1],
        codes[2],
        scales[0],
        scales[1],
        scales[2],
    )


def solution(mesh):
    split = Mesh(mesh.devices.reshape(8, 8, mesh.shape["tp"]), ("tok_0", "tok_1", "tp"))
    placed = (P(TOK, None), P(), P(TOK, "tp"), P(TOK, "tp"), P(TOK, "tp"), P(TOK))
    return jax.shard_map(
        on_device,
        mesh=split,
        in_specs=placed,
        out_specs=(
            P(TOK, "tp"),
            P("tp"),
            P(TOK_TP),
            P(TOK_TP, None),
            P(TOK_TP, None),
            P(TOK_TP, None),
            P("tp"),
            P("tp"),
            P("tp"),
        ),
        check_vma=False,
    )
```

profile of v0, /device:TPU:2, one launch (start us, length us, event | category | flops | bytes accessed | tf_op | source)
XLA Modules:
  0.0 434.4 jit_solution(10533357328130817659)
XLA Ops:
  7.3 1.7 pad_maximum_fusion
  9.1 1.8 fusion.10
  10.9 1.9 abs_reduce_fusion.6
  12.9 1.3 dynamic-slice
  14.8 0.3 dynamic-update-slice
  15.1 288.8 %all-reduce = s32[6144]{0:T(1024)S(1)} all-reduce(s32[6144]{0:T(1024)S(1)} %dynamic-update-slice), channel_id=1, replica_groups=mesh['tok_0'=8,'tok_1'=8,'tp'=8] {'tok_0','tok_1'}, use_global_device_ids=true, to_apply=%add | all-reduce | flops 6144 | bytes 49152
  303.9 2.2 fusion.18
  306.2 0.3 fusion.42
  306.4 2.2 fusion.21
  308.7 0.7 pad_maximum_fusion.1
  309.4 0.5 fusion.13
  310.0 0.2 multiply_cosine_fusion
  310.2 1.5 reshape.251
  311.8 0.2 reduce_max.112
  312.0 4.9 %fusion.2 = f32[96,512]{1,0:T(8,128)S(1)} fusion(bf16[8192,768]{1,0:T(8,128)(2,1)} %all-gather.5.cloned.1.call-done, bf16[96,8192]{1,0:T(8,128)(2,1)S(1)} %copy-done, f32[8192]{0:T(1024)S(1)} %copy-done.4, f32[96]{0:T(128)S(1)} %add_rsqrt_fusion), kind=kOutput, calls=%fused_computation.6 | convolution fusion | flops 808452096 | bytes 10191232 | tf_op jit(solution)/shard_map/dot_general | solution.py:90
  316.9 0.1 reshape.245
  317.0 3.7 abs_reduce_fusion.5
  320.6 5.3 %abs_reduce_fusion.1 = bf16[8192]{0:T(1024)(128)(2,1)S(1)} fusion(bf16[8192,768]{1,0:T(8,128)(2,1)} %all-gather.5.cloned.1.call-done), kind=kLoop, calls=%fused_computation.3 | loop fusion | flops 8380416 | bytes 8404992 | tf_op jit(solution)/shard_map/reduce_max | solution.py:93
  326.0 0.1 broadcast_in_dim.18
  326.1 0.5 broadcast.167
  326.6 1.4 reduce.9
  328.0 0.7 reshape.259
  328.8 5.3 %all-to-all-start = ((bf16[8,2,4096]{2,1,0:T(2,128)(2,1)}), bf16[8,2,4096]{2,1,0:T(2,128)(2,1)S(1)}, u32[]{:S(2)}, u32[]{:S(2)}) async-start(bf16[8,2,4096]{2,1,0:T(2,128)(2,1)} %reshape.259), calls=%async_computation | async-start | bytes 262144 | tf_op jit(solution)/shard_map/all_to_all | solution.py:31
  334.1 0.2 fusion.49
  334.3 4.4 %all-to-all-done = bf16[8,2,4096]{2,1,0:T(2,128)(2,1)S(1)} async-done(((bf16[8,2,4096]{2,1,0:T(2,128)(2,1)}), bf16[8,2,4096]{2,1,0:T(2,128)(2,1)S(1)}, u32[]{:S(2)}, u32[]{:S(2)}) %all-to-all-start) | async-done | bytes 131104 | tf_op jit(solution)/shard_map/all_to_all | solution.py:31
  338.7 0.1 reshape.260
  338.8 0.3 reduce_max.118
  339.2 0.1 dynamic_slice.14
  339.2 5.0 %abs_reduce_fusion.2 = (f32[128]{0:T(128)S(1)}, f32[128]{0:T(128)S(1)}) fusion(f32[8192]{0:T(1024)S(1)} %rsqrt_multiply_fusion, bf16[8192,768]{1,0:T(8,128)(2,1)} %all-gather.5.cloned.1.call-done), kind=kLoop, calls=%fused_computation.13 | loop fusion | flops 8388352 | bytes 4228096 | tf_op jit(solution)/shard_map/reduce_max | solution.py:101
  344.3 0.7 divide_convert_fusion.1
  345.0 4.7 %all-to-all-start.3 = ((bf16[8,16,128]{2,1,0:T(8,128)(2,1)}), bf16[8,16,128]{2,1,0:T(8,128)(2,1)S(1)}, u32[]{:S(2)}, u32[]{:S(2)}) async-start(bf16[8,16,128]{2,1,0:T(8,128)(2,1)} %bitcast.16), calls=%async_computation.3 | async-start | bytes 65536 | tf_op jit(solution)/shard_map/all_to_all | solution.py:172
  349.7 5.0 %abs_reduce_fusion = f32[512]{0:T(512)S(1)} fusion(f32[8192]{0:T(1024)S(1)} %rsqrt_multiply_fusion, bf16[8192,768]{1,0:T(8,128)(2,1)} %all-gather.5.cloned.1.call-done), kind=kLoop, calls=%fused_computation | loop fusion | flops 16776704 | bytes 8423424 | tf_op jit(solution)/shard_map/reduce_max | solution.py:101
  354.8 0.8 divide_convert_fusion
  355.5 0.6 dynamic-slice_divide_fusion
  356.1 4.8 %all-to-all-start.2 = ((bf16[8,16,128]{2,1,0:T(8,128)(2,1)}), bf16[8,16,128]{2,1,0:T(8,128)(2,1)S(1)}, u32[]{:S(2)}, u32[]{:S(2)}) async-start(bf16[8,16,128]{2,1,0:T(8,128)(2,1)} %bitcast.14), calls=%async_computation.2 | async-start | bytes 65536 | tf_op jit(solution)/shard_map/all_to_all | solution.py:172
  360.9 0.6 copy_bitcast_fusion.1
  361.6 3.4 all-to-all-done.2
  364.9 4.7 %all-to-all-start.1 = ((bf16[8,16,512]{2,1,0:T(8,128)(2,1)}), bf16[8,16,512]{2,1,0:T(8,128)(2,1)S(1)}, u32[]{:S(2)}, u32[]{:S(2)}) async-start(bf16[8,16,512]{2,1,0:T(8,128)(2,1)} %bitcast.12), calls=%async_computation.1 | async-start | bytes 262144 | tf_op jit(solution)/shard_map/all_to_all | solution.py:172
  369.7 0.6 copy_bitcast_fusion.2
  370.3 4.0 all-to-all-done.1
  374.4 0.7 copy.51
  375.1 12.6 %all-gather.7.cloned.1.call-done = bf16[6144,256]{1,0:T(8,128)(2,1)} async-done(((bf16[96,256]{1,0:T(8,128)(2,1)}), bf16[6144,256]{1,0:T(8,128)(2,1)}) %all-gather.7.cloned.1.call-update) | async-done | bytes 3145744 | tf_op jit(solution)/shard_map/all_gather | solution.py:25
  387.7 3.3 fusion.50
  391.1 2.2 fusion
  393.3 1.7 abs_reduce_fusion.7
  395.0 0.7 copy.62
  395.7 16.0 %pmax.14 = f32[512]{0:T(512)S(1)} all-reduce(f32[512]{0:T(512)S(1)} %bitcast_convert_fusion), channel_id=1, replica_groups=mesh['tok_0'=8,'tok_1'=8,'tp'=8] {'tok_0'}, use_global_device_ids=true, to_apply=%region_4.0 | all-reduce | flops 512 | bytes 4096 | tf_op jit(solution)/shard_map/pmax | solution.py:39
  411.6 16.2 %pmax.15 = f32[512]{0:T(512)} all-reduce(f32[512]{0:T(512)S(1)} %pmax.14), channel_id=1, replica_groups=mesh['tok_0'=8,'tok_1'=8,'tp'=8] {'tok_1'}, use_global_device_ids=true, to_apply=%region_5.0 | all-reduce | flops 512 | bytes 4096 | tf_op jit(solution)/shard_map/pmax | solution.py:39
  (43 shorter events, 0.5 us)
Async XLA Ops:
  7.2 3.7 copy-start
  7.2 296.7 %copy-start.4 = (f32[8192]{0:T(1024)S(1)}, f32[8192]{0:T(1024)}, u32[]{:S(2)}) copy-start(f32[8192]{0:T(1024)} %param.7) | copy-start | bytes 98308
  7.2 7.6 %copy-start.8 = (s32[96]{0:T(128)S(1)}, s32[96]{0:T(128)}, u32[]{:S(2)}) copy-start(s32[96]{0:T(128)} %param.11) | copy-start | bytes 1156
  7.2 296.7 %all-gather.5.cloned.1.call-start = ((), (), s32[]{:S(2)}) async-start(), calls=%async_computation.4 | async-start | bytes 12779520 | tf_op jit(solution)/shard_map/all_gather | solution.py:25
  9.0 301.2 %all-gather.9.cloned.1.call-start = ((), (), s32[]{:S(2)}) async-start(), calls=%async_computation.6 | async-start | bytes 1064960 | tf_op jit(solution)/shard_map/all_gather | solution.py:18
  12.8 374.9 %all-gather.7.cloned.1.call-start = ((), (), s32[]{:S(2)}) async-start(), calls=%async_computation.5 | async-start | bytes 3194880 | tf_op jit(solution)/shard_map/all_gather | solution.py:25
  328.8 9.9 %all-to-all-start = ((bf16[8,2,4096]{2,1,0:T(2,128)(2,1)}), bf16[8,2,4096]{2,1,0:T(2,128)(2,1)S(1)}, u32[]{:S(2)}, u32[]{:S(2)}) async-start(bf16[8,2,4096]{2,1,0:T(2,128)(2,1)} %reshape.259), calls=%async_computation | async-start | bytes 262144 | tf_op jit(solution)/shard_map/all_to_all | solution.py:31
  334.1 10.2 %copy-start.2 = (bf16[128,128]{1,0:T(8,128)(2,1)S(1)}, bf16[128,128]{1,0:T(8,128)(2,1)}, u32[]{:S(2)}) copy-start(bf16[128,128]{1,0:T(8,128)(2,1)} %param.10) | copy-start | bytes 98308
  334.1 10.2 %copy-start.3 = (bf16[128,128]{1,0:T(8,128)(2,1)S(1)}, bf16[128,128]{1,0:T(8,128)(2,1)}, u32[]{:S(2)}) copy-start(bf16[128,128]{1,0:T(8,128)(2,1)} %param.9) | copy-start | bytes 98308
  344.2 10.5 %copy-start.6 = (f32[128]{0:T(128)}, f32[128]{0:T(128)S(1)}, u32[]{:S(2)}) copy-start(f32[128]{0:T(128)S(1)} %get-tuple-element.27) | copy-start | bytes 1540
  344.2 10.5 %copy-start.7 = (f32[128]{0:T(128)}, f32[128]{0:T(128)S(1)}, u32[]{:S(2)}) copy-start(f32[128]{0:T(128)S(1)} %get-tuple-element.28) | copy-start | bytes 1540
  345.0 11.1 %all-to-all-start.3 = ((bf16[8,16,128]{2,1,0:T(8,128)(2,1)}), bf16[8,16,128]{2,1,0:T(8,128)(2,1)S(1)}, u32[]{:S(2)}, u32[]{:S(2)}) async-start(bf16[8,16,128]{2,1,0:T(8,128)(2,1)} %bitcast.16), calls=%async_computation.3 | async-start | bytes 65536 | tf_op jit(solution)/shard_map/all_to_all | solution.py:172
  349.7 5.1 %copy-start.1 = (bf16[128,512]{1,0:T(8,128)(2,1)S(1)}, bf16[128,512]{1,0:T(8,128)(2,1)}, u32[]{:S(2)}) copy-start(bf16[128,512]{1,0:T(8,128)(2,1)} %param.8) | copy-start | bytes 393220
  354.8 36.3 %copy-start.5 = (f32[512]{0:T(512)}, f32[512]{0:T(512)S(1)}, u32[]{:S(2)}) copy-start(f32[512]{0:T(512)S(1)} %maximum_multiply_fusion) | copy-start | bytes 6148
  356.1 8.8 %all-to-all-start.2 = ((bf16[8,16,128]{2,1,0:T(8,128)(2,1)}), bf16[8,16,128]{2,1,0:T(8,128)(2,1)S(1)}, u32[]{:S(2)}, u32[]{:S(2)}) async-start(bf16[8,16,128]{2,1,0:T(8,128)(2,1)} %bitcast.14), calls=%async_computation.2 | async-start | bytes 65536 | tf_op jit(solution)/shard_map/all_to_all | solution.py:172
  364.9 9.4 %all-to-all-start.1 = ((bf16[8,16,512]{2,1,0:T(8,128)(2,1)}), bf16[8,16,512]{2,1,0:T(8,128)(2,1)S(1)}, u32[]{:S(2)}, u32[]{:S(2)}) async-start(bf16[8,16,512]{2,1,0:T(8,128)(2,1)} %bitcast.12), calls=%async_computation.1 | async-start | bytes 262144 | tf_op jit(solution)/shard_map/all_to_all | solution.py:172
  391.1 2.2 copy-start.9
Sparse Core Ops, SparseCore 0:
  11.7 125.3 all-gather.4
  140.7 80.1 all-gather.8
  309.5 78.1 all-gather.6
where the time goes:
time: 435 us; the launch traced here: 434 us
  blocking collectives  321 us (74%)
  other arithmetic  33.7 us (8%)
  waiting for transfers between devices  24.5 us (6%)
  starting transfers between devices  19.7 us (5%)
  between operations  14.7 us (3%)
  matrix products  14.4 us (3%)
  local copies, waits for them, and re-layouts  6.39 us (1%)
    unnamed x1, blocking collectives  289 us
    pmax x2, blocking collectives, one_axis_at_a_time(): return functools.reduce(lax.pmax, axes, shard)  32.2 us
    all_to_all x3, starting transfers between devices, on_device(): lax.all_to_all(shortened(blocks), 'tp', split_axis=0, concat_axis=1, tile...  14.3 us
    all_gather x2, waiting for transfers between devices, side_by_side(): whole = lax.all_gather(both, axis, axis=dim, tiled=True)  12.6 us
    reduce_max x2, other arithmetic, on_device(): jnp.max(jnp.abs(smooth_all[:, None] * matrix.astype(jnp.float32)), axis=0)  9.99 us
    dot_general x3, matrix products, on_device(): jnp.dot(normed, matrix, preferred_element_type=jnp.float32)  9.38 us
    reduce_max x2, other arithmetic, on_device(): jnp.max(jnp.abs(matrix), axis=1)  8.98 us
  transfers between devices with their start and end apart: 7, of which 4 were waited for; matrix products, arithmetic and copies ran while one was open for 10% of the time, Pallas kernels for 0%

commit v1 on v0

v1 whole, which is shorter than its diff:
```python
import math

import jax
import jax.numpy as jnp
from jax import lax
from jax.sharding import Mesh
from jax.sharding import PartitionSpec as P

HEAD = 128
KVH = 8
QHEADS = 32
TOK = ("tok_0", "tok_1")
TOK_TP = ("tok_0", "tok_1", "tp")


def exchange(parts, axis):
    return lax.all_to_all(parts, axis, split_axis=0, concat_axis=0, tiled=True)


def to_everyone(shard, axis):
    return exchange(jnp.broadcast_to(shard, (lax.axis_size(axis), *shard.shape)), axis)


def rotate(states, positions):
    half = states.shape[-1] // 2
    inverse = jnp.exp(
        jnp.arange(half, dtype=jnp.float32) * (-2.0 * math.log(10000.0) / states.shape[-1])
    )
    angles = positions[:, None] * inverse[None, :]
    cosine = jnp.cos(angles)[:, None, :]
    sine = jnp.sin(angles)[:, None, :]
    first = states[..., :half]
    second = states[..., half:]
    return jnp.concatenate(
        [first * cosine - second * sine, second * cosine + first * sine], axis=-1
    )


def smooth_from(input_peak, weight_peak):
    return jnp.sqrt(jnp.maximum(input_peak, 1e-05)) / jnp.sqrt(jnp.maximum(weight_peak, 1e-05))


def on_device(hidden, norm_gain, w_query, w_key, w_value, doc_ids):
    tok_dev, width = hidden.shape
    row_count = w_query.shape[0]
    tok_count = lax.axis_size(TOK)
    tp_count = lax.axis_size("tp")
    tok_index = lax.axis_index(TOK)
    tp_index = lax.axis_index("tp")
    sub_rows = row_count // tp_count
    widths = (w_query.shape[1], w_key.shape[1], w_value.shape[1])
    cuts = (widths[0], widths[0] + widths[1])
    columns = sum(widths)
    heads_here = widths[0] // HEAD
    kv_here = widths[1] // HEAD
    group_size = QHEADS // KVH

    block = jnp.concatenate((w_query, w_key, w_value), axis=1)
    gathered = lax.all_gather(block, TOK, axis=0, tiled=True)

    states = hidden.astype(jnp.float32)
    inverse_rms = lax.rsqrt(jnp.mean(states * states, axis=1, keepdims=True) + 1e-05)
    normed = (states * inverse_rms * norm_gain[None, :]).astype(jnp.bfloat16)

    peaks = jnp.max(jnp.abs(normed), axis=0).reshape(tok_count, row_count)
    docs = jnp.broadcast_to(doc_ids.astype(jnp.bfloat16), (tok_count, tok_dev))
    arrived = exchange(jnp.concatenate((peaks, docs), axis=1), TOK)
    input_peak = jnp.max(arrived[:, :row_count], axis=0).astype(jnp.float32)
    doc_block = arrived[:, row_count:].astype(jnp.int32).reshape(tok_count * tok_dev)

    row_peak = jnp.max(jnp.abs(block), axis=1)
    sent = jnp.concatenate(
        (
            block.reshape(tp_count, sub_rows * columns),
            jnp.broadcast_to(row_peak, (tp_count, row_count)),
        ),
        axis=1,
    )
    rows = exchange(sent, "tp")
    weight_peak = jnp.max(rows[:, sub_rows * columns :], axis=0).astype(jnp.float32)
    own_rows = rows[:, : sub_rows * columns].reshape(tp_count, sub_rows, columns)

    smoothing = smooth_from(input_peak, weight_peak)
    column_peak = jnp.max(jnp.abs(smoothing[:, None] * block.astype(jnp.float32)), axis=0)
    column_peak = jnp.max(to_everyone(column_peak, TOK), axis=0)
    scale = jnp.maximum(column_peak, 1e-05) / 127.0
    all_scales = to_everyone(scale, "tp")
    scales = jnp.split(scale, cuts)

    smooth_part = lax.dynamic_slice_in_dim(smoothing, tp_index * sub_rows, sub_rows)
    gain_part = lax.dynamic_slice_in_dim(
        norm_gain, tok_index * row_count + tp_index * sub_rows, sub_rows
    )
    folded_gain = gain_part / smooth_part
    coded = (
        smooth_part[None, :, None] * own_rows.astype(jnp.float32) / all_scales[:, None, :]
    )
    codes = tuple(
        part.transpose(1, 0, 2).reshape(sub_rows, tp_count * part.shape[2])
        for part in jnp.split(coded, cuts, axis=2)
    )

    held_gain = jnp.where(all_scales[0, 0] > 0.0, norm_gain, 0.0)
    held = (states * inverse_rms * held_gain[None, :]).astype(jnp.bfloat16)
    projected = jnp.split(
        jnp.dot(held, gathered, preferred_element_type=jnp.float32), cuts, axis=1
    )
    query_positions = tok_index * tok_dev + jnp.arange(tok_dev, dtype=jnp.int32)
    positions = query_positions.astype(jnp.float32)
    query = (
        rotate(projected[0].reshape(tok_dev, heads_here, HEAD), positions)
        .astype(jnp.bfloat16)
        .reshape(tok_dev, kv_here, group_size, HEAD)
    )
    key = (
        rotate(projected[1].reshape(tok_dev, kv_here, HEAD), positions)
        .astype(jnp.bfloat16)
        .reshape(tok_dev, kv_here * HEAD)
    )
    value = projected[2].astype(jnp.bfloat16)

    both = jnp.concatenate((key, value), axis=1)
    line = to_everyone(both, "tok_1").reshape(-1, both.shape[1])
    everything = lax.all_gather(line, "tok_0", axis=0, tiled=True)
    key_block, value_block = jnp.split(everything, (widths[1],), axis=1)

    length = key_block.shape[0]
    scores = jnp.einsum(
        "tkgd,skd->kgts",
        query,
        key_block.reshape(length, kv_here, HEAD),
        preferred_element_type=jnp.float32,
    ) * (1.0 / math.sqrt(HEAD))
    key_positions = jnp.arange(length, dtype=jnp.int32)
    allowed = (doc_ids[:, None] == doc_block[None, :]) & (
        key_positions[None, :] <= query_positions[:, None]
    )
    scores = jnp.where(allowed, scores, -1e30)
    highest = jnp.max(scores, axis=3, keepdims=True)
    weights = jnp.where(allowed, jnp.exp(scores - highest), 0.0)
    totals = jnp.sum(weights, axis=3)
    accumulated = jnp.einsum(
        "kgts,skd->kgtd",
        weights.astype(jnp.bfloat16),
        value_block.reshape(length, kv_here, HEAD),
        preferred_element_type=jnp.float32,
    )
    attended = (
        (accumulated / totals[..., None])
        .transpose(2, 0, 1, 3)
        .reshape(tok_dev, heads_here * HEAD)
        .astype(jnp.bfloat16)
    )
    out_peak = to_everyone(jnp.max(jnp.abs(attended), axis=0), TOK)
    out_scale = jnp.max(out_peak, axis=0).astype(jnp.float32)
    return (
        attended,
        out_scale,
        folded_gain,
        codes[0],
        codes[1],
        codes[2],
        scales[0],
        scales[1],
        scales[2],
    )


def solution(mesh):
    split = Mesh(mesh.devices.reshape(8, 8, mesh.shape["tp"]), ("tok_0", "tok_1", "tp"))
    placed = (P(TOK, None), P(), P(TOK, "tp"), P(TOK, "tp"), P(TOK, "tp"), P(TOK))
    return jax.shard_map(
        on_device,
        mesh=split,
        in_specs=placed,
        out_specs=(
            P(TOK, "tp"),
            P("tp"),
            P(TOK_TP),
            P(TOK_TP, None),
            P(TOK_TP, None),
            P(TOK_TP, None),
            P("tp"),
            P("tp"),
            P("tp"),
        ),
        check_vma=False,
    )
```

time: 435 us -> 245 us (0.56)
  blocking collectives: 321 us -> 20.7 us
  waiting for transfers between devices: 24.5 us -> 132 us
  other arithmetic: 33.7 us -> 11 us
  starting transfers between devices: 19.7 us -> 41.7 us
  local copies, waits for them, and re-layouts: 6.39 us -> 12.1 us
    unnamed x1 -> x0, blocking collectives: 289 us -> none
    all_gather x3 -> x2, waiting for transfers between devices: 12.6 us -> 88.1 us  [the longest x1 50.7 us: on_device(): gathered = lax.all_gather(block, TOK, axis=0, tiled=True)]
    all_to_all x4 -> x5, waiting for transfers between devices: 11.8 us -> 44.2 us  [exchange(): return lax.all_to_all(parts, axis, split_axis=0, concat_axis=0, tiled=True)]
    pmax x2 -> x0, blocking collectives: 32.2 us -> none  [one_axis_at_a_time(): return functools.reduce(lax.pmax, axes, shard)]
    all_to_all x4 -> x5, starting transfers between devices: 19.6 us -> 41.6 us  [exchange(): return lax.all_to_all(parts, axis, split_axis=0, concat_axis=0, tiled=True)]
    all_to_all x0 -> x1, blocking collectives: none -> 20.7 us  [exchange(): return lax.all_to_all(parts, axis, split_axis=0, concat_axis=0, tiled=True)]
    reduce_max x8 -> x7, other arithmetic: 21.3 us -> 1.89 us  [the longest x1 1.32 us: on_device(): peaks = jnp.max(jnp.abs(normed), axis=0).reshape(tok_count, row_count)]
    dot_general x3 -> x1, matrix products: 9.38 us -> 6.77 us  [on_device(): jnp.dot(held, gathered, preferred_element_type=jnp.float32)]
  transfers between devices with their start and end apart: 7 -> 7, of which waited for: 4 -> 7; matrix products, arithmetic and copies ran while one was open for 10% -> 6% of each run, Pallas kernels for 0% -> 0%
where the time goes in v1:
time: 245 us
  waiting for transfers between devices  132 us (54%)
  starting transfers between devices  41.7 us (17%)
  blocking collectives  20.7 us (8%)
  between operations  15 us (6%)
  local copies, waits for them, and re-layouts  12.1 us (5%)
  matrix products  11.8 us (5%)
  other arithmetic  11 us (4%)
    all_gather x1, waiting for transfers between devices, on_device(): gathered = lax.all_gather(block, TOK, axis=0, tiled=True)  50.7 us
    all_to_all x5, waiting for transfers between devices, exchange(): return lax.all_to_all(parts, axis, split_axis=0, concat_axis=0, tiled=True)  44.2 us
    all_to_all x5, starting transfers between devices, exchange(): return lax.all_to_all(parts, axis, split_axis=0, concat_axis=0, tiled=True)  41.6 us
    all_gather x1, waiting for transfers between devices, on_device(): everything = lax.all_gather(line, 'tok_0', axis=0, tiled=True)  37.4 us
    all_to_all x1, blocking collectives, exchange(): return lax.all_to_all(parts, axis, split_axis=0, concat_axis=0, tiled=True)  20.7 us
    dot_general x1, matrix products, on_device(): jnp.dot(held, gathered, preferred_element_type=jnp.float32)  6.77 us
    unnamed x23, local copies, waits for them, and re-layouts  5.78 us
  transfers between devices with their start and end apart: 7, of which 7 were waited for; matrix products, arithmetic and copies ran while one was open for 6% of the time, Pallas kernels for 0%

profile of v1, /device:TPU:2, one launch (start us, length us, event | category | flops | bytes accessed | tf_op | source)
XLA Modules:
  0.0 244.5 jit_solution(8523871371343390615)
XLA Ops:
  7.2 1.0 constant_dynamic-update-slice_fusion.2
  8.3 0.8 constant_dynamic-update-slice_fusion.1
  9.0 0.8 constant_dynamic-update-slice_fusion
  9.8 0.7 copy-done.1
  10.5 0.7 convert_element_type.74
  11.2 1.8 fusion.12
  13.1 1.3 fusion.17
  14.4 0.7 copy.33
  15.1 16.6 %all-to-all-start = ((bf16[64,1,224]{2,1,0:T(2,128)(2,1)}), bf16[64,1,224]{2,1,0:T(2,128)(2,1)S(1)}, u32[]{:S(2)}, u32[]{:S(2)}) async-start(bf16[64,1,224]{2,1,0:T(2,128)(2,1)} %copy.33), calls=%async_computation | async-start | bytes 131072 | tf_op jit(solution)/shard_map/all_to_all | solution.py:17
  31.8 0.1 abs_reduce_fusion.1
  32.0 0.5 broadcast.133
  32.5 0.8 reduce.7
  33.3 0.9 reshape.264
  34.1 10.2 %all-to-all-done = bf16[64,1,224]{2,1,0:T(2,128)(2,1)S(1)} async-done(((bf16[64,1,224]{2,1,0:T(2,128)(2,1)}), bf16[64,1,224]{2,1,0:T(2,128)(2,1)S(1)}, u32[]{:S(2)}, u32[]{:S(2)}) %all-to-all-start) | async-done | bytes 28704 | tf_op jit(solution)/shard_map/all_to_all | solution.py:17
  44.3 4.8 %all-to-all-start.1 = ((bf16[8,2,6208]{2,1,0:T(2,128)(2,1)}), bf16[8,2,6208]{2,1,0:T(2,128)(2,1)S(1)}, u32[]{:S(2)}, u32[]{:S(2)}) async-start(bf16[8,2,6208]{2,1,0:T(2,128)(2,1)} %reshape.264), calls=%async_computation.1 | async-start | bytes 401408 | tf_op jit(solution)/shard_map/all_to_all | solution.py:17
  49.2 5.4 %all-to-all-done.1 = bf16[8,2,6208]{2,1,0:T(2,128)(2,1)S(1)} async-done(((bf16[8,2,6208]{2,1,0:T(2,128)(2,1)}), bf16[8,2,6208]{2,1,0:T(2,128)(2,1)S(1)}, u32[]{:S(2)}, u32[]{:S(2)}) %all-to-all-start.1) | async-done | bytes 198688 | tf_op jit(solution)/shard_map/all_to_all | solution.py:17
  54.5 0.2 reshape.265
  54.9 0.8 broadcast_in_dim.58
  55.7 4.6 %all-to-all-start.2 = ((f32[64,1,768]{2,1,0:T(1,128)}), f32[64,1,768]{2,1,0:T(1,128)S(1)}, u32[]{:S(2)}, u32[]{:S(2)}) async-start(f32[64,1,768]{2,1,0:T(1,128)} %broadcast_in_dim.58), calls=%async_computation.2 | async-start | bytes 393216 | tf_op jit(solution)/shard_map/all_to_all | solution.py:17
  60.4 13.8 %all-to-all-done.2 = f32[64,1,768]{2,1,0:T(1,128)S(1)} async-done(((f32[64,1,768]{2,1,0:T(1,128)}), f32[64,1,768]{2,1,0:T(1,128)S(1)}, u32[]{:S(2)}, u32[]{:S(2)}) %all-to-all-start.2) | async-done | bytes 196640 | tf_op jit(solution)/shard_map/all_to_all | solution.py:17
  74.1 0.1 reduce_max.86
  74.3 0.6 broadcast_in_dim.59
  74.9 4.7 %all-to-all-start.3 = ((f32[8,1,768]{2,1,0:T(1,128)}), f32[8,1,768]{2,1,0:T(1,128)S(1)}, u32[]{:S(2)}, u32[]{:S(2)}) async-start(f32[8,1,768]{2,1,0:T(1,128)} %broadcast_in_dim.59), calls=%async_computation.3 | async-start | bytes 49152 | tf_op jit(solution)/shard_map/all_to_all | solution.py:17
  79.6 4.0 %all-to-all-done.3 = f32[8,1,768]{2,1,0:T(1,128)S(1)} async-done(((f32[8,1,768]{2,1,0:T(1,128)}), f32[8,1,768]{2,1,0:T(1,128)S(1)}, u32[]{:S(2)}, u32[]{:S(2)}) %all-to-all-start.3) | async-done | bytes 24608 | tf_op jit(solution)/shard_map/all_to_all | solution.py:17
  83.6 0.5 slice.39
  84.8 50.7 %all-gather.3.cloned.1.call-done = bf16[8192,768]{1,0:T(8,128)(2,1)} async-done(((bf16[128,768]{1,0:T(8,128)(2,1)}), bf16[8192,768]{1,0:T(8,128)(2,1)}) %all-gather.3.cloned.1.call-update) | async-done | bytes 12582928 | tf_op jit(solution)/shard_map/all_gather | solution.py:59
  135.5 6.8 %fusion.14 = f32[96,768]{1,0:T(8,128)S(1)} fusion(bf16[8192,768]{1,0:T(8,128)(2,1)} %all-gather.3.cloned.1.call-done, bf16[96,8192]{1,0:T(8,128)(2,1)S(1)} %copy-done, f32[8192]{0:T(1024)S(1)} %broadcast_select_fusion, f32[96]{0:T(128)S(1)} %add_rsqrt_fusion), kind=kOutput, calls=%fused_computation.18 | convolution fusion | flops 1211105280 | bytes 14483840 | tf_op jit(solution)/shard_map/dot_general | solution.py:106
  142.3 0.3 fusion.39
  142.7 20.7 %all_to_all.50 = bf16[8,96,256]{2,1,0:T(8,128)(2,1)} all-to-all(bf16[8,96,256]{2,1,0:T(8,128)(2,1)S(1)} %broadcast_in_dim.61), channel_id=1, replica_groups=mesh['tok_0'=8,'tok_1'=8,'tp'=8] {'tok_1'}, dimensions={0} | all-to-all | bytes 786432 | tf_op jit(solution)/shard_map/all_to_all | solution.py:17
  163.4 0.2 multiply_cosine_fusion
  163.8 0.5 fusion.13
  164.3 0.6 dynamic-slice_divide_fusion
  164.9 0.6 split.42
  165.5 0.5 fusion.45
  166.2 0.9 copy.48
  167.1 0.2 fusion.44
  167.4 37.4 %all-gather.5.cloned.1.call-done = bf16[6144,256]{1,0:T(8,128)(2,1)} async-done(((bf16[768,256]{1,0:T(8,128)(2,1)}), bf16[6144,256]{1,0:T(8,128)(2,1)}) %all-gather.5.cloned.1.call-update) | async-done | bytes 3145744 | tf_op jit(solution)/shard_map/all_gather | solution.py:124
  204.7 3.3 %fusion.46 = (f32[4,96]{1,0:T(4,128)S(1)}, f32[1,4,96,6144]{3,2,1,0:T(8,128)S(1)}) fusion(bf16[96,4,64]{2,0,1:T(8,128)(2,1)S(1)} %get-tuple-element.12, bf16[96,4,64]{2,0,1:T(8,128)(2,1)S(1)} %get-tuple-element.11, bf16[6144,256]{1,0:T(8,128)(2,1)} %all-gather.5.cloned.1.call-done, pred[96,6144]{1,0:T(8,128)(4,1)S(1)} %fusion.13), kind=kOutput, calls=%fused_computation.81 | convolution fusion | flops 611253888 | bytes 11699712 | tf_op jit(solution)/shard_map/tkgd,skd->kgts/dot_general | solution.py:128
  208.1 2.2 fusion
  210.3 1.7 abs_reduce_fusion.2
  212.0 1.0 reduce.8
  213.1 0.6 reshape.266
  213.7 10.9 %all-to-all-start.5 = ((bf16[64,2,256]{2,1,0:T(2,128)(2,1)}), bf16[64,2,256]{2,1,0:T(2,128)(2,1)S(1)}, u32[]{:S(2)}, u32[]{:S(2)}) async-start(bf16[64,2,256]{2,1,0:T(2,128)(2,1)} %reshape.266), calls=%async_computation.5 | async-start | bytes 131072 | tf_op jit(solution)/shard_map/all_to_all | solution.py:17
  224.6 0.7 copy_bitcast_fusion.2
  225.3 0.7 copy.62
  226.0 10.9 %all-to-all-done.5 = bf16[64,2,256]{2,1,0:T(2,128)(2,1)S(1)} async-done(((bf16[64,2,256]{2,1,0:T(2,128)(2,1)}), bf16[64,2,256]{2,1,0:T(2,128)(2,1)S(1)}, u32[]{:S(2)}, u32[]{:S(2)}) %all-to-all-start.5) | async-done | bytes 65568 | tf_op jit(solution)/shard_map/all_to_all | solution.py:17
  236.9 0.1 reduce_max.89
  237.1 0.6 convert_element_type.85
  (49 shorter events, 1.2 us)
Async XLA Ops:
  7.2 5.9 %copy-start = (bf16[96,8192]{1,0:T(8,128)(2,1)S(1)}, bf16[96,8192]{1,0:T(8,128)(2,1)}, u32[]{:S(2)}) copy-start(bf16[96,8192]{1,0:T(8,128)(2,1)} %param.6) | copy-start | bytes 4718596
  7.2 128.3 %all-gather.3.cloned.1.call-start = ((), (), s32[]{:S(2)}) async-start(), calls=%async_computation.6 | async-start | bytes 12779520 | tf_op jit(solution)/shard_map/all_gather | solution.py:59
  9.8 0.7 copy-start.1
  10.5 21.2 %copy-start.2 = (bf16[128,768]{1,0:T(8,128)(2,1)S(1)}, bf16[128,768]{1,0:T(8,128)(2,1)}, u32[]{:S(2)}) copy-start(bf16[128,768]{1,0:T(8,128)(2,1)} %copy-done.1) | copy-start | bytes 589828
  13.1 71.7 %copy-start.3 = (f32[8192]{0:T(1024)S(1)}, f32[8192]{0:T(1024)}, u32[]{:S(2)}) copy-start(f32[8192]{0:T(1024)} %param.7) | copy-start | bytes 98308
  15.1 29.2 %all-to-all-start = ((bf16[64,1,224]{2,1,0:T(2,128)(2,1)}), bf16[64,1,224]{2,1,0:T(2,128)(2,1)S(1)}, u32[]{:S(2)}, u32[]{:S(2)}) async-start(bf16[64,1,224]{2,1,0:T(2,128)(2,1)} %copy.33), calls=%async_computation | async-start | bytes 131072 | tf_op jit(solution)/shard_map/all_to_all | solution.py:17
  44.3 10.2 %all-to-all-start.1 = ((bf16[8,2,6208]{2,1,0:T(2,128)(2,1)}), bf16[8,2,6208]{2,1,0:T(2,128)(2,1)S(1)}, u32[]{:S(2)}, u32[]{:S(2)}) async-start(bf16[8,2,6208]{2,1,0:T(2,128)(2,1)} %reshape.264), calls=%async_computation.1 | async-start | bytes 401408 | tf_op jit(solution)/shard_map/all_to_all | solution.py:17
  55.7 18.4 %all-to-all-start.2 = ((f32[64,1,768]{2,1,0:T(1,128)}), f32[64,1,768]{2,1,0:T(1,128)S(1)}, u32[]{:S(2)}, u32[]{:S(2)}) async-start(f32[64,1,768]{2,1,0:T(1,128)} %broadcast_in_dim.58), calls=%async_computation.2 | async-start | bytes 393216 | tf_op jit(solution)/shard_map/all_to_all | solution.py:17
  74.9 8.7 %all-to-all-start.3 = ((f32[8,1,768]{2,1,0:T(1,128)}), f32[8,1,768]{2,1,0:T(1,128)S(1)}, u32[]{:S(2)}, u32[]{:S(2)}) async-start(f32[8,1,768]{2,1,0:T(1,128)} %broadcast_in_dim.59), calls=%async_computation.3 | async-start | bytes 49152 | tf_op jit(solution)/shard_map/all_to_all | solution.py:17
  79.6 125.1 %all-gather.5.cloned.1.call-start = ((), (), s32[]{:S(2)}) async-start(), calls=%async_computation.7 | async-start | bytes 3538944 | tf_op jit(solution)/shard_map/all_gather | solution.py:124
  84.8 79.0 %copy-start.4 = (s32[96]{0:T(128)S(1)}, s32[96]{0:T(128)}, u32[]{:S(2)}) copy-start(s32[96]{0:T(128)} %param.11) | copy-start | bytes 1156
  208.1 2.2 copy-start.5
  213.7 23.2 %all-to-all-start.5 = ((bf16[64,2,256]{2,1,0:T(2,128)(2,1)}), bf16[64,2,256]{2,1,0:T(2,128)(2,1)S(1)}, u32[]{:S(2)}, u32[]{:S(2)}) async-start(bf16[64,2,256]{2,1,0:T(2,128)(2,1)} %reshape.266), calls=%async_computation.5 | async-start | bytes 131072 | tf_op jit(solution)/shard_map/all_to_all | solution.py:17
Sparse Core Ops, SparseCore 0:
  11.1 124.4 all-gather.2
  163.5 41.1 all-gather.4

commit v2 on v1

v2 whole, which is shorter than its diff:
```python
import math

import jax
import jax.numpy as jnp
from jax import lax
from jax.sharding import Mesh
from jax.sharding import PartitionSpec as P

HEAD = 128
KVH = 8
QHEADS = 32
LINE = ("z", "pair")
TOK = ("y", "z", "pair")
TP = ("x", "core")
TOK_TP = TOK + TP


def exchange(parts, axis):
    return lax.all_to_all(parts, axis, split_axis=0, concat_axis=0, tiled=True)


def to_everyone(shard, axis):
    return exchange(jnp.broadcast_to(shard, (lax.axis_size(axis), *shard.shape)), axis)


def rotate(states, positions):
    half = states.shape[-1] // 2
    inverse = jnp.exp(
        jnp.arange(half, dtype=jnp.float32) * (-2.0 * math.log(10000.0) / states.shape[-1])
    )
    angles = positions[:, None] * inverse[None, :]
    cosine = jnp.cos(angles)[:, None, :]
    sine = jnp.sin(angles)[:, None, :]
    first = states[..., :half]
    second = states[..., half:]
    return jnp.concatenate(
        [first * cosine - second * sine, second * cosine + first * sine], axis=-1
    )


def smooth_from(input_peak, weight_peak):
    return jnp.sqrt(jnp.maximum(input_peak, 1e-05)) / jnp.sqrt(jnp.maximum(weight_peak, 1e-05))


def on_device(hidden, norm_gain, w_query, w_key, w_value, doc_ids):
    tok_dev, width = hidden.shape
    row_count = w_query.shape[0]
    tok_count = lax.axis_size(TOK)
    tp_count = lax.axis_size(TP)
    tok_index = lax.axis_index(TOK)
    tp_index = lax.axis_index(TP)
    side = lax.axis_index("pair")
    core = lax.axis_index("core")
    line = lax.axis_size("z") * 2
    sub_rows = row_count // tp_count
    widths = (w_query.shape[1], w_key.shape[1], w_value.shape[1])
    cuts = (widths[0], widths[0] + widths[1])
    columns = sum(widths)
    half_query = widths[0] // 2
    half_columns = half_query + HEAD
    heads_half = half_query // HEAD
    group_size = QHEADS // KVH

    halves = jnp.stack(
        (
            jnp.concatenate((w_query[:, :half_query], w_key), axis=1),
            jnp.concatenate((w_query[:, half_query:], w_value), axis=1),
        )
    )
    sent = jnp.broadcast_to(halves, (line // 2, *halves.shape))
    along_z = exchange(sent.reshape(line, row_count, half_columns), LINE)
    gathered = lax.all_gather(
        along_z.reshape(line * row_count, half_columns), "y", axis=0, tiled=True
    )

    states = hidden.astype(jnp.float32)
    inverse_rms = lax.rsqrt(jnp.mean(states * states, axis=1, keepdims=True) + 1e-05)
    normed = (states * inverse_rms * norm_gain[None, :]).astype(jnp.bfloat16)

    swap = [(0, 1), (1, 0)]
    channels = width // 2
    near = lax.ppermute(
        lax.dynamic_slice_in_dim(normed, core * channels, channels, axis=1), "pair", swap
    )
    far = lax.ppermute(near, "core", swap)
    other = jnp.concatenate(
        (jnp.where(core == 0, near, far), jnp.where(core == 0, far, near)), axis=1
    )

    peaks = jnp.max(jnp.abs(normed), axis=0).reshape(tok_count, row_count)
    docs = jnp.broadcast_to(doc_ids.astype(jnp.bfloat16), (tok_count, tok_dev))
    arrived = exchange(jnp.concatenate((peaks, docs), axis=1), TOK)
    input_peak = jnp.max(arrived[:, :row_count], axis=0).astype(jnp.float32)
    doc_block = arrived[:, row_count:].astype(jnp.int32).reshape(tok_count * tok_dev)

    block = jnp.concatenate((w_query, w_key, w_value), axis=1)
    row_peak = jnp.max(jnp.abs(block), axis=1)
    sent = jnp.concatenate(
        (
            block.reshape(tp_count, sub_rows * columns),
            jnp.broadcast_to(row_peak, (tp_count, row_count)),
        ),
        axis=1,
    )
    rows = exchange(sent, TP)
    weight_peak = jnp.max(rows[:, sub_rows * columns :], axis=0).astype(jnp.float32)
    own_rows = rows[:, : sub_rows * columns].reshape(tp_count, sub_rows, columns)

    smoothing = smooth_from(input_peak, weight_peak)
    column_peak = jnp.max(jnp.abs(smoothing[:, None] * block.astype(jnp.float32)), axis=0)
    column_peak = jnp.max(to_everyone(column_peak, TOK), axis=0)
    scale = jnp.maximum(column_peak, 1e-05) / 127.0
    all_scales = to_everyone(scale, TP)
    scales = jnp.split(scale, cuts)

    smooth_part = lax.dynamic_slice_in_dim(smoothing, tp_index * sub_rows, sub_rows)
    gain_part = lax.dynamic_slice_in_dim(
        norm_gain, tok_index * row_count + tp_index * sub_rows, sub_rows
    )
    folded_gain = gain_part / smooth_part
    coded = (
        smooth_part[None, :, None] * own_rows.astype(jnp.float32) / all_scales[:, None, :]
    )
    codes = tuple(
        part.transpose(1, 0, 2).reshape(sub_rows, tp_count * part.shape[2])
        for part in jnp.split(coded, cuts, axis=2)
    )

    even = (side == 0) & (all_scales[0, 0] > 0.0)
    both_rows = jnp.concatenate(
        (jnp.where(even, normed, other), jnp.where(even, other, normed)), axis=0
    )
    projected = jnp.dot(both_rows, gathered, preferred_element_type=jnp.float32)
    pair_positions = (tok_index - side) * tok_dev + jnp.arange(2 * tok_dev, dtype=jnp.int32)
    last = projected[:, half_query:]
    turned = rotate(
        projected.reshape(2 * tok_dev, heads_half + 1, HEAD), pair_positions.astype(jnp.float32)
    )
    kept = jnp.where(side == 0, turned[:, heads_half], last).astype(jnp.bfloat16)

    spread = to_everyone(kept, LINE).reshape(line // 2, 2, 2 * tok_dev, HEAD)
    spread = jnp.concatenate(
        (spread[:, 0].reshape(-1, HEAD), spread[:, 1].reshape(-1, HEAD)), axis=1
    )
    everything = lax.all_gather(spread, "y", axis=0, tiled=True)
    key_block, value_block = jnp.split(everything, (HEAD,), axis=1)

    turned = turned[:, :heads_half].astype(jnp.bfloat16).reshape(2, tok_dev, half_query)
    mine = jnp.where(side == 0, turned[0], turned[1])
    swapped = lax.ppermute(jnp.where(side == 0, turned[1], turned[0]), "pair", swap)
    query = jnp.concatenate(
        (jnp.where(side == 0, mine, swapped), jnp.where(side == 0, swapped, mine)), axis=1
    ).reshape(tok_dev, group_size, HEAD)

    length = key_block.shape[0]
    scores = jnp.einsum(
        "tgd,sd->gts", query, key_block, preferred_element_type=jnp.float32
    ) * (1.0 / math.sqrt(HEAD))
    query_positions = tok_index * tok_dev + jnp.arange(tok_dev, dtype=jnp.int32)
    key_positions = jnp.arange(length, dtype=jnp.int32)
    allowed = (doc_ids[:, None] == doc_block[None, :]) & (
        key_positions[None, :] <= query_positions[:, None]
    )
    scores = jnp.where(allowed, scores, -1e30)
    highest = jnp.max(scores, axis=2, keepdims=True)
    weights = jnp.where(allowed, jnp.exp(scores - highest), 0.0)
    totals = jnp.sum(weights, axis=2)
    accumulated = jnp.einsum(
        "gts,sd->gtd",
        weights.astype(jnp.bfloat16),
        value_block,
        preferred_element_type=jnp.float32,
    )
    attended = (
        (accumulated / totals[..., None])
        .transpose(1, 0, 2)
        .reshape(tok_dev, group_size * HEAD)
        .astype(jnp.bfloat16)
    )
    out_peak = to_everyone(jnp.max(jnp.abs(attended), axis=0), TOK)
    out_scale = jnp.max(out_peak, axis=0).astype(jnp.float32)
    return (
        attended,
        out_scale,
        folded_gain,
        codes[0],
        codes[1],
        codes[2],
        scales[0],
        scales[1],
        scales[2],
    )


def solution(mesh):
    split = Mesh(mesh.devices.reshape(8, 4, 2, 4, 2), ("y", "z", "pair", "x", "core"))
    placed = (P(TOK, None), P(), P(TOK, TP), P(TOK, TP), P(TOK, TP), P(TOK))
    return jax.shard_map(
        on_device,
        mesh=split,
        in_specs=placed,
        out_specs=(
            P(TOK, TP),
            P(TP),
            P(TOK_TP),
            P(TOK_TP, None),
            P(TOK_TP, None),
            P(TOK_TP, None),
            P(TP),
            P(TP),
            P(TP),
        ),
        check_vma=False,
    )
```

time: 245 us -> 237 us (0.967)
  waiting for transfers between devices: 132 us -> 80.5 us
  blocking collectives: 20.7 us -> 55 us
  other arithmetic: 11 us -> 16.5 us
  starting transfers between devices: 41.7 us -> 44.4 us
    all_gather x2, waiting for transfers between devices: 88.1 us -> 34.3 us  [the longest x1 31.8 us: on_device(): everything = lax.all_gather(spread, 'y', axis=0, tiled=True)]
    all_to_all x1 -> x2, blocking collectives: 20.7 us -> 55 us  [exchange(): return lax.all_to_all(parts, axis, split_axis=0, concat_axis=0, tiled=True)]
    ppermute x0 -> x3, starting transfers between devices: none -> 7.03 us  [the longest x1 2.65 us: on_device(): lax.ppermute(jnp.where(side == 0, turned[1], turned[0]), 'pair', swap)]
    sub x0 -> x1, other arithmetic: none -> 4.49 us  [on_device(): weights = jnp.where(allowed, jnp.exp(scores - highest), 0.0)]
    all_to_all x5, starting transfers between devices: 41.6 us -> 37.4 us  [exchange(): return lax.all_to_all(parts, axis, split_axis=0, concat_axis=0, tiled=True)]
    select_n x1 -> x3, other arithmetic: 0.01 us -> 2.98 us  [the longest x1 1.73 us: on_device(): jnp.where(even, normed, other)]
    unnamed x23 -> x30, local copies, waits for them, and re-layouts: 5.78 us -> 3.29 us
  transfers between devices with their start and end apart: 7 -> 10, of which waited for: 7 -> 8; matrix products, arithmetic and copies ran while one was open for 6% -> 7% of each run, Pallas kernels for 0% -> 0%
where the time goes in v2:
time: 237 us; the launch traced here: 236 us
  waiting for transfers between devices  80.5 us (34%)
  blocking collectives  55 us (23%)
  starting transfers between devices  44.4 us (19%)
  other arithmetic  16.5 us (7%)
  between operations  15.2 us (6%)
  matrix products  12.3 us (5%)
  local copies, waits for them, and re-layouts  11.6 us (5%)
    all_to_all x2, blocking collectives, exchange(): return lax.all_to_all(parts, axis, split_axis=0, concat_axis=0, tiled=True)  55 us
    all_to_all x5, waiting for transfers between devices, exchange(): return lax.all_to_all(parts, axis, split_axis=0, concat_axis=0, tiled=True)  44.5 us
    all_to_all x5, starting transfers between devices, exchange(): return lax.all_to_all(parts, axis, split_axis=0, concat_axis=0, tiled=True)  37.4 us
    all_gather x1, waiting for transfers between devices, on_device(): everything = lax.all_gather(spread, 'y', axis=0, tiled=True)  31.8 us
    dot_general x1, matrix products, on_device(): projected = jnp.dot(both_rows, gathered, preferred_element_type=jnp.float32)  5.07 us
  transfers between devices with their start and end apart: 10, of which 8 were waited for; matrix products, arithmetic and copies ran while one was open for 7% of the time, Pallas kernels for 0%

profile of v2, /device:TPU:2, one launch (start us, length us, event | category | flops | bytes accessed | tf_op | source)
XLA Modules:
  0.0 235.6 jit_solution(9476190936402452797)
XLA Ops:
  7.2 1.0 fusion.33
  8.2 0.8 maximum_bitcast_fusion.1
  9.0 0.8 maximum_bitcast_fusion.2
  9.9 33.3 %all_to_all.55 = bf16[8,128,384]{2,1,0:T(8,128)(2,1)} all-to-all(bf16[8,128,384]{2,1,0:T(8,128)(2,1)S(1)} %bitcast.93), channel_id=1, replica_groups=mesh['y'=8,'z'=4,'pair'=2,'x'=4,'core'=2] {'z','pair'}, dimensions={0} | all-to-all | bytes 1572864 | tf_op jit(solution)/shard_map/all_to_all | solution.py:19
  43.7 0.6 abs_reduce_fusion
  44.3 1.0 constant_dynamic-slice_fusion
  45.2 2.5 %collective-permute-start = (bf16[96,4096]{1,0:T(8,128)(2,1)}, bf16[96,4096]{1,0:T(8,128)(2,1)}, u32[]{:S(2)}, u32[]{:S(2)}) collective-permute-start(bf16[96,4096]{1,0:T(8,128)(2,1)} %constant_dynamic-slice_fusion), channel_id=1, source_target_pairs={{0,8},{8,0},{1,9},{9,1},{2,10},{10,2},{3,11},{11,3},{4,12},{12,4},... | collective-permute-start | bytes 2359304 | tf_op jit(solution)/shard_map/ppermute | solution.py:82
  47.8 0.7 copy.43
  48.4 9.0 %all-to-all-start = ((bf16[64,1,224]{2,1,0:T(2,128)(2,1)}), bf16[64,1,224]{2,1,0:T(2,128)(2,1)S(1)}, u32[]{:S(2)}, u32[]{:S(2)}) async-start(bf16[64,1,224]{2,1,0:T(2,128)(2,1)} %copy.43), calls=%async_computation | async-start | bytes 131072 | tf_op jit(solution)/shard_map/all_to_all | solution.py:19
  57.8 0.5 broadcast.90
  58.3 0.8 reduce.3
  59.1 0.9 reshape.188
  60.0 10.4 %all-to-all-done = bf16[64,1,224]{2,1,0:T(2,128)(2,1)S(1)} async-done(((bf16[64,1,224]{2,1,0:T(2,128)(2,1)}), bf16[64,1,224]{2,1,0:T(2,128)(2,1)S(1)}, u32[]{:S(2)}, u32[]{:S(2)}) %all-to-all-start) | async-done | bytes 28704 | tf_op jit(solution)/shard_map/all_to_all | solution.py:19
  70.4 4.8 %all-to-all-start.1 = ((bf16[8,2,6208]{2,1,0:T(2,128)(2,1)}), bf16[8,2,6208]{2,1,0:T(2,128)(2,1)S(1)}, u32[]{:S(2)}, u32[]{:S(2)}) async-start(bf16[8,2,6208]{2,1,0:T(2,128)(2,1)} %reshape.188), calls=%async_computation.1 | async-start | bytes 401408 | tf_op jit(solution)/shard_map/all_to_all | solution.py:19
  75.2 0.6 copy-done.2
  75.8 4.8 %all-to-all-done.1 = bf16[8,2,6208]{2,1,0:T(2,128)(2,1)S(1)} async-done(((bf16[8,2,6208]{2,1,0:T(2,128)(2,1)}), bf16[8,2,6208]{2,1,0:T(2,128)(2,1)S(1)}, u32[]{:S(2)}, u32[]{:S(2)}) %all-to-all-start.1) | async-done | bytes 198688 | tf_op jit(solution)/shard_map/all_to_all | solution.py:19
  81.0 0.8 broadcast_in_dim.52
  81.7 8.0 %all-to-all-start.2 = ((f32[64,1,768]{2,1,0:T(1,128)}), f32[64,1,768]{2,1,0:T(1,128)S(1)}, u32[]{:S(2)}, u32[]{:S(2)}) async-start(f32[64,1,768]{2,1,0:T(1,128)} %broadcast_in_dim.52), calls=%async_computation.2 | async-start | bytes 393216 | tf_op jit(solution)/shard_map/all_to_all | solution.py:19
  89.8 1.9 collective-permute-start.1
  91.7 14.1 %all-to-all-done.2 = f32[64,1,768]{2,1,0:T(1,128)S(1)} async-done(((f32[64,1,768]{2,1,0:T(1,128)}), f32[64,1,768]{2,1,0:T(1,128)S(1)}, u32[]{:S(2)}, u32[]{:S(2)}) %all-to-all-start.2) | async-done | bytes 196640 | tf_op jit(solution)/shard_map/all_to_all | solution.py:19
  106.0 0.6 broadcast_in_dim.53
  106.6 4.6 %all-to-all-start.3 = ((f32[8,1,768]{2,1,0:T(1,128)}), f32[8,1,768]{2,1,0:T(1,128)S(1)}, u32[]{:S(2)}, u32[]{:S(2)}) async-start(f32[8,1,768]{2,1,0:T(1,128)} %broadcast_in_dim.53), calls=%async_computation.3 | async-start | bytes 49152 | tf_op jit(solution)/shard_map/all_to_all | solution.py:19
  111.7 3.5 %all-to-all-done.3 = f32[8,1,768]{2,1,0:T(1,128)S(1)} async-done(((f32[8,1,768]{2,1,0:T(1,128)}), f32[8,1,768]{2,1,0:T(1,128)S(1)}, u32[]{:S(2)}, u32[]{:S(2)}) %all-to-all-start.3) | async-done | bytes 24608 | tf_op jit(solution)/shard_map/all_to_all | solution.py:19
  115.3 0.5 slice.71
  116.5 1.2 broadcast_select_fusion.3
  117.7 1.7 broadcast_select_fusion.1
  119.4 2.5 %all-gather.3.cloned.1.call-done = bf16[8192,384]{1,0:T(8,128)(2,1)} async-done(((bf16[1024,384]{1,0:T(8,128)(2,1)}), bf16[8192,384]{1,0:T(8,128)(2,1)}) %all-gather.3.cloned.1.call-update) | async-done | bytes 6291472 | tf_op jit(solution)/shard_map/all_gather | solution.py:72
  121.9 5.1 %fusion.7 = f32[192,384]{1,0:T(8,128)S(1)} fusion(bf16[8192,384]{1,0:T(8,128)(2,1)} %all-gather.3.cloned.1.call-done, bf16[96,8192]{1,0:T(8,128)(2,1)} %get-tuple-element.14, bf16[96,8192]{1,0:T(8,128)(2,1)S(1)} %get-tuple-element.13), kind=kOutput, calls=%fused_computation.11 | convolution fusion | flops 1214251008 | bytes 9732096 | tf_op jit(solution)/shard_map/dot_general | solution.py:133
  127.7 21.7 %all_to_all.56 = bf16[8,192,128]{2,1,0:T(8,128)(2,1)S(1)} all-to-all(bf16[8,192,128]{2,1,0:T(8,128)(2,1)S(1)} %broadcast_in_dim.55), channel_id=1, replica_groups=mesh['y'=8,'z'=4,'pair'=2,'x'=4,'core'=2] {'z','pair'}, dimensions={0} | all-to-all | bytes 786432 | tf_op jit(solution)/shard_map/all_to_all | solution.py:19
  149.4 0.8 pad_maximum_fusion.1
  150.3 0.5 fusion.11
  150.9 1.3 dynamic-slice_divide_fusion
  152.2 0.6 split.29
  152.8 0.5 fusion.34
  153.6 2.7 %collective-permute-start.2 = (bf16[96,256]{1,0:T(8,128)(2,1)S(1)}, bf16[96,256]{1,0:T(8,128)(2,1)S(1)}, u32[]{:S(2)}, u32[]{:S(2)}) collective-permute-start(bf16[96,256]{1,0:T(8,128)(2,1)S(1)} %bitcast.109), channel_id=1, source_target_pairs={{0,8},{8,0},{1,9},{9,1},{2,10},{10,2},{3,11},{11,3},{4,12},{12,4},... | collective-permute-start | bytes 147464 | tf_op jit(solution)/shard_map/ppermute | solution.py:150
  156.2 0.7 copy_bitcast_fusion.2
  156.9 0.9 copy.64
  157.8 1.8 collective-permute-done.2
  159.6 31.8 %all-gather.5.cloned.1.call-done = bf16[6144,256]{1,0:T(8,128)(2,1)} async-done(((bf16[768,256]{1,0:T(8,128)(2,1)}), bf16[6144,256]{1,0:T(8,128)(2,1)}) %all-gather.5.cloned.1.call-update) | async-done | bytes 3145744 | tf_op jit(solution)/shard_map/all_gather | solution.py:145
  191.4 3.0 %bitcast_select_fusion = f32[4,96,6144]{2,1,0:T(8,128)S(1)} fusion(pred[96,6144]{1,0:T(8,128)(4,1)S(1)} %fusion.11, bf16[6144,256]{1,0:T(8,128)(2,1)} %all-gather.5.cloned.1.call-done, bf16[96,256]{1,0:T(8,128)(2,1)S(1)} %get-tuple-element.30, bf16[96,256]{1,0:T(8,128)(2,1)S(1)} %get-tuple-element.29), kind=kOutput, calls=%fused_computation.2 | convolution fusion | flops 608894976 | bytes 11698176 | tf_op jit(solution)/shard_map/tgd,sd->gts/dot_general | solution.py:156
  194.4 4.5 %fusion.35 = (f32[4,96]{1,0:T(4,128)S(1)}, bf16[4,96,6144]{2,1,0:T(8,128)(2,1)}) fusion(f32[4,96,6144]{2,1,0:T(8,128)S(1)} %bitcast_select_fusion, pred[96,6144]{1,0:T(8,128)(4,1)S(1)} %fusion.11), kind=kOutput, calls=%fused_computation.84 | output fusion | flops 9443327 | bytes 14747136 | tf_op jit(solution)/shard_map/sub | solution.py:166
  198.8 4.2 %abs_reduce_fusion.3 = (bf16[4,128]{1,0:T(4,128)(2,1)S(1)}, bf16[96,4,128]{2,0,1:T(8,128)(2,1)S(1)}) fusion(f32[96,4]{0,1:T(4,128)S(1)} %bitcast.111, bf16[6144,256]{1,0:T(8,128)(2,1)} %all-gather.5.cloned.1.call-done, bf16[4,96,6144]{2,1,0:T(8,128)(2,1)} %get-tuple-element.36), kind=kOutput, calls=%fused_computation.53 | convolution fusion | flops 604175872 | bytes 6392320 | tf_op jit(solution)/shard_map/gts,sd->gtd/dot_general | solution.py:168
  203.2 1.0 reduce.4
  204.2 0.6 reshape.190
  204.8 10.9 %all-to-all-start.6 = ((bf16[64,2,256]{2,1,0:T(2,128)(2,1)}), bf16[64,2,256]{2,1,0:T(2,128)(2,1)S(1)}, u32[]{:S(2)}, u32[]{:S(2)}) async-start(bf16[64,2,256]{2,1,0:T(2,128)(2,1)} %reshape.190), calls=%async_computation.6 | async-start | bytes 131072 | tf_op jit(solution)/shard_map/all_to_all | solution.py:19
  215.7 0.6 copy_bitcast_fusion.1
  216.4 11.6 %all-to-all-done.6 = bf16[64,2,256]{2,1,0:T(2,128)(2,1)S(1)} async-done(((bf16[64,2,256]{2,1,0:T(2,128)(2,1)}), bf16[64,2,256]{2,1,0:T(2,128)(2,1)S(1)}, u32[]{:S(2)}, u32[]{:S(2)}) %all-to-all-start.6) | async-done | bytes 65568 | tf_op jit(solution)/shard_map/all_to_all | solution.py:19
  228.2 0.6 convert_element_type.68
  (72 shorter events, 3.3 us)
Async XLA Ops:
  7.2 36.1 %copy-start = (bf16[96,8192]{1,0:T(8,128)(2,1)S(1)}, bf16[96,8192]{1,0:T(8,128)(2,1)}, u32[]{:S(2)}) copy-start(bf16[96,8192]{1,0:T(8,128)(2,1)} %param.6) | copy-start | bytes 4718596
  7.2 36.5 %copy-start.8 = (f32[8192]{0:T(1024)S(1)}, f32[8192]{0:T(1024)}, u32[]{:S(2)}) copy-start(f32[8192]{0:T(1024)} %param.7) | copy-start | bytes 98308
  7.2 114.7 %all-gather.3.cloned.1.call-start = ((), (), s32[]{:S(2)}) async-start(), calls=%async_computation.7 | async-start | bytes 7077888 | tf_op jit(solution)/shard_map/all_gather | solution.py:72
  43.3 4.4 %copy-start.9 = (s32[96]{0:T(128)S(1)}, s32[96]{0:T(128)}, u32[]{:S(2)}) copy-start(s32[96]{0:T(128)} %param.11) | copy-start | bytes 1156
  43.3 14.2 %copy-start.1 = (bf16[128,512]{1,0:T(8,128)(2,1)S(1)}, bf16[128,512]{1,0:T(8,128)(2,1)}, u32[]{:S(2)}) copy-start(bf16[128,512]{1,0:T(8,128)(2,1)} %param.8) | copy-start | bytes 393220
  43.3 14.2 %copy-start.4 = (bf16[128,128]{1,0:T(8,128)(2,1)S(1)}, bf16[128,128]{1,0:T(8,128)(2,1)}, u32[]{:S(2)}) copy-start(bf16[128,128]{1,0:T(8,128)(2,1)} %param.9) | copy-start | bytes 98308
  43.3 14.2 %copy-start.5 = (bf16[128,128]{1,0:T(8,128)(2,1)S(1)}, bf16[128,128]{1,0:T(8,128)(2,1)}, u32[]{:S(2)}) copy-start(bf16[128,128]{1,0:T(8,128)(2,1)} %param.10) | copy-start | bytes 98308
  45.2 44.5 %collective-permute-start = (bf16[96,4096]{1,0:T(8,128)(2,1)}, bf16[96,4096]{1,0:T(8,128)(2,1)}, u32[]{:S(2)}, u32[]{:S(2)}) collective-permute-start(bf16[96,4096]{1,0:T(8,128)(2,1)} %constant_dynamic-slice_fusion), channel_id=1, source_target_pairs={{0,8},{8,0},{1,9},{9,1},{2,10},{10,2},{3,11},{11,3},{4,12},{12,4},... | collective-permute-start | bytes 2359304 | tf_op jit(solution)/shard_map/ppermute | solution.py:82
  48.4 21.9 %all-to-all-start = ((bf16[64,1,224]{2,1,0:T(2,128)(2,1)}), bf16[64,1,224]{2,1,0:T(2,128)(2,1)S(1)}, u32[]{:S(2)}, u32[]{:S(2)}) async-start(bf16[64,1,224]{2,1,0:T(2,128)(2,1)} %copy.43), calls=%async_computation | async-start | bytes 131072 | tf_op jit(solution)/shard_map/all_to_all | solution.py:19
  70.4 10.2 %all-to-all-start.1 = ((bf16[8,2,6208]{2,1,0:T(2,128)(2,1)}), bf16[8,2,6208]{2,1,0:T(2,128)(2,1)S(1)}, u32[]{:S(2)}, u32[]{:S(2)}) async-start(bf16[8,2,6208]{2,1,0:T(2,128)(2,1)} %reshape.188), calls=%async_computation.1 | async-start | bytes 401408 | tf_op jit(solution)/shard_map/all_to_all | solution.py:19
  75.2 0.6 copy-start.2
  81.7 24.1 %all-to-all-start.2 = ((f32[64,1,768]{2,1,0:T(1,128)}), f32[64,1,768]{2,1,0:T(1,128)S(1)}, u32[]{:S(2)}, u32[]{:S(2)}) async-start(f32[64,1,768]{2,1,0:T(1,128)} %broadcast_in_dim.52), calls=%async_computation.2 | async-start | bytes 393216 | tf_op jit(solution)/shard_map/all_to_all | solution.py:19
  89.8 26.7 %collective-permute-start.1 = (bf16[96,4096]{1,0:T(8,128)(2,1)}, bf16[96,4096]{1,0:T(8,128)(2,1)S(1)}, u32[]{:S(2)}, u32[]{:S(2)}) collective-permute-start(bf16[96,4096]{1,0:T(8,128)(2,1)} %collective-permute-done), channel_id=1, source_target_pairs={{0,1},{1,0},{2,3},{3,2},{4,5},{5,4},{6,7},{7,6},{8,9},{9,8},{10,11... | collective-permute-start | bytes 2359304 | tf_op jit(solution)/shard_map/ppermute | solution.py:85
  106.6 8.6 %all-to-all-start.3 = ((f32[8,1,768]{2,1,0:T(1,128)}), f32[8,1,768]{2,1,0:T(1,128)S(1)}, u32[]{:S(2)}, u32[]{:S(2)}) async-start(f32[8,1,768]{2,1,0:T(1,128)} %broadcast_in_dim.53), calls=%async_computation.3 | async-start | bytes 49152 | tf_op jit(solution)/shard_map/all_to_all | solution.py:19
  111.3 80.1 %all-gather.5.cloned.1.call-start = ((), (), s32[]{:S(2)}) async-start(), calls=%async_computation.8 | async-start | bytes 3538944 | tf_op jit(solution)/shard_map/all_gather | solution.py:145
  115.3 2.4 %copy-start.6 = (f32[8,1,768]{2,0,1:T(8,128)}, f32[8,1,768]{2,0,1:T(8,128)S(1)}, u32[]{:S(2)}) copy-start(f32[8,1,768]{2,0,1:T(8,128)S(1)} %copy.87) | copy-start | bytes 73732
  127.1 23.1 %copy-start.3 = (bf16[64,1,224]{2,0,1:T(8,128)(2,1)S(1)}, bf16[64,1,224]{2,0,1:T(8,128)(2,1)}, u32[]{:S(2)}) copy-start(bf16[64,1,224]{2,0,1:T(8,128)(2,1)} %copy-done.2) | copy-start | bytes 86020
  127.4 25.9 %copy-start.7 = (f32[8,1,768]{2,0,1:T(8,128)S(1)}, f32[8,1,768]{2,0,1:T(8,128)}, u32[]{:S(2)}) copy-start(f32[8,1,768]{2,0,1:T(8,128)} %copy-done.6) | copy-start | bytes 73732
  153.6 6.0 %collective-permute-start.2 = (bf16[96,256]{1,0:T(8,128)(2,1)S(1)}, bf16[96,256]{1,0:T(8,128)(2,1)S(1)}, u32[]{:S(2)}, u32[]{:S(2)}) collective-permute-start(bf16[96,256]{1,0:T(8,128)(2,1)S(1)} %bitcast.109), channel_id=1, source_target_pairs={{0,8},{8,0},{1,9},{9,1},{2,10},{10,2},{3,11},{11,3},{4,12},{12,4},... | collective-permute-start | bytes 147464 | tf_op jit(solution)/shard_map/ppermute | solution.py:150
  204.8 23.2 %all-to-all-start.6 = ((bf16[64,2,256]{2,1,0:T(2,128)(2,1)}), bf16[64,2,256]{2,1,0:T(2,128)(2,1)S(1)}, u32[]{:S(2)}, u32[]{:S(2)}) async-start(bf16[64,2,256]{2,1,0:T(2,128)(2,1)} %reshape.190), calls=%async_computation.6 | async-start | bytes 131072 | tf_op jit(solution)/shard_map/all_to_all | solution.py:19
Sparse Core Ops, SparseCore 0:
  43.4 78.4 all-gather.2
  150.3 40.9 all-gather.4

commit v3 on v2

--- a/solution.py
+++ b/solution.py
@@ -21,6 +21,23 @@
 
 def to_everyone(shard, axis):
     return exchange(jnp.broadcast_to(shard, (lax.axis_size(axis), *shard.shape)), axis)
+
+
+def to_sides(even, odd):
+    halves = jnp.stack((even, odd))
+    sent = jnp.broadcast_to(halves, (lax.axis_size("z"), *halves.shape))
+    return exchange(sent.reshape(-1, *even.shape), LINE).reshape(-1, even.shape[1])
+
+
+def present(array):
+    first = array.reshape(-1)[0]
+    return first < 1e30
+
+
+def in_pair_order(even, own, other):
+    return jnp.concatenate(
+        (jnp.where(even, own, other), jnp.where(even, other, own)), axis=0
+    )
 
 
 def rotate(states, positions):
@@ -57,21 +74,10 @@
     cuts = (widths[0], widths[0] + widths[1])
     columns = sum(widths)
     half_query = widths[0] // 2
-    half_columns = half_query + HEAD
-    heads_half = half_query // HEAD
     group_size = QHEADS // KVH
 
-    halves = jnp.stack(
-        (
-            jnp.concatenate((w_query[:, :half_query], w_key), axis=1),
-            jnp.concatenate((w_query[:, half_query:], w_value), axis=1),
-        )
-    )
-    sent = jnp.broadcast_to(halves, (line // 2, *halves.shape))
-    along_z = exchange(sent.reshape(line, row_count, half_columns), LINE)
-    gathered = lax.all_gather(
-        along_z.reshape(line * row_count, half_columns), "y", axis=0, tiled=True
-    )
+    along_z = to_sides(w_key, w_value)
+    gathered_last = lax.all_gather(along_z, "y", axis=0, tiled=True)
 
     states = hidden.astype(jnp.float32)
     inverse_rms = lax.rsqrt(jnp.mean(states * states, axis=1, keepdims=True) + 1e-05)
@@ -82,12 +88,31 @@
     near = lax.ppermute(
         lax.dynamic_slice_in_dim(normed, core * channels, channels, axis=1), "pair", swap
     )
+    held_query = jnp.where(present(normed), w_query, 0.0)
+    along_z = to_sides(held_query[:, :half_query], held_query[:, half_query:])
+    gathered_query = lax.all_gather(along_z, "y", axis=0, tiled=True)
     far = lax.ppermute(near, "core", swap)
     other = jnp.concatenate(
         (jnp.where(core == 0, near, far), jnp.where(core == 0, far, near)), axis=1
     )
 
+    even = (side == 0) & present(along_z)
+    both_rows = in_pair_order(even, normed, other)
+    pair_positions = (tok_index - side) * tok_dev + jnp.arange(2 * tok_dev, dtype=jnp.int32)
+    pair_positions = pair_positions.astype(jnp.float32)
+    last = jnp.dot(both_rows, gathered_last, preferred_element_type=jnp.float32)
+    turned = rotate(last[:, None, :], pair_positions)[:, 0]
+    kept = jnp.where(side == 0, turned, last).astype(jnp.bfloat16)
+
+    spread = to_everyone(kept, LINE).reshape(line // 2, 2, 2 * tok_dev, HEAD)
+    sent_y = jnp.concatenate(
+        (spread[:, 0].reshape(-1, HEAD), spread[:, 1].reshape(-1, HEAD)), axis=1
+    )
+    everything = lax.all_gather(sent_y, "y", axis=0, tiled=True)
+    key_block, value_block = jnp.split(everything, (HEAD,), axis=1)
+
     peaks = jnp.max(jnp.abs(normed), axis=0).reshape(tok_count, row_count)
+    peaks = jnp.where(present(spread), peaks, 0.0)
     docs = jnp.broadcast_to(doc_ids.astype(jnp.bfloat16), (tok_count, tok_dev))
     arrived = exchange(jnp.concatenate((peaks, docs), axis=1), TOK)
     input_peak = jnp.max(arrived[:, :row_count], axis=0).astype(jnp.float32)
@@ -126,35 +151,20 @@
         for part in jnp.split(coded, cuts, axis=2)
     )
 
-    even = (side == 0) & (all_scales[0, 0] > 0.0)
-    both_rows = jnp.concatenate(
-        (jnp.where(even, normed, other), jnp.where(even, other, normed)), axis=0
-    )
-    projected = jnp.dot(both_rows, gathered, preferred_element_type=jnp.float32)
-    pair_positions = (tok_index - side) * tok_dev + jnp.arange(2 * tok_dev, dtype=jnp.int32)
-    last = projected[:, half_query:]
-    turned = rotate(
-        projected.reshape(2 * tok_dev, heads_half + 1, HEAD), pair_positions.astype(jnp.float32)
-    )
-    kept = jnp.where(side == 0, turned[:, heads_half], last).astype(jnp.bfloat16)
-
-    spread = to_everyone(kept, LINE).reshape(line // 2, 2, 2 * tok_dev, HEAD)
-    spread = jnp.concatenate(
-        (spread[:, 0].reshape(-1, HEAD), spread[:, 1].reshape(-1, HEAD)), axis=1
-    )
-    everything = lax.all_gather(spread, "y", axis=0, tiled=True)
-    key_block, value_block = jnp.split(everything, (HEAD,), axis=1)
-
-    turned = turned[:, :heads_half].astype(jnp.bfloat16).reshape(2, tok_dev, half_query)
+    even = (side == 0) & present(all_scales)
+    both_rows = in_pair_order(even, normed, other)
+    turned = jnp.dot(both_rows, gathered_query, preferred_element_type=jnp.float32)
+    turned = rotate(turned.reshape(2 * tok_dev, -1, HEAD), pair_positions)
+    turned = turned.astype(jnp.bfloat16).reshape(2, tok_dev, half_query)
     mine = jnp.where(side == 0, turned[0], turned[1])
     swapped = lax.ppermute(jnp.where(side == 0, turned[1], turned[0]), "pair", swap)
     query = jnp.concatenate(
         (jnp.where(side == 0, mine, swapped), jnp.where(side == 0, swapped, mine)), axis=1
-    ).reshape(tok_dev, group_size, HEAD)
+    ).reshape(tok_dev, 1, group_size, HEAD)
 
     length = key_block.shape[0]
     scores = jnp.einsum(
-        "tgd,sd->gts", query, key_block, preferred_element_type=jnp.float32
+        "tkgd,skd->kgts", query, key_block[:, None, :], preferred_element_type=jnp.float32
     ) * (1.0 / math.sqrt(HEAD))
     query_positions = tok_index * tok_dev + jnp.arange(tok_dev, dtype=jnp.int32)
     key_positions = jnp.arange(length, dtype=jnp.int32)
@@ -162,23 +172,24 @@
         key_positions[None, :] <= query_positions[:, None]
     )
     scores = jnp.where(allowed, scores, -1e30)
-    highest = jnp.max(scores, axis=2, keepdims=True)
+    highest = jnp.max(scores, axis=3, keepdims=True)
     weights = jnp.where(allowed, jnp.exp(scores - highest), 0.0)
-    totals = jnp.sum(weights, axis=2)
+    totals = jnp.sum(weights, axis=3)
     accumulated = jnp.einsum(
-        "gts,sd->gtd",
+        "kgts,skd->kgtd",
         weights.astype(jnp.bfloat16),
-        value_block,
+        value_block[:, None, :],
         preferred_element_type=jnp.float32,
     )
     attended = (
         (accumulated / totals[..., None])
-        .transpose(1, 0, 2)
+        .transpose(2, 0, 1, 3)
         .reshape(tok_dev, group_size * HEAD)
         .astype(jnp.bfloat16)
     )
-    out_peak = to_everyone(jnp.max(jnp.abs(attended), axis=0), TOK)
-    out_scale = jnp.max(out_peak, axis=0).astype(jnp.float32)
+    out_peak = jnp.max(jnp.abs(attended), axis=0)
+    out_peak = jnp.max(to_everyone(out_peak, LINE), axis=0)
+    out_scale = jnp.max(to_everyone(out_peak, "y"), axis=0).astype(jnp.float32)
     return (
         attended,
         out_scale,

time: 237 us -> 228 us (0.962)
  blocking collectives: 55 us -> 22.1 us
  local copies, waits for them, and re-layouts: 11.6 us -> 22.2 us
  other arithmetic: 16.5 us -> 26.1 us
  starting transfers between devices: 44.4 us -> 49.3 us
  waiting for transfers between devices: 80.5 us -> 76.9 us
    all_gather x2 -> x3, waiting for transfers between devices: 34.3 us -> 0.02 us  [the longest x1 0.02 us: on_device(): everything = lax.all_gather(sent_y, 'y', axis=0, tiled=True)]
    all_to_all x2 -> x1, blocking collectives: 55 us -> 22.1 us  [exchange(): return lax.all_to_all(parts, axis, split_axis=0, concat_axis=0, tiled=True)]
    ppermute x1, waiting for transfers between devices: 0.01 us -> 24.9 us  [on_device(): lax.ppermute(lax.dynamic_slice_in_dim(normed, core * channels, channels,...]
    unnamed x30 -> x37, local copies, waits for them, and re-layouts: 3.29 us -> 9.18 us
    all_to_all x5 -> x8, waiting for transfers between devices: 44.5 us -> 48.8 us  [exchange(): return lax.all_to_all(parts, axis, split_axis=0, concat_axis=0, tiled=True)]
    sub x1, other arithmetic: 4.49 us -> 0.45 us  [rotate(): first * cosine - second * sine]
    select_n x1 -> x5, other arithmetic: 1.73 us -> 5.63 us  [the longest x2 4.59 us: in_pair_order(): jnp.where(even, own, other)]
    all_to_all x5 -> x8, starting transfers between devices: 37.4 us -> 40.7 us  [exchange(): return lax.all_to_all(parts, axis, split_axis=0, concat_axis=0, tiled=True)]
  transfers between devices with their start and end apart: 10 -> 14, of which waited for: 8 -> 8; matrix products, arithmetic and copies ran while one was open for 7% -> 22% of each run, Pallas kernels for 0% -> 0%
where the time goes in v3:
time: 228 us; the launch traced here: 226 us
  waiting for transfers between devices  76.9 us (34%)
  starting transfers between devices  49.3 us (22%)
  other arithmetic  26.1 us (11%)
  local copies, waits for them, and re-layouts  22.2 us (10%)
  blocking collectives  22.1 us (10%)
  between operations  16.8 us (7%)
  matrix products  13 us (6%)
    all_to_all x8, waiting for transfers between devices, exchange(): return lax.all_to_all(parts, axis, split_axis=0, concat_axis=0, tiled=True)  48.8 us
    all_to_all x8, starting transfers between devices, exchange(): return lax.all_to_all(parts, axis, split_axis=0, concat_axis=0, tiled=True)  40.7 us
    ppermute x1, waiting for transfers between devices, on_device(): lax.ppermute(lax.dynamic_slice_in_dim(normed, core * channels, channels,...  24.9 us
    all_to_all x1, blocking collectives, exchange(): return lax.all_to_all(parts, axis, split_axis=0, concat_axis=0, tiled=True)  22.1 us
    unnamed x37, local copies, waits for them, and re-layouts  9.18 us
    select_n x2, other arithmetic, in_pair_order(): jnp.where(even, own, other)  4.59 us
  transfers between devices with their start and end apart: 14, of which 8 were waited for; matrix products, arithmetic and copies ran while one was open for 22% of the time, Pallas kernels for 0%

profile of v3, /device:TPU:2, one launch (start us, length us, event | category | flops | bytes accessed | tf_op | source)
XLA Modules:
  0.0 226.3 jit_solution(1044954389254057516)
XLA Ops:
  7.2 0.9 pad_maximum_fusion.3
  8.2 22.1 %all_to_all.63 = bf16[8,128,128]{2,1,0:T(8,128)(2,1)} all-to-all(bf16[8,128,128]{2,1,0:T(8,128)(2,1)S(1)} %bitcast.121), channel_id=1, replica_groups=mesh['y'=8,'z'=4,'pair'=2,'x'=4,'core'=2] {'z','pair'}, dimensions={0} | all-to-all | bytes 524288 | tf_op jit(solution)/shard_map/all_to_all | solution.py:19
  30.3 1.8 fusion.8
  32.1 1.9 abs_reduce_fusion
  35.8 0.8 broadcast_in_dim.73
  36.6 3.5 %all-to-all-start = ((bf16[8,128,256]{2,1,0:T(8,128)(2,1)}), bf16[8,128,256]{2,1,0:T(8,128)(2,1)S(1)}, u32[]{:S(2)}, u32[]{:S(2)}) async-start(bf16[8,128,256]{2,1,0:T(8,128)(2,1)} %bitcast.3), calls=%async_computation | async-start | bytes 1048576 | tf_op jit(solution)/shard_map/all_to_all | solution.py:19
  40.2 3.8 %collective-permute-start = (bf16[96,4096]{1,0:T(8,128)(2,1)S(1)}, bf16[96,4096]{1,0:T(8,128)(2,1)}, u32[]{:S(2)}, u32[]{:S(2)}) collective-permute-start(bf16[96,4096]{1,0:T(8,128)(2,1)S(1)} %constant_dynamic-slice_fusion), channel_id=1, source_target_pairs={{0,8},{8,0},{1,9},{9,1},{2,10},{10,2},{3,11},{11,3},{4,12},{12,4},... | collective-permute-start | bytes 2359304 | tf_op jit(solution)/shard_map/ppermute | solution.py:88
  44.3 24.9 %collective-permute-done = bf16[96,4096]{1,0:T(8,128)(2,1)} collective-permute-done((bf16[96,4096]{1,0:T(8,128)(2,1)S(1)}, bf16[96,4096]{1,0:T(8,128)(2,1)}, u32[]{:S(2)}, u32[]{:S(2)}) %collective-permute-start) | collective-permute-done | bytes 786464 | tf_op jit(solution)/shard_map/ppermute | solution.py:88
  69.2 1.9 collective-permute-start.1
  71.1 0.8 copy-done.1
  73.3 0.9 reshape.287
  74.1 4.9 %all-to-all-start.4 = ((bf16[8,2,6208]{2,1,0:T(2,128)(2,1)}), bf16[8,2,6208]{2,1,0:T(2,128)(2,1)S(1)}, u32[]{:S(2)}, u32[]{:S(2)}) async-start(bf16[8,2,6208]{2,1,0:T(2,128)(2,1)} %reshape.287), calls=%async_computation.4 | async-start | bytes 401408 | tf_op jit(solution)/shard_map/all_to_all | solution.py:19
  79.1 1.5 copy.42
  81.7 1.5 broadcast_select_fusion.5
  83.2 2.3 %broadcast_select_fusion.3 = (bf16[96,8192]{1,0:T(8,128)(2,1)}, bf16[96,8192]{1,0:T(8,128)(2,1)}) fusion(bf16[96,8192]{1,0:T(8,128)(2,1)S(1)} %get-tuple-element.15, pred[]{:T(512)S(6)} %and.14, bf16[96,4096]{1,0:T(8,128)(2,1)S(1)} %get-tuple-element.21, bf16[96,4096]{1,0:T(8,128)(2,1)S(1)} %get-tuple-element.20), kind=kLoop, calls=%fused_computation.31 | loop fusion | flops 4718592 | bytes 6291457 | tf_op jit(solution)/shard_map/jit(_where)/select_n | solution.py:39
  85.5 3.7 %fusion.11 = f32[192,128]{1,0:T(8,128)S(1)} fusion(bf16[8192,128]{1,0:T(8,128)(2,1)} %all-gather.4.cloned.1.call-done, bf16[96,8192]{1,0:T(8,128)(2,1)} %get-tuple-element.19, bf16[96,8192]{1,0:T(8,128)(2,1)} %get-tuple-element.18), kind=kOutput, calls=%fused_computation.14 | convolution fusion | flops 408944640 | bytes 5341184 | tf_op jit(solution)/shard_map/dot_general | solution.py:103
  90.4 1.6 broadcast_in_dim.76
  92.0 5.8 %all-to-all-start.2 = ((bf16[8,192,128]{2,1,0:T(8,128)(2,1)}), bf16[8,192,128]{2,1,0:T(8,128)(2,1)}, u32[]{:S(2)}, u32[]{:S(2)}) async-start(bf16[8,192,128]{2,1,0:T(8,128)(2,1)} %broadcast_in_dim.76), calls=%async_computation.2 | async-start | bytes 786432 | tf_op jit(solution)/shard_map/all_to_all | solution.py:19
  98.8 1.1 multiply_cosine_fusion
  99.9 1.0 reshape.288
  100.9 1.0 copy.64
  101.9 10.9 %all-to-all-done.2 = bf16[8,192,128]{2,1,0:T(8,128)(2,1)} async-done(((bf16[8,192,128]{2,1,0:T(8,128)(2,1)}), bf16[8,192,128]{2,1,0:T(8,128)(2,1)}, u32[]{:S(2)}, u32[]{:S(2)}) %all-to-all-start.2) | async-done | bytes 393248 | tf_op jit(solution)/shard_map/all_to_all | solution.py:19
  112.8 1.2 slice.82
  116.7 8.4 %all-to-all-start.3 = ((bf16[64,1,224]{2,1,0:T(2,128)(2,1)}), bf16[64,1,224]{2,1,0:T(2,128)(2,1)}, u32[]{:S(2)}, u32[]{:S(2)}) async-start(bf16[64,1,224]{2,1,0:T(2,128)(2,1)} %copy.27), calls=%async_computation.3 | async-start | bytes 131072 | tf_op jit(solution)/shard_map/all_to_all | solution.py:19
  125.2 1.1 fusion.44
  126.2 0.8 pad_maximum_fusion.1
  127.0 10.6 %all-to-all-done.3 = bf16[64,1,224]{2,1,0:T(2,128)(2,1)} async-done(((bf16[64,1,224]{2,1,0:T(2,128)(2,1)}), bf16[64,1,224]{2,1,0:T(2,128)(2,1)}, u32[]{:S(2)}, u32[]{:S(2)}) %all-to-all-start.3) | async-done | bytes 28704 | tf_op jit(solution)/shard_map/all_to_all | solution.py:19
  137.7 0.8 copy.67
  139.2 1.4 reshape.281
  140.8 0.8 broadcast_in_dim.81
  141.5 4.6 %all-to-all-start.5 = ((f32[64,1,768]{2,1,0:T(1,128)}), f32[64,1,768]{2,1,0:T(1,128)S(1)}, u32[]{:S(2)}, u32[]{:S(2)}) async-start(f32[64,1,768]{2,1,0:T(1,128)} %broadcast_in_dim.81), calls=%async_computation.5 | async-start | bytes 393216 | tf_op jit(solution)/shard_map/all_to_all | solution.py:19
  146.2 2.1 fusion.19
  148.3 1.3 dynamic-slice_divide_fusion
  149.6 11.2 %all-to-all-done.5 = f32[64,1,768]{2,1,0:T(1,128)S(1)} async-done(((f32[64,1,768]{2,1,0:T(1,128)}), f32[64,1,768]{2,1,0:T(1,128)S(1)}, u32[]{:S(2)}, u32[]{:S(2)}) %all-to-all-start.5) | async-done | bytes 196640 | tf_op jit(solution)/shard_map/all_to_all | solution.py:19
  161.6 4.8 %all-to-all-start.6 = ((f32[8,1,768]{2,1,0:T(1,128)}), f32[8,1,768]{2,1,0:T(1,128)S(1)}, u32[]{:S(2)}, u32[]{:S(2)}) async-start(f32[8,1,768]{2,1,0:T(1,128)} %broadcast_in_dim.82), calls=%async_computation.6 | async-start | bytes 49152 | tf_op jit(solution)/shard_map/all_to_all | solution.py:19
  167.5 2.9 %all-to-all-done.6 = f32[8,1,768]{2,1,0:T(1,128)S(1)} async-done(((f32[8,1,768]{2,1,0:T(1,128)}), f32[8,1,768]{2,1,0:T(1,128)S(1)}, u32[]{:S(2)}, u32[]{:S(2)}) %all-to-all-start.6) | async-done | bytes 24608 | tf_op jit(solution)/shard_map/all_to_all | solution.py:19
  171.5 2.3 %broadcast_select_fusion.1 = (bf16[96,8192]{1,0:T(8,128)(2,1)}, bf16[96,8192]{1,0:T(8,128)(2,1)}) fusion(bf16[96,8192]{1,0:T(8,128)(2,1)S(1)} %get-tuple-element.15, pred[]{:T(512)S(6)} %and.16, bf16[96,4096]{1,0:T(8,128)(2,1)S(1)} %get-tuple-element.21, bf16[96,4096]{1,0:T(8,128)(2,1)S(1)} %get-tuple-element.20), kind=kLoop, calls=%fused_computation.29 | loop fusion | flops 4718592 | bytes 6291457 | tf_op jit(solution)/shard_map/jit(_where)/select_n | solution.py:39
  173.8 4.3 %fusion.15 = f32[192,256]{1,0:T(8,128)S(1)} fusion(bf16[8192,256]{1,0:T(8,128)(2,1)} %all-gather.8.cloned.1.call-done, bf16[96,8192]{1,0:T(8,128)(2,1)} %get-tuple-element.17, bf16[96,8192]{1,0:T(8,128)(2,1)} %get-tuple-element.16), kind=kOutput, calls=%fused_computation.18 | convolution fusion | flops 811597824 | bytes 7536640 | tf_op jit(solution)/shard_map/dot_general | solution.py:156
  178.9 2.7 %collective-permute-start.2 = (bf16[96,256]{1,0:T(8,128)(2,1)S(1)}, bf16[96,256]{1,0:T(8,128)(2,1)S(1)}, u32[]{:S(2)}, u32[]{:S(2)}) collective-permute-start(bf16[96,256]{1,0:T(8,128)(2,1)S(1)} %bitcast.147), channel_id=1, source_target_pairs={{0,8},{8,0},{1,9},{9,1},{2,10},{10,2},{3,11},{11,3},{4,12},{12,4},... | collective-permute-start | bytes 147464 | tf_op jit(solution)/shard_map/ppermute | solution.py:160
  181.8 3.1 %collective-permute-done.2 = bf16[96,256]{1,0:T(8,128)(2,1)S(1)} collective-permute-done((bf16[96,256]{1,0:T(8,128)(2,1)S(1)}, bf16[96,256]{1,0:T(8,128)(2,1)S(1)}, u32[]{:S(2)}, u32[]{:S(2)}) %collective-permute-start.2) | collective-permute-done | bytes 49184 | tf_op jit(solution)/shard_map/ppermute | solution.py:160
  185.0 3.3 %fusion.46 = (f32[4,96]{1,0:T(4,128)S(1)}, f32[1,4,96,6144]{3,2,1,0:T(8,128)S(1)}) fusion(bf16[6144,256]{1,0:T(8,128)(2,1)} %all-gather.6.cloned.1.call-done, pred[96,6144]{1,0:T(8,128)(4,1)S(1)} %copy-done.2, bf16[96,256]{1,0:T(8,128)(2,1)S(1)} %get-tuple-element.35, bf16[96,256]{1,0:T(8,128)(2,1)S(1)} %get-tuple-element.34), kind=kOutput, calls=%fused_computation.103 | convolution fusion | flops 611253888 | bytes 11699712 | tf_op jit(solution)/shard_map/tkgd,skd->kgts/dot_general | solution.py:166
  188.3 2.2 fusion
  190.6 1.7 abs_reduce_fusion.3
  193.6 4.6 %all-to-all-start.7 = ((bf16[8,2,256]{2,1,0:T(2,128)(2,1)}), bf16[8,2,256]{2,1,0:T(2,128)(2,1)S(1)}, u32[]{:S(2)}, u32[]{:S(2)}) async-start(bf16[8,2,256]{2,1,0:T(2,128)(2,1)} %reshape.289), calls=%async_computation.7 | async-start | bytes 16384 | tf_op jit(solution)/shard_map/all_to_all | solution.py:19
  198.1 7.7 %all-to-all-done.7 = bf16[8,2,256]{2,1,0:T(2,128)(2,1)S(1)} async-done(((bf16[8,2,256]{2,1,0:T(2,128)(2,1)}), bf16[8,2,256]{2,1,0:T(2,128)(2,1)S(1)}, u32[]{:S(2)}, u32[]{:S(2)}) %all-to-all-start.7) | async-done | bytes 8224 | tf_op jit(solution)/shard_map/all_to_all | solution.py:19
  207.2 4.2 %all-to-all-start.8 = ((bf16[8,2,256]{2,1,0:T(2,128)(2,1)}), bf16[8,2,256]{2,1,0:T(2,128)(2,1)S(1)}, u32[]{:S(2)}, u32[]{:S(2)}) async-start(bf16[8,2,256]{2,1,0:T(2,128)(2,1)} %reshape.291), calls=%async_computation.8 | async-start | bytes 16384 | tf_op jit(solution)/shard_map/all_to_all | solution.py:19
  212.1 0.9 copy.46
  213.7 5.5 %all-to-all-done.8 = bf16[8,2,256]{2,1,0:T(2,128)(2,1)S(1)} async-done(((bf16[8,2,256]{2,1,0:T(2,128)(2,1)}), bf16[8,2,256]{2,1,0:T(2,128)(2,1)S(1)}, u32[]{:S(2)}, u32[]{:S(2)}) %all-to-all-start.8) | async-done | bytes 8224 | tf_op jit(solution)/shard_map/all_to_all | solution.py:19
  (96 shorter events, 16.6 us)
Async XLA Ops:
  7.2 24.9 %copy-start = (bf16[96,8192]{1,0:T(8,128)(2,1)S(1)}, bf16[96,8192]{1,0:T(8,128)(2,1)}, u32[]{:S(2)}) copy-start(bf16[96,8192]{1,0:T(8,128)(2,1)} %param.6) | copy-start | bytes 4718596
  7.2 78.3 %all-gather.4.cloned.1.call-start = ((), (), s32[]{:S(2)}) async-start(), calls=%async_computation.9 | async-start | bytes 2359296 | tf_op jit(solution)/shard_map/all_gather | solution.py:80
  32.1 3.6 %copy-start.5 = (bf16[128,512]{1,0:T(8,128)(2,1)S(1)}, bf16[128,512]{1,0:T(8,128)(2,1)}, u32[]{:S(2)}) copy-start(bf16[128,512]{1,0:T(8,128)(2,1)} %param.8) | copy-start | bytes 393220
  34.1 9.9 %copy-start.6 = (bf16[128,128]{1,0:T(8,128)(2,1)S(1)}, bf16[128,128]{1,0:T(8,128)(2,1)}, u32[]{:S(2)}) copy-start(bf16[128,128]{1,0:T(8,128)(2,1)} %param.9) | copy-start | bytes 98308
  34.1 10.0 %copy-start.7 = (bf16[128,128]{1,0:T(8,128)(2,1)S(1)}, bf16[128,128]{1,0:T(8,128)(2,1)}, u32[]{:S(2)}) copy-start(bf16[128,128]{1,0:T(8,128)(2,1)} %param.10) | copy-start | bytes 98308
  36.6 34.5 %all-to-all-start = ((bf16[8,128,256]{2,1,0:T(8,128)(2,1)}), bf16[8,128,256]{2,1,0:T(8,128)(2,1)S(1)}, u32[]{:S(2)}, u32[]{:S(2)}) async-start(bf16[8,128,256]{2,1,0:T(8,128)(2,1)} %bitcast.3), calls=%async_computation | async-start | bytes 1048576 | tf_op jit(solution)/shard_map/all_to_all | solution.py:19
  40.1 133.7 %all-gather.8.cloned.1.call-start = ((), (), s32[]{:S(2)}) async-start(), calls=%async_computation.11 | async-start | bytes 4718592 | tf_op jit(solution)/shard_map/all_gather | solution.py:93
  40.2 28.9 %collective-permute-start = (bf16[96,4096]{1,0:T(8,128)(2,1)S(1)}, bf16[96,4096]{1,0:T(8,128)(2,1)}, u32[]{:S(2)}, u32[]{:S(2)}) collective-permute-start(bf16[96,4096]{1,0:T(8,128)(2,1)S(1)} %constant_dynamic-slice_fusion), channel_id=1, source_target_pairs={{0,8},{8,0},{1,9},{9,1},{2,10},{10,2},{3,11},{11,3},{4,12},{12,4},... | collective-permute-start | bytes 2359304 | tf_op jit(solution)/shard_map/ppermute | solution.py:88
  69.2 12.5 %collective-permute-start.1 = (bf16[96,4096]{1,0:T(8,128)(2,1)}, bf16[96,4096]{1,0:T(8,128)(2,1)}, u32[]{:S(2)}, u32[]{:S(2)}) collective-permute-start(bf16[96,4096]{1,0:T(8,128)(2,1)} %collective-permute-done), channel_id=1, source_target_pairs={{0,1},{1,0},{2,3},{3,2},{4,5},{5,4},{6,7},{7,6},{8,9},{9,8},{10,11... | collective-permute-start | bytes 2359304 | tf_op jit(solution)/shard_map/ppermute | solution.py:94
  71.1 0.8 copy-start.1
  74.1 16.3 %all-to-all-start.4 = ((bf16[8,2,6208]{2,1,0:T(2,128)(2,1)}), bf16[8,2,6208]{2,1,0:T(2,128)(2,1)S(1)}, u32[]{:S(2)}, u32[]{:S(2)}) async-start(bf16[8,2,6208]{2,1,0:T(2,128)(2,1)} %reshape.287), calls=%async_computation.4 | async-start | bytes 401408 | tf_op jit(solution)/shard_map/all_to_all | solution.py:19
  85.5 12.3 %copy-start.8 = (s32[96]{0:T(128)S(1)}, s32[96]{0:T(128)}, u32[]{:S(2)}) copy-start(s32[96]{0:T(128)} %param.11) | copy-start | bytes 1156
  92.0 20.8 %all-to-all-start.2 = ((bf16[8,192,128]{2,1,0:T(8,128)(2,1)}), bf16[8,192,128]{2,1,0:T(8,128)(2,1)}, u32[]{:S(2)}, u32[]{:S(2)}) async-start(bf16[8,192,128]{2,1,0:T(8,128)(2,1)} %broadcast_in_dim.76), calls=%async_computation.2 | async-start | bytes 786432 | tf_op jit(solution)/shard_map/all_to_all | solution.py:19
  99.9 46.3 %copy-start.9 = (s32[96]{0:T(128)S(1)}, s32[96]{0:T(128)}, u32[]{:S(2)}) copy-start(s32[96]{0:T(128)} %iota_add_fusion) | copy-start | bytes 1156
  116.7 21.0 %all-to-all-start.3 = ((bf16[64,1,224]{2,1,0:T(2,128)(2,1)}), bf16[64,1,224]{2,1,0:T(2,128)(2,1)}, u32[]{:S(2)}, u32[]{:S(2)}) async-start(bf16[64,1,224]{2,1,0:T(2,128)(2,1)} %copy.27), calls=%async_computation.3 | async-start | bytes 131072 | tf_op jit(solution)/shard_map/all_to_all | solution.py:19
  125.1 59.9 %all-gather.6.cloned.1.call-start = ((), (), s32[]{:S(2)}) async-start(), calls=%async_computation.10 | async-start | bytes 3538944 | tf_op jit(solution)/shard_map/all_gather | solution.py:111
  141.5 19.3 %all-to-all-start.5 = ((f32[64,1,768]{2,1,0:T(1,128)}), f32[64,1,768]{2,1,0:T(1,128)S(1)}, u32[]{:S(2)}, u32[]{:S(2)}) async-start(f32[64,1,768]{2,1,0:T(1,128)} %broadcast_in_dim.81), calls=%async_computation.5 | async-start | bytes 393216 | tf_op jit(solution)/shard_map/all_to_all | solution.py:19
  161.6 8.7 %all-to-all-start.6 = ((f32[8,1,768]{2,1,0:T(1,128)}), f32[8,1,768]{2,1,0:T(1,128)S(1)}, u32[]{:S(2)}, u32[]{:S(2)}) async-start(f32[8,1,768]{2,1,0:T(1,128)} %broadcast_in_dim.82), calls=%async_computation.6 | async-start | bytes 49152 | tf_op jit(solution)/shard_map/all_to_all | solution.py:19
  173.8 4.4 %copy-start.3 = (f32[192,64]{1,0:T(8,128)S(1)}, f32[192,64]{1,0:T(8,128)}, u32[]{:S(2)}) copy-start(f32[192,64]{1,0:T(8,128)} %get-tuple-element.38) | copy-start | bytes 147460
  173.8 4.4 %copy-start.4 = (f32[192,64]{1,0:T(8,128)S(1)}, f32[192,64]{1,0:T(8,128)}, u32[]{:S(2)}) copy-start(f32[192,64]{1,0:T(8,128)} %get-tuple-element.39) | copy-start | bytes 147460
  173.8 11.2 %copy-start.2 = (pred[96,6144]{1,0:T(8,128)(4,1)S(1)}, pred[96,6144]{1,0:T(8,128)(4,1)}, u32[]{:S(2)}) copy-start(pred[96,6144]{1,0:T(8,128)(4,1)} %fusion.19) | copy-start | bytes 1769476
  178.9 6.0 %collective-permute-start.2 = (bf16[96,256]{1,0:T(8,128)(2,1)S(1)}, bf16[96,256]{1,0:T(8,128)(2,1)S(1)}, u32[]{:S(2)}, u32[]{:S(2)}) collective-permute-start(bf16[96,256]{1,0:T(8,128)(2,1)S(1)} %bitcast.147), channel_id=1, source_target_pairs={{0,8},{8,0},{1,9},{9,1},{2,10},{10,2},{3,11},{11,3},{4,12},{12,4},... | collective-permute-start | bytes 147464 | tf_op jit(solution)/shard_map/ppermute | solution.py:160
  188.3 2.2 copy-start.10
  193.6 12.3 %all-to-all-start.7 = ((bf16[8,2,256]{2,1,0:T(2,128)(2,1)}), bf16[8,2,256]{2,1,0:T(2,128)(2,1)S(1)}, u32[]{:S(2)}, u32[]{:S(2)}) async-start(bf16[8,2,256]{2,1,0:T(2,128)(2,1)} %reshape.289), calls=%async_computation.7 | async-start | bytes 16384 | tf_op jit(solution)/shard_map/all_to_all | solution.py:19
  207.2 11.9 %all-to-all-start.8 = ((bf16[8,2,256]{2,1,0:T(2,128)(2,1)}), bf16[8,2,256]{2,1,0:T(2,128)(2,1)S(1)}, u32[]{:S(2)}, u32[]{:S(2)}) async-start(bf16[8,2,256]{2,1,0:T(2,128)(2,1)} %reshape.291), calls=%async_computation.8 | async-start | bytes 16384 | tf_op jit(solution)/shard_map/all_to_all | solution.py:19
Sparse Core Ops, SparseCore 0:
  30.4 39.6 all-gather.3
  72.1 57.4 all-gather.7
  131.8 50.8 all-gather.5

commit v4 on v3

--- a/solution.py
+++ b/solution.py
@@ -112,7 +112,7 @@
     key_block, value_block = jnp.split(everything, (HEAD,), axis=1)
 
     peaks = jnp.max(jnp.abs(normed), axis=0).reshape(tok_count, row_count)
-    peaks = jnp.where(present(spread), peaks, 0.0)
+    peaks = jnp.where(present(along_z), peaks, 0.0)
     docs = jnp.broadcast_to(doc_ids.astype(jnp.bfloat16), (tok_count, tok_dev))
     arrived = exchange(jnp.concatenate((peaks, docs), axis=1), TOK)
     input_peak = jnp.max(arrived[:, :row_count], axis=0).astype(jnp.float32)
@@ -133,7 +133,9 @@
 
     smoothing = smooth_from(input_peak, weight_peak)
     column_peak = jnp.max(jnp.abs(smoothing[:, None] * block.astype(jnp.float32)), axis=0)
-    column_peak = jnp.max(to_everyone(column_peak, TOK), axis=0)
+    column_peak = jnp.where(present(spread), column_peak, 0.0)
+    column_peak = jnp.max(to_everyone(column_peak, LINE), axis=0)
+    column_peak = jnp.max(to_everyone(column_peak, "y"), axis=0)
     scale = jnp.maximum(column_peak, 1e-05) / 127.0
     all_scales = to_everyone(scale, TP)
     scales = jnp.split(scale, cuts)
@@ -187,9 +189,9 @@
         .reshape(tok_dev, group_size * HEAD)
         .astype(jnp.bfloat16)
     )
-    out_peak = jnp.max(jnp.abs(attended), axis=0)
+    out_peak = jnp.max(jnp.abs(attended), axis=0).astype(jnp.float32)
     out_peak = jnp.max(to_everyone(out_peak, LINE), axis=0)
-    out_scale = jnp.max(to_everyone(out_peak, "y"), axis=0).astype(jnp.float32)
+    out_scale = jnp.max(to_everyone(out_peak, "y"), axis=0)
     return (
         attended,
         out_scale,

time: 228 us -> 222 us (0.974)
  waiting for transfers between devices: 76.9 us -> 70.3 us
  starting transfers between devices: 49.3 us -> 55.4 us
  local copies, waits for them, and re-layouts: 22.2 us -> 19.1 us
    ppermute x1, waiting for transfers between devices: 24.9 us -> 3.61 us  [on_device(): lax.ppermute(lax.dynamic_slice_in_dim(normed, core * channels, channels,...]
    all_to_all x8 -> x9, waiting for transfers between devices: 48.8 us -> 63.4 us  [exchange(): return lax.all_to_all(parts, axis, split_axis=0, concat_axis=0, tiled=True)]
    all_to_all x8 -> x9, starting transfers between devices: 40.7 us -> 47 us  [exchange(): return lax.all_to_all(parts, axis, split_axis=0, concat_axis=0, tiled=True)]
    unnamed x37 -> x33, local copies, waits for them, and re-layouts: 9.18 us -> 4.9 us
  transfers between devices with their start and end apart: 14 -> 15, of which waited for: 8 -> 10; matrix products, arithmetic and copies ran while one was open for 22% -> 21% of each run, Pallas kernels for 0% -> 0%
where the time goes in v4:
time: 222 us; the launch traced here: 221 us
  waiting for transfers between devices  70.3 us (32%)
  starting transfers between devices  55.4 us (25%)
  other arithmetic  24.2 us (11%)
  blocking collectives  22.1 us (10%)
  local copies, waits for them, and re-layouts  19.1 us (9%)
  between operations  16.9 us (8%)
  matrix products  12.8 us (6%)
    all_to_all x9, waiting for transfers between devices, exchange(): return lax.all_to_all(parts, axis, split_axis=0, concat_axis=0, tiled=True)  63.4 us
    all_to_all x9, starting transfers between devices, exchange(): return lax.all_to_all(parts, axis, split_axis=0, concat_axis=0, tiled=True)  47 us
    all_to_all x1, blocking collectives, exchange(): return lax.all_to_all(parts, axis, split_axis=0, concat_axis=0, tiled=True)  22.1 us
    unnamed x33, local copies, waits for them, and re-layouts  4.9 us
    select_n x2, other arithmetic, in_pair_order(): jnp.where(even, own, other)  4.61 us
  transfers between devices with their start and end apart: 15, of which 10 were waited for; matrix products, arithmetic and copies ran while one was open for 21% of the time, Pallas kernels for 0%

profile of v4, /device:TPU:2, one launch (start us, length us, event | category | flops | bytes accessed | tf_op | source)
XLA Modules:
  0.0 220.8 jit_solution(6383678487275785804)
XLA Ops:
  7.2 0.9 pad_maximum_fusion.3
  8.2 22.1 %all_to_all.69 = bf16[8,128,128]{2,1,0:T(8,128)(2,1)} all-to-all(bf16[8,128,128]{2,1,0:T(8,128)(2,1)S(1)} %bitcast.123), channel_id=1, replica_groups=mesh['y'=8,'z'=4,'pair'=2,'x'=4,'core'=2] {'z','pair'}, dimensions={0} | all-to-all | bytes 524288 | tf_op jit(solution)/shard_map/all_to_all | solution.py:19
  30.3 1.8 fusion.8
  32.1 1.3 abs_reduce_fusion
  35.2 0.8 broadcast_in_dim.78
  36.0 3.5 %all-to-all-start = ((bf16[8,128,256]{2,1,0:T(8,128)(2,1)}), bf16[8,128,256]{2,1,0:T(8,128)(2,1)S(1)}, u32[]{:S(2)}, u32[]{:S(2)}) async-start(bf16[8,128,256]{2,1,0:T(8,128)(2,1)} %bitcast.3), calls=%async_computation | async-start | bytes 1048576 | tf_op jit(solution)/shard_map/all_to_all | solution.py:19
  39.6 0.9 constant_dynamic-slice_fusion
  40.5 3.8 %collective-permute-start = (bf16[96,4096]{1,0:T(8,128)(2,1)}, bf16[96,4096]{1,0:T(8,128)(2,1)}, u32[]{:S(2)}, u32[]{:S(2)}) collective-permute-start(bf16[96,4096]{1,0:T(8,128)(2,1)} %constant_dynamic-slice_fusion), channel_id=1, source_target_pairs={{0,8},{8,0},{1,9},{9,1},{2,10},{10,2},{3,11},{11,3},{4,12},{12,4},... | collective-permute-start | bytes 2359304 | tf_op jit(solution)/shard_map/ppermute | solution.py:88
  44.6 12.5 %all-to-all-done = bf16[8,128,256]{2,1,0:T(8,128)(2,1)S(1)} async-done(((bf16[8,128,256]{2,1,0:T(8,128)(2,1)}), bf16[8,128,256]{2,1,0:T(8,128)(2,1)S(1)}, u32[]{:S(2)}, u32[]{:S(2)}) %all-to-all-start) | async-done | bytes 524320 | tf_op jit(solution)/shard_map/all_to_all | solution.py:19
  57.1 0.8 copy-done.1
  59.2 0.9 reshape.291
  60.1 4.8 %all-to-all-start.4 = ((bf16[8,2,6208]{2,1,0:T(2,128)(2,1)}), bf16[8,2,6208]{2,1,0:T(2,128)(2,1)S(1)}, u32[]{:S(2)}, u32[]{:S(2)}) async-start(bf16[8,2,6208]{2,1,0:T(2,128)(2,1)} %reshape.291), calls=%async_computation.4 | async-start | bytes 401408 | tf_op jit(solution)/shard_map/all_to_all | solution.py:19
  65.0 3.6 %collective-permute-done = bf16[96,4096]{1,0:T(8,128)(2,1)} collective-permute-done((bf16[96,4096]{1,0:T(8,128)(2,1)}, bf16[96,4096]{1,0:T(8,128)(2,1)}, u32[]{:S(2)}, u32[]{:S(2)}) %collective-permute-start) | collective-permute-done | bytes 786464 | tf_op jit(solution)/shard_map/ppermute | solution.py:88
  68.6 1.9 collective-permute-start.1
  70.5 1.1 multiply_cosine_fusion
  74.2 12.0 %all-to-all-start.1 = ((bf16[64,1,224]{2,1,0:T(2,128)(2,1)}), bf16[64,1,224]{2,1,0:T(2,128)(2,1)S(1)}, u32[]{:S(2)}, u32[]{:S(2)}) async-start(bf16[64,1,224]{2,1,0:T(2,128)(2,1)} %copy.27), calls=%async_computation.1 | async-start | bytes 131072 | tf_op jit(solution)/shard_map/all_to_all | solution.py:19
  86.8 12.5 %all-to-all-done.1 = bf16[64,1,224]{2,1,0:T(2,128)(2,1)S(1)} async-done(((bf16[64,1,224]{2,1,0:T(2,128)(2,1)}), bf16[64,1,224]{2,1,0:T(2,128)(2,1)S(1)}, u32[]{:S(2)}, u32[]{:S(2)}) %all-to-all-start.1) | async-done | bytes 28704 | tf_op jit(solution)/shard_map/all_to_all | solution.py:19
  99.9 1.5 broadcast_select_fusion.5
  101.4 2.3 %broadcast_select_fusion.3 = (bf16[96,8192]{1,0:T(8,128)(2,1)}, bf16[96,8192]{1,0:T(8,128)(2,1)}) fusion(bf16[96,8192]{1,0:T(8,128)(2,1)S(1)} %get-tuple-element.15, pred[]{:T(512)S(6)} %and.15, bf16[96,4096]{1,0:T(8,128)(2,1)S(1)} %get-tuple-element.21, bf16[96,4096]{1,0:T(8,128)(2,1)S(1)} %get-tuple-element.20), kind=kLoop, calls=%fused_computation.31 | loop fusion | flops 4718592 | bytes 6291457 | tf_op jit(solution)/shard_map/jit(_where)/select_n | solution.py:39
  103.7 3.6 %fusion.11 = f32[192,128]{1,0:T(8,128)S(1)} fusion(bf16[8192,128]{1,0:T(8,128)(2,1)} %all-gather.4.cloned.1.call-done, bf16[96,8192]{1,0:T(8,128)(2,1)} %get-tuple-element.19, bf16[96,8192]{1,0:T(8,128)(2,1)} %get-tuple-element.18), kind=kOutput, calls=%fused_computation.14 | convolution fusion | flops 408944640 | bytes 5341184 | tf_op jit(solution)/shard_map/dot_general | solution.py:103
  107.9 0.8 broadcast_in_dim.84
  108.7 4.1 %all-to-all-start.3 = ((bf16[8,192,128]{2,1,0:T(8,128)(2,1)}), bf16[8,192,128]{2,1,0:T(8,128)(2,1)}, u32[]{:S(2)}, u32[]{:S(2)}) async-start(bf16[8,192,128]{2,1,0:T(8,128)(2,1)} %broadcast_in_dim.84), calls=%async_computation.3 | async-start | bytes 786432 | tf_op jit(solution)/shard_map/all_to_all | solution.py:19
  112.8 1.3 slice_convert_fusion
  114.2 1.4 reshape.284
  117.1 9.5 %all-to-all-done.3 = bf16[8,192,128]{2,1,0:T(8,128)(2,1)} async-done(((bf16[8,192,128]{2,1,0:T(8,128)(2,1)}), bf16[8,192,128]{2,1,0:T(8,128)(2,1)}, u32[]{:S(2)}, u32[]{:S(2)}) %all-to-all-start.3) | async-done | bytes 393248 | tf_op jit(solution)/shard_map/all_to_all | solution.py:19
  126.7 1.2 slice.86
  128.5 1.1 fusion.44
  129.5 0.8 pad_maximum_fusion.1
  131.0 3.3 %all-to-all-start.5 = ((f32[8,1,768]{2,1,0:T(1,128)}), f32[8,1,768]{2,1,0:T(1,128)S(1)}, u32[]{:S(2)}, u32[]{:S(2)}) async-start(f32[8,1,768]{2,1,0:T(1,128)} %broadcast_in_dim.87), calls=%async_computation.5 | async-start | bytes 49152 | tf_op jit(solution)/shard_map/all_to_all | solution.py:19
  134.4 2.1 fusion.19
  136.5 5.8 %all-to-all-done.5 = f32[8,1,768]{2,1,0:T(1,128)S(1)} async-done(((f32[8,1,768]{2,1,0:T(1,128)}), f32[8,1,768]{2,1,0:T(1,128)S(1)}, u32[]{:S(2)}, u32[]{:S(2)}) %all-to-all-start.5) | async-done | bytes 24608 | tf_op jit(solution)/shard_map/all_to_all | solution.py:19
  142.9 3.3 %all-to-all-start.6 = ((f32[8,1,768]{2,1,0:T(1,128)}), f32[8,1,768]{2,1,0:T(1,128)S(1)}, u32[]{:S(2)}, u32[]{:S(2)}) async-start(f32[8,1,768]{2,1,0:T(1,128)} %broadcast_in_dim.88), calls=%async_computation.6 | async-start | bytes 49152 | tf_op jit(solution)/shard_map/all_to_all | solution.py:19
  146.2 1.3 dynamic-slice_divide_fusion
  147.5 7.0 %all-to-all-done.6 = f32[8,1,768]{2,1,0:T(1,128)S(1)} async-done(((f32[8,1,768]{2,1,0:T(1,128)}), f32[8,1,768]{2,1,0:T(1,128)S(1)}, u32[]{:S(2)}, u32[]{:S(2)}) %all-to-all-start.6) | async-done | bytes 24608 | tf_op jit(solution)/shard_map/all_to_all | solution.py:19
  155.1 4.8 %all-to-all-start.7 = ((f32[8,1,768]{2,1,0:T(1,128)}), f32[8,1,768]{2,1,0:T(1,128)S(1)}, u32[]{:S(2)}, u32[]{:S(2)}) async-start(f32[8,1,768]{2,1,0:T(1,128)} %broadcast_in_dim.89), calls=%async_computation.7 | async-start | bytes 49152 | tf_op jit(solution)/shard_map/all_to_all | solution.py:19
  161.1 2.9 %all-to-all-done.7 = f32[8,1,768]{2,1,0:T(1,128)S(1)} async-done(((f32[8,1,768]{2,1,0:T(1,128)}), f32[8,1,768]{2,1,0:T(1,128)S(1)}, u32[]{:S(2)}, u32[]{:S(2)}) %all-to-all-start.7) | async-done | bytes 24608 | tf_op jit(solution)/shard_map/all_to_all | solution.py:19
  165.1 2.3 %broadcast_select_fusion.1 = (bf16[96,8192]{1,0:T(8,128)(2,1)}, bf16[96,8192]{1,0:T(8,128)(2,1)}) fusion(bf16[96,8192]{1,0:T(8,128)(2,1)S(1)} %get-tuple-element.15, pred[]{:T(512)S(6)} %and.16, bf16[96,4096]{1,0:T(8,128)(2,1)S(1)} %get-tuple-element.21, bf16[96,4096]{1,0:T(8,128)(2,1)S(1)} %get-tuple-element.20), kind=kLoop, calls=%fused_computation.29 | loop fusion | flops 4718592 | bytes 6291457 | tf_op jit(solution)/shard_map/jit(_where)/select_n | solution.py:39
  167.4 4.3 %fusion.15 = f32[192,256]{1,0:T(8,128)S(1)} fusion(bf16[8192,256]{1,0:T(8,128)(2,1)} %all-gather.8.cloned.1.call-done, bf16[96,8192]{1,0:T(8,128)(2,1)} %get-tuple-element.17, bf16[96,8192]{1,0:T(8,128)(2,1)} %get-tuple-element.16), kind=kOutput, calls=%fused_computation.18 | convolution fusion | flops 811597824 | bytes 7536640 | tf_op jit(solution)/shard_map/dot_general | solution.py:158
  172.6 2.6 %collective-permute-start.2 = (bf16[96,256]{1,0:T(8,128)(2,1)S(1)}, bf16[96,256]{1,0:T(8,128)(2,1)S(1)}, u32[]{:S(2)}, u32[]{:S(2)}) collective-permute-start(bf16[96,256]{1,0:T(8,128)(2,1)S(1)} %bitcast.149), channel_id=1, source_target_pairs={{0,8},{8,0},{1,9},{9,1},{2,10},{10,2},{3,11},{11,3},{4,12},{12,4},... | collective-permute-start | bytes 147464 | tf_op jit(solution)/shard_map/ppermute | solution.py:162
  175.3 3.3 %collective-permute-done.2 = bf16[96,256]{1,0:T(8,128)(2,1)S(1)} collective-permute-done((bf16[96,256]{1,0:T(8,128)(2,1)S(1)}, bf16[96,256]{1,0:T(8,128)(2,1)S(1)}, u32[]{:S(2)}, u32[]{:S(2)}) %collective-permute-start.2) | collective-permute-done | bytes 49184 | tf_op jit(solution)/shard_map/ppermute | solution.py:162
  178.6 3.3 %fusion.46 = (f32[4,96]{1,0:T(4,128)S(1)}, f32[1,4,96,6144]{3,2,1,0:T(8,128)S(1)}) fusion(bf16[6144,256]{1,0:T(8,128)(2,1)} %all-gather.6.cloned.1.call-done, pred[96,6144]{1,0:T(8,128)(4,1)S(1)} %copy-done.3, bf16[96,256]{1,0:T(8,128)(2,1)S(1)} %get-tuple-element.35, bf16[96,256]{1,0:T(8,128)(2,1)S(1)} %get-tuple-element.34), kind=kOutput, calls=%fused_computation.105 | convolution fusion | flops 611253888 | bytes 11699712 | tf_op jit(solution)/shard_map/tkgd,skd->kgts/dot_general | solution.py:168
  181.9 2.2 %fusion = f32[4,96]{1,0:T(4,128)S(1)} fusion(f32[1,4,96,6144]{3,2,1,0:T(8,128)S(1)} %get-tuple-element.41, f32[4,96]{1,0:T(4,128)S(1)} %get-tuple-element.40, pred[96,6144]{1,0:T(8,128)(4,1)S(1)} %copy-done.3), kind=kLoop, calls=%fused_computation.2 | loop fusion | flops 7077504 | bytes 10030080 | tf_op jit(solution)/shard_map/reduce_sum | solution.py:179
  184.2 1.7 abs_reduce_fusion.3
  186.5 6.7 %all-to-all-start.8 = ((f32[8,1,512]{2,1,0:T(1,128)}), f32[8,1,512]{2,1,0:T(1,128)S(1)}, u32[]{:S(2)}, u32[]{:S(2)}) async-start(f32[8,1,512]{2,1,0:T(1,128)} %broadcast_in_dim.92), calls=%async_computation.8 | async-start | bytes 32768 | tf_op jit(solution)/shard_map/all_to_all | solution.py:19
  193.2 7.8 %all-to-all-done.8 = f32[8,1,512]{2,1,0:T(1,128)S(1)} async-done(((f32[8,1,512]{2,1,0:T(1,128)}), f32[8,1,512]{2,1,0:T(1,128)S(1)}, u32[]{:S(2)}, u32[]{:S(2)}) %all-to-all-start.8) | async-done | bytes 16416 | tf_op jit(solution)/shard_map/all_to_all | solution.py:19
  201.6 4.3 %all-to-all-start.9 = ((f32[8,1,512]{2,1,0:T(1,128)}), f32[8,1,512]{2,1,0:T(1,128)S(1)}, u32[]{:S(2)}, u32[]{:S(2)}) async-start(f32[8,1,512]{2,1,0:T(1,128)} %broadcast_in_dim.93), calls=%async_computation.9 | async-start | bytes 32768 | tf_op jit(solution)/shard_map/all_to_all | solution.py:19
  206.6 0.9 copy.48
  208.2 5.5 %all-to-all-done.9 = f32[8,1,512]{2,1,0:T(1,128)S(1)} async-done(((f32[8,1,512]{2,1,0:T(1,128)}), f32[8,1,512]{2,1,0:T(1,128)S(1)}, u32[]{:S(2)}, u32[]{:S(2)}) %all-to-all-start.9) | async-done | bytes 16416 | tf_op jit(solution)/shard_map/all_to_all | solution.py:19
  (95 shorter events, 15.7 us)
Async XLA Ops:
  7.2 24.9 %copy-start = (bf16[96,8192]{1,0:T(8,128)(2,1)S(1)}, bf16[96,8192]{1,0:T(8,128)(2,1)}, u32[]{:S(2)}) copy-start(bf16[96,8192]{1,0:T(8,128)(2,1)} %param.6) | copy-start | bytes 4718596
  7.2 96.5 %all-gather.4.cloned.1.call-start = ((), (), s32[]{:S(2)}) async-start(), calls=%async_computation.10 | async-start | bytes 2359296 | tf_op jit(solution)/shard_map/all_gather | solution.py:80
  32.1 3.0 %copy-start.6 = (bf16[128,512]{1,0:T(8,128)(2,1)S(1)}, bf16[128,512]{1,0:T(8,128)(2,1)}, u32[]{:S(2)}) copy-start(bf16[128,512]{1,0:T(8,128)(2,1)} %param.8) | copy-start | bytes 393220
  33.5 10.8 %copy-start.7 = (bf16[128,128]{1,0:T(8,128)(2,1)S(1)}, bf16[128,128]{1,0:T(8,128)(2,1)}, u32[]{:S(2)}) copy-start(bf16[128,128]{1,0:T(8,128)(2,1)} %param.9) | copy-start | bytes 98308
  33.5 10.8 %copy-start.8 = (bf16[128,128]{1,0:T(8,128)(2,1)S(1)}, bf16[128,128]{1,0:T(8,128)(2,1)}, u32[]{:S(2)}) copy-start(bf16[128,128]{1,0:T(8,128)(2,1)} %param.10) | copy-start | bytes 98308
  35.2 29.7 %copy-start.9 = (s32[96]{0:T(128)S(1)}, s32[96]{0:T(128)}, u32[]{:S(2)}) copy-start(s32[96]{0:T(128)} %param.11) | copy-start | bytes 1156
  36.0 21.0 %all-to-all-start = ((bf16[8,128,256]{2,1,0:T(8,128)(2,1)}), bf16[8,128,256]{2,1,0:T(8,128)(2,1)S(1)}, u32[]{:S(2)}, u32[]{:S(2)}) async-start(bf16[8,128,256]{2,1,0:T(8,128)(2,1)} %bitcast.3), calls=%async_computation | async-start | bytes 1048576 | tf_op jit(solution)/shard_map/all_to_all | solution.py:19
  39.5 127.9 %all-gather.8.cloned.1.call-start = ((), (), s32[]{:S(2)}) async-start(), calls=%async_computation.12 | async-start | bytes 4718592 | tf_op jit(solution)/shard_map/all_gather | solution.py:93
  40.5 28.1 %collective-permute-start = (bf16[96,4096]{1,0:T(8,128)(2,1)}, bf16[96,4096]{1,0:T(8,128)(2,1)}, u32[]{:S(2)}, u32[]{:S(2)}) collective-permute-start(bf16[96,4096]{1,0:T(8,128)(2,1)} %constant_dynamic-slice_fusion), channel_id=1, source_target_pairs={{0,8},{8,0},{1,9},{9,1},{2,10},{10,2},{3,11},{11,3},{4,12},{12,4},... | collective-permute-start | bytes 2359304 | tf_op jit(solution)/shard_map/ppermute | solution.py:88
  57.1 0.8 copy-start.1
  57.9 14.0 %copy-start.2 = (bf16[8,128,256]{2,1,0:T(8,128)(2,1)S(1)}, bf16[8,128,256]{2,1,0:T(8,128)(2,1)}, u32[]{:S(2)}) copy-start(bf16[8,128,256]{2,1,0:T(8,128)(2,1)} %copy-done.1) | copy-start | bytes 1572868
  60.1 11.5 %all-to-all-start.4 = ((bf16[8,2,6208]{2,1,0:T(2,128)(2,1)}), bf16[8,2,6208]{2,1,0:T(2,128)(2,1)S(1)}, u32[]{:S(2)}, u32[]{:S(2)}) async-start(bf16[8,2,6208]{2,1,0:T(2,128)(2,1)} %reshape.291), calls=%async_computation.4 | async-start | bytes 401408 | tf_op jit(solution)/shard_map/all_to_all | solution.py:19
  68.6 31.3 %collective-permute-start.1 = (bf16[96,4096]{1,0:T(8,128)(2,1)}, bf16[96,4096]{1,0:T(8,128)(2,1)}, u32[]{:S(2)}, u32[]{:S(2)}) collective-permute-start(bf16[96,4096]{1,0:T(8,128)(2,1)} %collective-permute-done), channel_id=1, source_target_pairs={{0,1},{1,0},{2,3},{3,2},{4,5},{5,4},{6,7},{7,6},{8,9},{9,8},{10,11... | collective-permute-start | bytes 2359304 | tf_op jit(solution)/shard_map/ppermute | solution.py:94
  74.2 25.1 %all-to-all-start.1 = ((bf16[64,1,224]{2,1,0:T(2,128)(2,1)}), bf16[64,1,224]{2,1,0:T(2,128)(2,1)S(1)}, u32[]{:S(2)}, u32[]{:S(2)}) async-start(bf16[64,1,224]{2,1,0:T(2,128)(2,1)} %copy.27), calls=%async_computation.1 | async-start | bytes 131072 | tf_op jit(solution)/shard_map/all_to_all | solution.py:19
  108.7 18.0 %all-to-all-start.3 = ((bf16[8,192,128]{2,1,0:T(8,128)(2,1)}), bf16[8,192,128]{2,1,0:T(8,128)(2,1)}, u32[]{:S(2)}, u32[]{:S(2)}) async-start(bf16[8,192,128]{2,1,0:T(8,128)(2,1)} %broadcast_in_dim.84), calls=%async_computation.3 | async-start | bytes 786432 | tf_op jit(solution)/shard_map/all_to_all | solution.py:19
  112.8 65.8 %all-gather.6.cloned.1.call-start = ((), (), s32[]{:S(2)}) async-start(), calls=%async_computation.11 | async-start | bytes 3538944 | tf_op jit(solution)/shard_map/all_gather | solution.py:111
  131.0 11.2 %all-to-all-start.5 = ((f32[8,1,768]{2,1,0:T(1,128)}), f32[8,1,768]{2,1,0:T(1,128)S(1)}, u32[]{:S(2)}, u32[]{:S(2)}) async-start(f32[8,1,768]{2,1,0:T(1,128)} %broadcast_in_dim.87), calls=%async_computation.5 | async-start | bytes 49152 | tf_op jit(solution)/shard_map/all_to_all | solution.py:19
  142.9 11.6 %all-to-all-start.6 = ((f32[8,1,768]{2,1,0:T(1,128)}), f32[8,1,768]{2,1,0:T(1,128)S(1)}, u32[]{:S(2)}, u32[]{:S(2)}) async-start(f32[8,1,768]{2,1,0:T(1,128)} %broadcast_in_dim.88), calls=%async_computation.6 | async-start | bytes 49152 | tf_op jit(solution)/shard_map/all_to_all | solution.py:19
  155.1 8.8 %all-to-all-start.7 = ((f32[8,1,768]{2,1,0:T(1,128)}), f32[8,1,768]{2,1,0:T(1,128)S(1)}, u32[]{:S(2)}, u32[]{:S(2)}) async-start(f32[8,1,768]{2,1,0:T(1,128)} %broadcast_in_dim.89), calls=%async_computation.7 | async-start | bytes 49152 | tf_op jit(solution)/shard_map/all_to_all | solution.py:19
  167.4 4.4 %copy-start.4 = (f32[192,64]{1,0:T(8,128)S(1)}, f32[192,64]{1,0:T(8,128)}, u32[]{:S(2)}) copy-start(f32[192,64]{1,0:T(8,128)} %get-tuple-element.38) | copy-start | bytes 147460
  167.4 4.4 %copy-start.5 = (f32[192,64]{1,0:T(8,128)S(1)}, f32[192,64]{1,0:T(8,128)}, u32[]{:S(2)}) copy-start(f32[192,64]{1,0:T(8,128)} %get-tuple-element.39) | copy-start | bytes 147460
  167.4 11.2 %copy-start.3 = (pred[96,6144]{1,0:T(8,128)(4,1)S(1)}, pred[96,6144]{1,0:T(8,128)(4,1)}, u32[]{:S(2)}) copy-start(pred[96,6144]{1,0:T(8,128)(4,1)} %fusion.19) | copy-start | bytes 1769476
  172.6 6.0 %collective-permute-start.2 = (bf16[96,256]{1,0:T(8,128)(2,1)S(1)}, bf16[96,256]{1,0:T(8,128)(2,1)S(1)}, u32[]{:S(2)}, u32[]{:S(2)}) collective-permute-start(bf16[96,256]{1,0:T(8,128)(2,1)S(1)} %bitcast.149), channel_id=1, source_target_pairs={{0,8},{8,0},{1,9},{9,1},{2,10},{10,2},{3,11},{11,3},{4,12},{12,4},... | collective-permute-start | bytes 147464 | tf_op jit(solution)/shard_map/ppermute | solution.py:162
  181.9 2.2 %copy-start.10 = (bf16[6144,256]{1,0:T(8,128)(2,1)S(1)}, bf16[6144,256]{1,0:T(8,128)(2,1)}, u32[]{:S(2)}) copy-start(bf16[6144,256]{1,0:T(8,128)(2,1)} %all-gather.6.cloned.1.call-done) | copy-start | bytes 9437188
  186.5 14.5 %all-to-all-start.8 = ((f32[8,1,512]{2,1,0:T(1,128)}), f32[8,1,512]{2,1,0:T(1,128)S(1)}, u32[]{:S(2)}, u32[]{:S(2)}) async-start(f32[8,1,512]{2,1,0:T(1,128)} %broadcast_in_dim.92), calls=%async_computation.8 | async-start | bytes 32768 | tf_op jit(solution)/shard_map/all_to_all | solution.py:19
  201.6 12.1 %all-to-all-start.9 = ((f32[8,1,512]{2,1,0:T(1,128)}), f32[8,1,512]{2,1,0:T(1,128)S(1)}, u32[]{:S(2)}, u32[]{:S(2)}) async-start(f32[8,1,512]{2,1,0:T(1,128)} %broadcast_in_dim.93), calls=%async_computation.9 | async-start | bytes 32768 | tf_op jit(solution)/shard_map/all_to_all | solution.py:19
Sparse Core Ops, SparseCore 0:
  30.4 39.4 all-gather.3
  72.0 57.2 all-gather.7
  131.4 46.8 all-gather.5

commit v5 on v4

--- a/solution.py
+++ b/solution.py
@@ -68,7 +68,8 @@
     tp_index = lax.axis_index(TP)
     side = lax.axis_index("pair")
     core = lax.axis_index("core")
-    line = lax.axis_size("z") * 2
+    line = lax.axis_size(LINE)
+    tall = lax.axis_size("y")
     sub_rows = row_count // tp_count
     widths = (w_query.shape[1], w_key.shape[1], w_value.shape[1])
     cuts = (widths[0], widths[0] + widths[1])
@@ -88,9 +89,27 @@
     near = lax.ppermute(
         lax.dynamic_slice_in_dim(normed, core * channels, channels, axis=1), "pair", swap
     )
-    held_query = jnp.where(present(normed), w_query, 0.0)
-    along_z = to_sides(held_query[:, :half_query], held_query[:, half_query:])
-    gathered_query = lax.all_gather(along_z, "y", axis=0, tiled=True)
+    heads_wide = half_query
+    peaks = jnp.max(jnp.abs(normed), axis=0).reshape(tall, line, row_count)
+    peaks = peaks.transpose(1, 0, 2).reshape(line, -1, heads_wide)
+    docs = jnp.pad(doc_ids.astype(jnp.bfloat16), (0, heads_wide - tok_dev))
+    docs = jnp.broadcast_to(docs, (line, 1, heads_wide))
+    peak_rows = peaks.shape[1]
+    blank = jnp.zeros((line, 15 - peak_rows, heads_wide), jnp.bfloat16)
+    halves = jnp.stack((w_query[:, :half_query], w_query[:, half_query:]))
+    sent = jnp.broadcast_to(halves, (line // 2, *halves.shape))
+    sent = sent.reshape(line, row_count, heads_wide)
+    along_z = exchange(jnp.concatenate((sent, peaks, docs, blank), axis=1), LINE)
+    gathered_query = lax.all_gather(
+        along_z[:, :row_count].reshape(-1, heads_wide), "y", axis=0, tiled=True
+    )
+    riders = along_z[:, row_count:]
+    peaks = jnp.max(riders[:, :peak_rows], axis=0).reshape(tall, row_count)
+    docs = riders[:, peak_rows, :tok_dev].reshape(line * tok_dev)
+    docs = jnp.broadcast_to(docs, (tall, line * tok_dev))
+    arrived = exchange(jnp.concatenate((peaks, docs), axis=1), "y")
+    input_peak = jnp.max(arrived[:, :row_count], axis=0).astype(jnp.float32)
+    doc_block = arrived[:, row_count:].astype(jnp.int32).reshape(tok_count * tok_dev)
     far = lax.ppermute(near, "core", swap)
     other = jnp.concatenate(
         (jnp.where(core == 0, near, far), jnp.where(core == 0, far, near)), axis=1
@@ -110,13 +129,6 @@
     )
     everything = lax.all_gather(sent_y, "y", axis=0, tiled=True)
     key_block, value_block = jnp.split(everything, (HEAD,), axis=1)
-
-    peaks = jnp.max(jnp.abs(normed), axis=0).reshape(tok_count, row_count)
-    peaks = jnp.where(present(along_z), peaks, 0.0)
-    docs = jnp.broadcast_to(doc_ids.astype(jnp.bfloat16), (tok_count, tok_dev))
-    arrived = exchange(jnp.concatenate((peaks, docs), axis=1), TOK)
-    input_peak = jnp.max(arrived[:, :row_count], axis=0).astype(jnp.float32)
-    doc_block = arrived[:, row_count:].astype(jnp.int32).reshape(tok_count * tok_dev)
 
     block = jnp.concatenate((w_query, w_key, w_value), axis=1)
     row_peak = jnp.max(jnp.abs(block), axis=1)
@@ -190,8 +202,7 @@
         .astype(jnp.bfloat16)
     )
     out_peak = jnp.max(jnp.abs(attended), axis=0).astype(jnp.float32)
-    out_peak = jnp.max(to_everyone(out_peak, LINE), axis=0)
-    out_scale = jnp.max(to_everyone(out_peak, "y"), axis=0)
+    out_scale = jnp.max(to_everyone(out_peak, TOK), axis=0)
     return (
         attended,
         out_scale,

time: 222 us -> 217 us (0.977)
  waiting for transfers between devices: 70.3 us -> 64.3 us
  local copies, waits for them, and re-layouts: 19.1 us -> 23 us
  starting transfers between devices: 55.4 us -> 52.1 us
    all_to_all x9 -> x8, waiting for transfers between devices: 63.4 us -> 52.4 us  [exchange(): return lax.all_to_all(parts, axis, split_axis=0, concat_axis=0, tiled=True)]
    all_gather x1, waiting for transfers between devices: 0.02 us -> 6.5 us  [on_device(): everything = lax.all_gather(sent_y, 'y', axis=0, tiled=True)]
    unnamed x33 -> x49, local copies, waits for them, and re-layouts: 4.9 us -> 11.1 us
    all_to_all x9 -> x8, starting transfers between devices: 47 us -> 43.7 us  [exchange(): return lax.all_to_all(parts, axis, split_axis=0, concat_axis=0, tiled=True)]
  transfers between devices with their start and end apart: 15 -> 14, of which waited for: 10 -> 10; matrix products, arithmetic and copies ran while one was open for 21% -> 23% of each run, Pallas kernels for 0% -> 0%
where the time goes in v5:
time: 217 us; the launch traced here: 216 us
  waiting for transfers between devices  64.3 us (30%)
  starting transfers between devices  52.1 us (24%)
  other arithmetic  25.1 us (12%)
  local copies, waits for them, and re-layouts  23 us (11%)
  blocking collectives  22.1 us (10%)
  between operations  16.3 us (8%)
  matrix products  12.8 us (6%)
    all_to_all x8, waiting for transfers between devices, exchange(): return lax.all_to_all(parts, axis, split_axis=0, concat_axis=0, tiled=True)  52.4 us
    all_to_all x8, starting transfers between devices, exchange(): return lax.all_to_all(parts, axis, split_axis=0, concat_axis=0, tiled=True)  43.7 us
    all_to_all x1, blocking collectives, exchange(): return lax.all_to_all(parts, axis, split_axis=0, concat_axis=0, tiled=True)  22.1 us
    unnamed x49, local copies, waits for them, and re-layouts  11.1 us
    all_gather x1, waiting for transfers between devices, on_device(): everything = lax.all_gather(sent_y, 'y', axis=0, tiled=True)  6.5 us
    select_n x2, other arithmetic, in_pair_order(): jnp.where(even, own, other)  4.6 us
  transfers between devices with their start and end apart: 14, of which 10 were waited for; matrix products, arithmetic and copies ran while one was open for 23% of the time, Pallas kernels for 0%

profile of v5, /device:TPU:2, one launch (start us, length us, event | category | flops | bytes accessed | tf_op | source)
XLA Modules:
  0.0 215.6 jit_solution(204950408951269916)
XLA Ops:
  7.3 0.9 pad_maximum_fusion.3
  8.2 22.1 %all_to_all.63 = bf16[8,128,128]{2,1,0:T(8,128)(2,1)} all-to-all(bf16[8,128,128]{2,1,0:T(8,128)(2,1)S(1)} %bitcast.122), channel_id=1, replica_groups=mesh['y'=8,'z'=4,'pair'=2,'x'=4,'core'=2] {'z','pair'}, dimensions={0} | all-to-all | bytes 524288 | tf_op jit(solution)/shard_map/all_to_all | solution.py:19
  30.3 1.8 fusion.8
  32.2 1.3 abs_reduce_fusion
  33.8 1.0 maximum_maximum_fusion
  34.7 3.5 %all-to-all-start = ((bf16[8,144,256]{2,1,0:T(8,128)(2,1)}), bf16[8,144,256]{2,1,0:T(8,128)(2,1)S(1)}, u32[]{:S(2)}, u32[]{:S(2)}) async-start(bf16[8,144,256]{2,1,0:T(8,128)(2,1)} %maximum_maximum_fusion), calls=%async_computation | async-start | bytes 1179648 | tf_op jit(solution)/shard_map/all_to_all | solution.py:19
  38.4 3.8 %collective-permute-start = (bf16[96,4096]{1,0:T(8,128)(2,1)S(1)}, bf16[96,4096]{1,0:T(8,128)(2,1)}, u32[]{:S(2)}, u32[]{:S(2)}) collective-permute-start(bf16[96,4096]{1,0:T(8,128)(2,1)S(1)} %constant_dynamic-slice_fusion), channel_id=1, source_target_pairs={{0,8},{8,0},{1,9},{9,1},{2,10},{10,2},{3,11},{11,3},{4,12},{12,4},... | collective-permute-start | bytes 2359304 | tf_op jit(solution)/shard_map/ppermute | solution.py:89
  43.1 13.9 %all-to-all-done = bf16[8,144,256]{2,1,0:T(8,128)(2,1)S(1)} async-done(((bf16[8,144,256]{2,1,0:T(8,128)(2,1)}), bf16[8,144,256]{2,1,0:T(8,128)(2,1)S(1)}, u32[]{:S(2)}, u32[]{:S(2)}) %all-to-all-start) | async-done | bytes 589856 | tf_op jit(solution)/shard_map/all_to_all | solution.py:19
  57.1 0.8 slice.99
  57.9 0.8 maximum_bitcast_fusion
  60.0 0.9 reshape.296
  60.8 4.8 %all-to-all-start.4 = ((bf16[8,2,6208]{2,1,0:T(2,128)(2,1)}), bf16[8,2,6208]{2,1,0:T(2,128)(2,1)}, u32[]{:S(2)}, u32[]{:S(2)}) async-start(bf16[8,2,6208]{2,1,0:T(2,128)(2,1)} %reshape.296), calls=%async_computation.4 | async-start | bytes 401408 | tf_op jit(solution)/shard_map/all_to_all | solution.py:19
  65.7 3.1 %collective-permute-done = bf16[96,4096]{1,0:T(8,128)(2,1)} collective-permute-done((bf16[96,4096]{1,0:T(8,128)(2,1)S(1)}, bf16[96,4096]{1,0:T(8,128)(2,1)}, u32[]{:S(2)}, u32[]{:S(2)}) %collective-permute-start) | collective-permute-done | bytes 786464 | tf_op jit(solution)/shard_map/ppermute | solution.py:89
  68.8 1.9 collective-permute-start.1
  74.5 1.5 broadcast_select_fusion.5
  76.0 2.3 %broadcast_select_fusion.3 = (bf16[96,8192]{1,0:T(8,128)(2,1)}, bf16[96,8192]{1,0:T(8,128)(2,1)}) fusion(bf16[96,8192]{1,0:T(8,128)(2,1)S(1)} %get-tuple-element.15, pred[]{:T(512)S(6)} %and.15, bf16[96,4096]{1,0:T(8,128)(2,1)S(1)} %get-tuple-element.21, bf16[96,4096]{1,0:T(8,128)(2,1)S(1)} %get-tuple-element.20), kind=kLoop, calls=%fused_computation.31 | loop fusion | flops 4718592 | bytes 6291457 | tf_op jit(solution)/shard_map/jit(_where)/select_n | solution.py:39
  78.3 3.5 %fusion.11 = f32[192,128]{1,0:T(8,128)S(1)} fusion(bf16[8192,128]{1,0:T(8,128)(2,1)} %all-gather.4.cloned.1.call-done, bf16[96,8192]{1,0:T(8,128)(2,1)} %get-tuple-element.19, bf16[96,8192]{1,0:T(8,128)(2,1)} %get-tuple-element.18), kind=kOutput, calls=%fused_computation.14 | convolution fusion | flops 408944640 | bytes 5341184 | tf_op jit(solution)/shard_map/dot_general | solution.py:122
  82.3 7.1 %all-to-all-start.1 = ((bf16[8,2,448]{2,1,0:T(2,128)(2,1)}), bf16[8,2,448]{2,1,0:T(2,128)(2,1)S(1)}, u32[]{:S(2)}, u32[]{:S(2)}) async-start(bf16[8,2,448]{2,1,0:T(2,128)(2,1)} %reshape.294), calls=%async_computation.1 | async-start | bytes 32768 | tf_op jit(solution)/shard_map/all_to_all | solution.py:19
  90.1 7.4 %all-to-all-done.1 = bf16[8,2,448]{2,1,0:T(2,128)(2,1)S(1)} async-done(((bf16[8,2,448]{2,1,0:T(2,128)(2,1)}), bf16[8,2,448]{2,1,0:T(2,128)(2,1)S(1)}, u32[]{:S(2)}, u32[]{:S(2)}) %all-to-all-start.1) | async-done | bytes 14368 | tf_op jit(solution)/shard_map/all_to_all | solution.py:19
  97.5 1.6 broadcast_in_dim.79
  99.1 5.8 %all-to-all-start.3 = ((bf16[8,192,128]{2,1,0:T(8,128)(2,1)}), bf16[8,192,128]{2,1,0:T(8,128)(2,1)}, u32[]{:S(2)}, u32[]{:S(2)}) async-start(bf16[8,192,128]{2,1,0:T(8,128)(2,1)} %broadcast_in_dim.79), calls=%async_computation.3 | async-start | bytes 786432 | tf_op jit(solution)/shard_map/all_to_all | solution.py:19
  104.9 1.8 multiply_cosine_fusion
  106.7 2.3 %reshape.297 = bf16[8,1,12416]{2,1,0:T(2,128)(2,1)} reshape(bf16[8,2,6208]{2,1,0:T(2,128)(2,1)} %all-to-all-done.4) | data formatting | bytes 397312
  109.1 1.1 copy.73
  110.8 1.4 reshape.295
  113.7 5.2 %all-to-all-done.3 = bf16[8,192,128]{2,1,0:T(8,128)(2,1)} async-done(((bf16[8,192,128]{2,1,0:T(8,128)(2,1)}), bf16[8,192,128]{2,1,0:T(8,128)(2,1)}, u32[]{:S(2)}, u32[]{:S(2)}) %all-to-all-start.3) | async-done | bytes 393248 | tf_op jit(solution)/shard_map/all_to_all | solution.py:19
  118.9 1.2 slice.95
  120.8 1.1 fusion.44
  121.8 0.8 pad_maximum_fusion.1
  123.3 3.3 %all-to-all-start.5 = ((f32[8,1,768]{2,1,0:T(1,128)}), f32[8,1,768]{2,1,0:T(1,128)S(1)}, u32[]{:S(2)}, u32[]{:S(2)}) async-start(f32[8,1,768]{2,1,0:T(1,128)} %broadcast_in_dim.82), calls=%async_computation.5 | async-start | bytes 49152 | tf_op jit(solution)/shard_map/all_to_all | solution.py:19
  127.4 7.1 %all-to-all-done.5 = f32[8,1,768]{2,1,0:T(1,128)S(1)} async-done(((f32[8,1,768]{2,1,0:T(1,128)}), f32[8,1,768]{2,1,0:T(1,128)S(1)}, u32[]{:S(2)}, u32[]{:S(2)}) %all-to-all-start.5) | async-done | bytes 24608 | tf_op jit(solution)/shard_map/all_to_all | solution.py:19
  135.2 3.3 %all-to-all-start.6 = ((f32[8,1,768]{2,1,0:T(1,128)}), f32[8,1,768]{2,1,0:T(1,128)S(1)}, u32[]{:S(2)}, u32[]{:S(2)}) async-start(f32[8,1,768]{2,1,0:T(1,128)} %broadcast_in_dim.83), calls=%async_computation.6 | async-start | bytes 49152 | tf_op jit(solution)/shard_map/all_to_all | solution.py:19
  138.5 1.4 fusion.19
  139.9 6.5 %all-to-all-done.6 = f32[8,1,768]{2,1,0:T(1,128)S(1)} async-done(((f32[8,1,768]{2,1,0:T(1,128)}), f32[8,1,768]{2,1,0:T(1,128)S(1)}, u32[]{:S(2)}, u32[]{:S(2)}) %all-to-all-start.6) | async-done | bytes 24608 | tf_op jit(solution)/shard_map/all_to_all | solution.py:19
  147.0 4.8 %all-to-all-start.7 = ((f32[8,1,768]{2,1,0:T(1,128)}), f32[8,1,768]{2,1,0:T(1,128)S(1)}, u32[]{:S(2)}, u32[]{:S(2)}) async-start(f32[8,1,768]{2,1,0:T(1,128)} %broadcast_in_dim.84), calls=%async_computation.7 | async-start | bytes 49152 | tf_op jit(solution)/shard_map/all_to_all | solution.py:19
  151.9 1.3 dynamic-slice_divide_fusion
  153.1 2.7 %all-to-all-done.7 = f32[8,1,768]{2,1,0:T(1,128)S(1)} async-done(((f32[8,1,768]{2,1,0:T(1,128)}), f32[8,1,768]{2,1,0:T(1,128)S(1)}, u32[]{:S(2)}, u32[]{:S(2)}) %all-to-all-start.7) | async-done | bytes 24608 | tf_op jit(solution)/shard_map/all_to_all | solution.py:19
  157.0 2.3 %broadcast_select_fusion.1 = (bf16[96,8192]{1,0:T(8,128)(2,1)}, bf16[96,8192]{1,0:T(8,128)(2,1)}) fusion(bf16[96,8192]{1,0:T(8,128)(2,1)S(1)} %get-tuple-element.15, pred[]{:T(512)S(6)} %and.16, bf16[96,4096]{1,0:T(8,128)(2,1)S(1)} %get-tuple-element.21, bf16[96,4096]{1,0:T(8,128)(2,1)S(1)} %get-tuple-element.20), kind=kLoop, calls=%fused_computation.29 | loop fusion | flops 4718592 | bytes 6291457 | tf_op jit(solution)/shard_map/jit(_where)/select_n | solution.py:39
  159.3 4.3 %fusion.15 = f32[192,256]{1,0:T(8,128)S(1)} fusion(bf16[8192,256]{1,0:T(8,128)(2,1)} %all-gather.8.cloned.1.call-done, bf16[96,8192]{1,0:T(8,128)(2,1)} %get-tuple-element.17, bf16[96,8192]{1,0:T(8,128)(2,1)} %get-tuple-element.16), kind=kOutput, calls=%fused_computation.18 | convolution fusion | flops 811597824 | bytes 7536640 | tf_op jit(solution)/shard_map/dot_general | solution.py:170
  164.4 2.6 %collective-permute-start.2 = (bf16[96,256]{1,0:T(8,128)(2,1)S(1)}, bf16[96,256]{1,0:T(8,128)(2,1)S(1)}, u32[]{:S(2)}, u32[]{:S(2)}) collective-permute-start(bf16[96,256]{1,0:T(8,128)(2,1)S(1)} %bitcast.151), channel_id=1, source_target_pairs={{0,8},{8,0},{1,9},{9,1},{2,10},{10,2},{3,11},{11,3},{4,12},{12,4},... | collective-permute-start | bytes 147464 | tf_op jit(solution)/shard_map/ppermute | solution.py:174
  168.2 2.3 %collective-permute-done.2 = bf16[96,256]{1,0:T(8,128)(2,1)S(1)} collective-permute-done((bf16[96,256]{1,0:T(8,128)(2,1)S(1)}, bf16[96,256]{1,0:T(8,128)(2,1)S(1)}, u32[]{:S(2)}, u32[]{:S(2)}) %collective-permute-start.2) | collective-permute-done | bytes 49184 | tf_op jit(solution)/shard_map/ppermute | solution.py:174
  170.4 6.5 %all-gather.6.cloned.1.call-done = bf16[6144,256]{1,0:T(8,128)(2,1)} async-done(((bf16[768,256]{1,0:T(8,128)(2,1)}), bf16[6144,256]{1,0:T(8,128)(2,1)}) %all-gather.6.cloned.1.call-update) | async-done | bytes 3145744 | tf_op jit(solution)/shard_map/all_gather | solution.py:130
  176.9 3.3 %fusion.46 = (f32[4,96]{1,0:T(4,128)S(1)}, f32[1,4,96,6144]{3,2,1,0:T(8,128)S(1)}) fusion(bf16[6144,256]{1,0:T(8,128)(2,1)} %all-gather.6.cloned.1.call-done, pred[96,6144]{1,0:T(8,128)(4,1)S(1)} %copy-done.1, bf16[96,256]{1,0:T(8,128)(2,1)S(1)} %get-tuple-element.33, bf16[96,256]{1,0:T(8,128)(2,1)S(1)} %get-tuple-element.32), kind=kOutput, calls=%fused_computation.106 | convolution fusion | flops 611253888 | bytes 11699712 | tf_op jit(solution)/shard_map/tkgd,skd->kgts/dot_general | solution.py:180
  180.3 2.2 %fusion = f32[4,96]{1,0:T(4,128)S(1)} fusion(f32[1,4,96,6144]{3,2,1,0:T(8,128)S(1)} %get-tuple-element.39, f32[4,96]{1,0:T(4,128)S(1)} %get-tuple-element.38, pred[96,6144]{1,0:T(8,128)(4,1)S(1)} %copy-done.1), kind=kLoop, calls=%fused_computation.2 | loop fusion | flops 7077504 | bytes 10030080 | tf_op jit(solution)/shard_map/reduce_sum | solution.py:191
  182.5 1.7 abs_reduce_fusion.3
  184.9 10.9 %all-to-all-start.8 = ((f32[64,1,512]{2,1,0:T(1,128)}), f32[64,1,512]{2,1,0:T(1,128)S(1)}, u32[]{:S(2)}, u32[]{:S(2)}) async-start(f32[64,1,512]{2,1,0:T(1,128)} %broadcast_in_dim.87), calls=%async_computation.8 | async-start | bytes 262144 | tf_op jit(solution)/shard_map/all_to_all | solution.py:19
  196.0 0.9 copy.55
  198.8 9.6 %all-to-all-done.8 = f32[64,1,512]{2,1,0:T(1,128)S(1)} async-done(((f32[64,1,512]{2,1,0:T(1,128)}), f32[64,1,512]{2,1,0:T(1,128)S(1)}, u32[]{:S(2)}, u32[]{:S(2)}) %all-to-all-start.8) | async-done | bytes 131104 | tf_op jit(solution)/shard_map/all_to_all | solution.py:19
  (114 shorter events, 17.7 us)
Async XLA Ops:
  7.2 25.0 %copy-start = (bf16[96,8192]{1,0:T(8,128)(2,1)S(1)}, bf16[96,8192]{1,0:T(8,128)(2,1)}, u32[]{:S(2)}) copy-start(bf16[96,8192]{1,0:T(8,128)(2,1)} %param.6) | copy-start | bytes 4718596
  7.2 26.4 %copy-start.13 = (s32[96]{0:T(128)S(1)}, s32[96]{0:T(128)}, u32[]{:S(2)}) copy-start(s32[96]{0:T(128)} %param.11) | copy-start | bytes 1156
  7.2 26.5 %copy-start.3 = (bf16[128,512]{1,0:T(8,128)(2,1)S(1)}, bf16[128,512]{1,0:T(8,128)(2,1)}, u32[]{:S(2)}) copy-start(bf16[128,512]{1,0:T(8,128)(2,1)} %param.8) | copy-start | bytes 393220
  7.2 71.0 %all-gather.4.cloned.1.call-start = ((), (), s32[]{:S(2)}) async-start(), calls=%async_computation.9 | async-start | bytes 2359296 | tf_op jit(solution)/shard_map/all_gather | solution.py:81
  33.5 8.7 %copy-start.4 = (bf16[128,512]{1,0:T(8,128)(2,1)S(1)}, bf16[128,512]{1,0:T(8,128)(2,1)}, u32[]{:S(2)}) copy-start(bf16[128,512]{1,0:T(8,128)(2,1)} %param.8) | copy-start | bytes 393220
  33.5 8.7 %copy-start.7 = (bf16[128,128]{1,0:T(8,128)(2,1)S(1)}, bf16[128,128]{1,0:T(8,128)(2,1)}, u32[]{:S(2)}) copy-start(bf16[128,128]{1,0:T(8,128)(2,1)} %param.9) | copy-start | bytes 98308
  33.5 8.8 %copy-start.8 = (bf16[128,128]{1,0:T(8,128)(2,1)S(1)}, bf16[128,128]{1,0:T(8,128)(2,1)}, u32[]{:S(2)}) copy-start(bf16[128,128]{1,0:T(8,128)(2,1)} %param.10) | copy-start | bytes 98308
  34.7 22.3 %all-to-all-start = ((bf16[8,144,256]{2,1,0:T(8,128)(2,1)}), bf16[8,144,256]{2,1,0:T(8,128)(2,1)S(1)}, u32[]{:S(2)}, u32[]{:S(2)}) async-start(bf16[8,144,256]{2,1,0:T(8,128)(2,1)} %maximum_maximum_fusion), calls=%async_computation | async-start | bytes 1179648 | tf_op jit(solution)/shard_map/all_to_all | solution.py:19
  38.3 121.0 %all-gather.8.cloned.1.call-start = ((), (), s32[]{:S(2)}) async-start(), calls=%async_computation.11 | async-start | bytes 4718592 | tf_op jit(solution)/shard_map/all_gather | solution.py:103
  38.4 30.3 %collective-permute-start = (bf16[96,4096]{1,0:T(8,128)(2,1)S(1)}, bf16[96,4096]{1,0:T(8,128)(2,1)}, u32[]{:S(2)}, u32[]{:S(2)}) collective-permute-start(bf16[96,4096]{1,0:T(8,128)(2,1)S(1)} %constant_dynamic-slice_fusion), channel_id=1, source_target_pairs={{0,8},{8,0},{1,9},{9,1},{2,10},{10,2},{3,11},{11,3},{4,12},{12,4},... | collective-permute-start | bytes 2359304 | tf_op jit(solution)/shard_map/ppermute | solution.py:89
  60.8 21.4 %all-to-all-start.4 = ((bf16[8,2,6208]{2,1,0:T(2,128)(2,1)}), bf16[8,2,6208]{2,1,0:T(2,128)(2,1)}, u32[]{:S(2)}, u32[]{:S(2)}) async-start(bf16[8,2,6208]{2,1,0:T(2,128)(2,1)} %reshape.296), calls=%async_computation.4 | async-start | bytes 401408 | tf_op jit(solution)/shard_map/all_to_all | solution.py:19
  68.8 5.7 %collective-permute-start.1 = (bf16[96,4096]{1,0:T(8,128)(2,1)}, bf16[96,4096]{1,0:T(8,128)(2,1)}, u32[]{:S(2)}, u32[]{:S(2)}) collective-permute-start(bf16[96,4096]{1,0:T(8,128)(2,1)} %collective-permute-done), channel_id=1, source_target_pairs={{0,1},{1,0},{2,3},{3,2},{4,5},{5,4},{6,7},{7,6},{8,9},{9,8},{10,11... | collective-permute-start | bytes 2359304 | tf_op jit(solution)/shard_map/ppermute | solution.py:113
  70.7 11.1 %copy-start.12 = (f32[64]{0:T(128)}, f32[64]{0:T(128)S(1)}, u32[]{:S(2)}) copy-start(f32[64]{0:T(128)S(1)} %multiply_exponential_fusion) | copy-start | bytes 772
  71.2 10.6 %copy-start.11 = (f32[192]{0:T(256)}, f32[192]{0:T(256)S(1)}, u32[]{:S(2)}) copy-start(f32[192]{0:T(256)S(1)} %add_convert_fusion.1) | copy-start | bytes 2308
  82.3 15.3 %all-to-all-start.1 = ((bf16[8,2,448]{2,1,0:T(2,128)(2,1)}), bf16[8,2,448]{2,1,0:T(2,128)(2,1)S(1)}, u32[]{:S(2)}, u32[]{:S(2)}) async-start(bf16[8,2,448]{2,1,0:T(2,128)(2,1)} %reshape.294), calls=%async_computation.1 | async-start | bytes 32768 | tf_op jit(solution)/shard_map/all_to_all | solution.py:19
  97.5 9.2 %copy-start.9 = (bf16[8,2,448]{2,1,0:T(2,128)(2,1)}, bf16[8,2,448]{2,1,0:T(2,128)(2,1)S(1)}, u32[]{:S(2)}) copy-start(bf16[8,2,448]{2,1,0:T(2,128)(2,1)S(1)} %all-to-all-done.1) | copy-start | bytes 43012
  99.1 19.8 %all-to-all-start.3 = ((bf16[8,192,128]{2,1,0:T(8,128)(2,1)}), bf16[8,192,128]{2,1,0:T(8,128)(2,1)}, u32[]{:S(2)}, u32[]{:S(2)}) async-start(bf16[8,192,128]{2,1,0:T(8,128)(2,1)} %broadcast_in_dim.79), calls=%async_computation.3 | async-start | bytes 786432 | tf_op jit(solution)/shard_map/all_to_all | solution.py:19
  104.9 72.0 %all-gather.6.cloned.1.call-start = ((), (), s32[]{:S(2)}) async-start(), calls=%async_computation.10 | async-start | bytes 3538944 | tf_op jit(solution)/shard_map/all_gather | solution.py:130
  109.1 29.4 %copy-start.14 = (s32[96]{0:T(128)S(1)}, s32[96]{0:T(128)}, u32[]{:S(2)}) copy-start(s32[96]{0:T(128)} %param.11) | copy-start | bytes 1156
  109.1 29.4 %copy-start.15 = (s32[96]{0:T(128)S(1)}, s32[96]{0:T(128)}, u32[]{:S(2)}) copy-start(s32[96]{0:T(128)} %iota_add_fusion) | copy-start | bytes 1156
  113.0 0.6 copy-start.10
  123.3 11.2 %all-to-all-start.5 = ((f32[8,1,768]{2,1,0:T(1,128)}), f32[8,1,768]{2,1,0:T(1,128)S(1)}, u32[]{:S(2)}, u32[]{:S(2)}) async-start(f32[8,1,768]{2,1,0:T(1,128)} %broadcast_in_dim.82), calls=%async_computation.5 | async-start | bytes 49152 | tf_op jit(solution)/shard_map/all_to_all | solution.py:19
  135.2 11.2 %all-to-all-start.6 = ((f32[8,1,768]{2,1,0:T(1,128)}), f32[8,1,768]{2,1,0:T(1,128)S(1)}, u32[]{:S(2)}, u32[]{:S(2)}) async-start(f32[8,1,768]{2,1,0:T(1,128)} %broadcast_in_dim.83), calls=%async_computation.6 | async-start | bytes 49152 | tf_op jit(solution)/shard_map/all_to_all | solution.py:19
  147.0 8.8 %all-to-all-start.7 = ((f32[8,1,768]{2,1,0:T(1,128)}), f32[8,1,768]{2,1,0:T(1,128)S(1)}, u32[]{:S(2)}, u32[]{:S(2)}) async-start(f32[8,1,768]{2,1,0:T(1,128)} %broadcast_in_dim.84), calls=%async_computation.7 | async-start | bytes 49152 | tf_op jit(solution)/shard_map/all_to_all | solution.py:19
  159.3 4.4 %copy-start.5 = (f32[192,64]{1,0:T(8,128)S(1)}, f32[192,64]{1,0:T(8,128)}, u32[]{:S(2)}) copy-start(f32[192,64]{1,0:T(8,128)} %get-tuple-element.36) | copy-start | bytes 147460
  159.3 4.4 %copy-start.6 = (f32[192,64]{1,0:T(8,128)S(1)}, f32[192,64]{1,0:T(8,128)}, u32[]{:S(2)}) copy-start(f32[192,64]{1,0:T(8,128)} %get-tuple-element.37) | copy-start | bytes 147460
  159.3 17.7 %copy-start.1 = (pred[96,6144]{1,0:T(8,128)(4,1)S(1)}, pred[96,6144]{1,0:T(8,128)(4,1)}, u32[]{:S(2)}) copy-start(pred[96,6144]{1,0:T(8,128)(4,1)} %fusion.19) | copy-start | bytes 1769476
  164.4 6.0 %collective-permute-start.2 = (bf16[96,256]{1,0:T(8,128)(2,1)S(1)}, bf16[96,256]{1,0:T(8,128)(2,1)S(1)}, u32[]{:S(2)}, u32[]{:S(2)}) collective-permute-start(bf16[96,256]{1,0:T(8,128)(2,1)S(1)} %bitcast.151), channel_id=1, source_target_pairs={{0,8},{8,0},{1,9},{9,1},{2,10},{10,2},{3,11},{11,3},{4,12},{12,4},... | collective-permute-start | bytes 147464 | tf_op jit(solution)/shard_map/ppermute | solution.py:174
  180.3 2.2 %copy-start.16 = (bf16[6144,256]{1,0:T(8,128)(2,1)S(1)}, bf16[6144,256]{1,0:T(8,128)(2,1)}, u32[]{:S(2)}) copy-start(bf16[6144,256]{1,0:T(8,128)(2,1)} %all-gather.6.cloned.1.call-done) | copy-start | bytes 9437188
  182.5 13.3 %copy-start.2 = (bf16[8,12288]{1,0:T(8,128)(2,1)S(1)}, bf16[8,12288]{1,0:T(8,128)(2,1)}, u32[]{:S(2)}) copy-start(bf16[8,12288]{1,0:T(8,128)(2,1)} %slice.104) | copy-start | bytes 589828
  184.9 23.5 %all-to-all-start.8 = ((f32[64,1,512]{2,1,0:T(1,128)}), f32[64,1,512]{2,1,0:T(1,128)S(1)}, u32[]{:S(2)}, u32[]{:S(2)}) async-start(f32[64,1,512]{2,1,0:T(1,128)} %broadcast_in_dim.87), calls=%async_computation.8 | async-start | bytes 262144 | tf_op jit(solution)/shard_map/all_to_all | solution.py:19
Sparse Core Ops, SparseCore 0:
  30.4 39.6 all-gather.3
  72.2 56.0 all-gather.7
  130.4 46.5 all-gather.5

commit v6 on v5

--- a/solution.py
+++ b/solution.py
@@ -3,6 +3,8 @@
 import jax
 import jax.numpy as jnp
 from jax import lax
+from jax.experimental import pallas as pl
+from jax.experimental.pallas import tpu as pltpu
 from jax.sharding import Mesh
 from jax.sharding import PartitionSpec as P
 
@@ -53,6 +55,77 @@
     return jnp.concatenate(
         [first * cosine - second * sine, second * cosine + first * sine], axis=-1
     )
+
+
+def attend(span, bounds, query, keyed, tok_dev):
+    total, head = query.shape
+    length = keyed.shape[0]
+    block = 512
+    group = total // tok_dev
+    factor = 1.0 / math.sqrt(head)
+
+    def kernel(span_ref, bounds_ref, query_ref, keyed_ref, out_ref, peak_ref, score_ref):
+        first, last = span_ref[0], span_ref[1]
+        start_most, token_least = span_ref[2], span_ref[3]
+        queries = query_ref[...]
+
+        def scored(index, highest):
+            base = index * block
+            keys = keyed_ref[pl.ds(base, block), :head]
+            score_ref[index] = lax.dot_general(
+                queries, keys, (((1,), (1,)), ((), ())), preferred_element_type=jnp.float32
+            )
+
+            @pl.when((base < start_most) | (base + block - 1 > token_least))
+            def _():
+                place = base + lax.broadcasted_iota(jnp.int32, (total, block), 1)
+                inside = (place >= bounds_ref[:, :1]) & (place <= bounds_ref[:, 1:])
+                score_ref[index] = jnp.where(inside, score_ref[index], -1e30)
+
+            scores = score_ref[index]
+            for k in range(0, block, 128):
+                highest = jnp.maximum(highest, scores[:, k : k + 128])
+            return highest
+
+        highest = lax.fori_loop(
+            first, last, scored, jnp.full((total, 128), -1e30, jnp.float32)
+        )
+        highest = jnp.max(highest, axis=1, keepdims=True)
+
+        def weighted(index, carried):
+            sums, gathered = carried
+            weights = jnp.exp((score_ref[index] - highest) * factor)
+            for k in range(0, block, 128):
+                sums = sums + weights[:, k : k + 128]
+            values = keyed_ref[pl.ds(index * block, block), head:]
+            gathered = gathered + jnp.dot(
+                weights.astype(jnp.bfloat16), values, preferred_element_type=jnp.float32
+            )
+            return sums, gathered
+
+        zeros = jnp.zeros((total, 128), jnp.float32)
+        sums, gathered = lax.fori_loop(first, last, weighted, (zeros, zeros))
+        attended = (gathered / jnp.sum(sums, axis=1, keepdims=True)).astype(jnp.bfloat16)
+        for g in range(group):
+            part = attended[g * tok_dev : (g + 1) * tok_dev]
+            out_ref[:, g * head : (g + 1) * head] = part
+            peak_ref[:, g * head : (g + 1) * head] = jnp.max(
+                jnp.abs(part.astype(jnp.float32)), axis=0, keepdims=True
+            )
+
+    in_vmem = pl.BlockSpec(memory_space=pltpu.VMEM)
+    return pl.pallas_call(
+        kernel,
+        out_shape=(
+            jax.ShapeDtypeStruct((tok_dev, group * head), jnp.bfloat16),
+            jax.ShapeDtypeStruct((1, group * head), jnp.float32),
+        ),
+        in_specs=[pl.BlockSpec(memory_space=pltpu.SMEM), in_vmem, in_vmem, in_vmem],
+        out_specs=(in_vmem, in_vmem),
+        scratch_shapes=[pltpu.VMEM((length // block, total, block), jnp.float32)],
+        name="attend",
+        compiler_params=pltpu.CompilerParams(vmem_limit_bytes=32 * 1024 * 1024),
+    )(span, bounds, query, keyed)
 
 
 def smooth_from(input_peak, weight_peak):
@@ -128,7 +201,6 @@
         (spread[:, 0].reshape(-1, HEAD), spread[:, 1].reshape(-1, HEAD)), axis=1
     )
     everything = lax.all_gather(sent_y, "y", axis=0, tiled=True)
-    key_block, value_block = jnp.split(everything, (HEAD,), axis=1)
 
     block = jnp.concatenate((w_query, w_key, w_value), axis=1)
     row_peak = jnp.max(jnp.abs(block), axis=1)
@@ -174,35 +246,15 @@
     swapped = lax.ppermute(jnp.where(side == 0, turned[1], turned[0]), "pair", swap)
     query = jnp.concatenate(
         (jnp.where(side == 0, mine, swapped), jnp.where(side == 0, swapped, mine)), axis=1
-    ).reshape(tok_dev, 1, group_size, HEAD)
-
-    length = key_block.shape[0]
-    scores = jnp.einsum(
-        "tkgd,skd->kgts", query, key_block[:, None, :], preferred_element_type=jnp.float32
-    ) * (1.0 / math.sqrt(HEAD))
-    query_positions = tok_index * tok_dev + jnp.arange(tok_dev, dtype=jnp.int32)
-    key_positions = jnp.arange(length, dtype=jnp.int32)
-    allowed = (doc_ids[:, None] == doc_block[None, :]) & (
-        key_positions[None, :] <= query_positions[:, None]
-    )
-    scores = jnp.where(allowed, scores, -1e30)
-    highest = jnp.max(scores, axis=3, keepdims=True)
-    weights = jnp.where(allowed, jnp.exp(scores - highest), 0.0)
-    totals = jnp.sum(weights, axis=3)
-    accumulated = jnp.einsum(
-        "kgts,skd->kgtd",
-        weights.astype(jnp.bfloat16),
-        value_block[:, None, :],
-        preferred_element_type=jnp.float32,
-    )
-    attended = (
-        (accumulated / totals[..., None])
-        .transpose(2, 0, 1, 3)
-        .reshape(tok_dev, group_size * HEAD)
-        .astype(jnp.bfloat16)
-    )
-    out_peak = jnp.max(jnp.abs(attended), axis=0).astype(jnp.float32)
-    out_scale = jnp.max(to_everyone(out_peak, TOK), axis=0)
+    ).reshape(tok_dev, group_size, HEAD)
+    query = query.transpose(1, 0, 2).reshape(group_size * tok_dev, HEAD)
+
+    places = tok_index * tok_dev + jnp.arange(tok_dev, dtype=jnp.int32)
+    starts = jnp.sum((doc_block[None, :] < doc_ids[:, None]).astype(jnp.int32), axis=1)
+    span = jnp.stack((starts[0] // 512, places[-1] // 512 + 1, starts[-1], places[0]))
+    bounds = jnp.tile(jnp.stack((starts, places), axis=1), (group_size, 1))
+    attended, out_peak = attend(span, bounds, query, everything, tok_dev)
+    out_scale = jnp.max(to_everyone(out_peak[0], TOK), axis=0)
     return (
         attended,
         out_scale,

time: 217 us -> 219 us (level)
  waiting for transfers between devices: 64.3 us -> 56.1 us
  between operations: 16.3 us -> 21.5 us
  matrix products: 12.8 us -> 7.78 us
  local copies, waits for them, and re-layouts: 23 us -> 27.1 us
  starting transfers between devices: 52.1 us -> 55.4 us
  Pallas kernels: 0 us -> 2.36 us
    all_to_all x8, waiting for transfers between devices: 52.4 us -> 33.7 us  [exchange(): return lax.all_to_all(parts, axis, split_axis=0, concat_axis=0, tiled=True)]
    ppermute x1, waiting for transfers between devices: 3.08 us -> 19.8 us  [on_device(): lax.ppermute(lax.dynamic_slice_in_dim(normed, core * channels, channels,...]
    all_gather x1, waiting for transfers between devices: 6.5 us -> 0.02 us  [on_device(): everything = lax.all_gather(sent_y, 'y', axis=0, tiled=True)]
    dot_general x2 -> x0, matrix products: 5.02 us -> none  [the longest x1 3.32 us: on_device(): jnp.einsum('tkgd,skd->kgts', query, key_block[:, None, :], preferred_elem...]
    all_to_all x8, starting transfers between devices: 43.7 us -> 48.5 us  [exchange(): return lax.all_to_all(parts, axis, split_axis=0, concat_axis=0, tiled=True)]
    all_to_all x4, other arithmetic: 2.22 us -> 4.97 us  [exchange(): return lax.all_to_all(parts, axis, split_axis=0, concat_axis=0, tiled=True)]
    pallas_call x0 -> x1, Pallas kernels: none -> 2.36 us  [attend(): pl.pallas_call(kernel, out_shape=(jax.ShapeDtypeStruct((tok_dev, group *...]
    unnamed x49 -> x38, local copies, waits for them, and re-layouts: 11.1 us -> 12.6 us
  transfers between devices with their start and end apart: 14 -> 14, of which waited for: 10 -> 9; matrix products, arithmetic and copies ran while one was open for 23% -> 25% of each run, Pallas kernels for 0% -> 0%
where the time goes in v6:
time: 219 us; the launch traced here: 218 us
  waiting for transfers between devices  56.1 us (26%)
  starting transfers between devices  55.4 us (25%)
  local copies, waits for them, and re-layouts  27.1 us (12%)
  other arithmetic  25.4 us (12%)
  blocking collectives  22.1 us (10%)
  between operations  21.5 us (10%)
  matrix products  7.78 us (4%)
  Pallas kernels  2.36 us (1%)
    all_to_all x8, starting transfers between devices, exchange(): return lax.all_to_all(parts, axis, split_axis=0, concat_axis=0, tiled=True)  48.5 us
    all_to_all x8, waiting for transfers between devices, exchange(): return lax.all_to_all(parts, axis, split_axis=0, concat_axis=0, tiled=True)  33.7 us
    all_to_all x1, blocking collectives, exchange(): return lax.all_to_all(parts, axis, split_axis=0, concat_axis=0, tiled=True)  22.1 us
    ppermute x1, waiting for transfers between devices, on_device(): lax.ppermute(lax.dynamic_slice_in_dim(normed, core * channels, channels,...  19.8 us
    unnamed x38, local copies, waits for them, and re-layouts  12.6 us
    all_to_all x4, other arithmetic, exchange(): return lax.all_to_all(parts, axis, split_axis=0, concat_axis=0, tiled=True)  4.97 us
    select_n x2, other arithmetic, in_pair_order(): jnp.where(even, own, other)  4.59 us
  transfers between devices with their start and end apart: 14, of which 9 were waited for; matrix products, arithmetic and copies ran while one was open for 25% of the time, Pallas kernels for 0%

profile of v6, /device:TPU:2, one launch (start us, length us, event | category | flops | bytes accessed | tf_op | source)
XLA Modules:
  0.0 217.7 jit_solution(4678217665261601180)
XLA Ops:
  7.2 0.9 pad_maximum_fusion.4
  8.2 22.1 %all_to_all.63 = bf16[8,128,128]{2,1,0:T(8,128)(2,1)} all-to-all(bf16[8,128,128]{2,1,0:T(8,128)(2,1)S(1)} %bitcast.86), channel_id=1, replica_groups=mesh['y'=8,'z'=4,'pair'=2,'x'=4,'core'=2] {'z','pair'}, dimensions={0} | all-to-all | bytes 524288 | tf_op jit(solution)/shard_map/all_to_all | solution.py:21
  30.3 1.8 fusion
  32.8 2.5 %collective-permute-start = (bf16[96,4096]{1,0:T(8,128)(2,1)S(1)}, bf16[96,4096]{1,0:T(8,128)(2,1)}, u32[]{:S(2)}, u32[]{:S(2)}) collective-permute-start(bf16[96,4096]{1,0:T(8,128)(2,1)S(1)} %constant_dynamic-slice_fusion), channel_id=1, source_target_pairs={{0,8},{8,0},{1,9},{9,1},{2,10},{10,2},{3,11},{11,3},{4,12},{12,4},... | collective-permute-start | bytes 2359304 | tf_op jit(solution)/shard_map/ppermute | solution.py:162
  35.6 1.0 maximum_maximum_fusion
  36.5 3.5 %all-to-all-start = ((bf16[8,144,256]{2,1,0:T(8,128)(2,1)}), bf16[8,144,256]{2,1,0:T(8,128)(2,1)S(1)}, u32[]{:S(2)}, u32[]{:S(2)}) async-start(bf16[8,144,256]{2,1,0:T(8,128)(2,1)} %maximum_maximum_fusion), calls=%async_computation | async-start | bytes 1179648 | tf_op jit(solution)/shard_map/all_to_all | solution.py:21
  40.1 19.8 %collective-permute-done = bf16[96,4096]{1,0:T(8,128)(2,1)} collective-permute-done((bf16[96,4096]{1,0:T(8,128)(2,1)S(1)}, bf16[96,4096]{1,0:T(8,128)(2,1)}, u32[]{:S(2)}, u32[]{:S(2)}) %collective-permute-start) | collective-permute-done | bytes 786464 | tf_op jit(solution)/shard_map/ppermute | solution.py:162
  60.0 1.9 collective-permute-start.1
  65.8 0.8 slice.113
  66.7 1.5 broadcast_select_fusion.5
  68.2 2.3 %broadcast_select_fusion.3 = (bf16[96,8192]{1,0:T(8,128)(2,1)}, bf16[96,8192]{1,0:T(8,128)(2,1)}) fusion(bf16[96,8192]{1,0:T(8,128)(2,1)S(1)} %get-tuple-element.19, pred[]{:T(512)S(6)} %and.22, bf16[96,4096]{1,0:T(8,128)(2,1)S(1)} %get-tuple-element.25, bf16[96,4096]{1,0:T(8,128)(2,1)S(1)} %get-tuple-element.24), kind=kLoop, calls=%fused_computation.19 | loop fusion | flops 4718592 | bytes 6291457 | tf_op jit(solution)/shard_map/jit(_where)/select_n | solution.py:41
  70.5 3.5 %fusion.3 = f32[192,128]{1,0:T(8,128)S(1)} fusion(bf16[8192,128]{1,0:T(8,128)(2,1)} %all-gather.4.cloned.1.call-done, bf16[96,8192]{1,0:T(8,128)(2,1)} %get-tuple-element.23, bf16[96,8192]{1,0:T(8,128)(2,1)} %get-tuple-element.22), kind=kOutput, calls=%fused_computation.5 | convolution fusion | flops 408944640 | bytes 5341184 | tf_op jit(solution)/shard_map/dot_general | solution.py:195
  74.6 0.8 broadcast_in_dim.60
  75.4 6.6 %all-to-all-start.3 = ((bf16[8,192,128]{2,1,0:T(8,128)(2,1)}), bf16[8,192,128]{2,1,0:T(8,128)(2,1)}, u32[]{:S(2)}, u32[]{:S(2)}) async-start(bf16[8,192,128]{2,1,0:T(8,128)(2,1)} %broadcast_in_dim.60), calls=%async_computation.3 | async-start | bytes 786432 | tf_op jit(solution)/shard_map/all_to_all | solution.py:21
  82.0 1.0 maximum_bitcast_fusion
  83.5 1.4 reduce.6
  84.9 1.8 reshape.273
  86.7 1.1 multiply_cosine_fusion
  89.4 5.1 %all-to-all-done.3 = bf16[8,192,128]{2,1,0:T(8,128)(2,1)} async-done(((bf16[8,192,128]{2,1,0:T(8,128)(2,1)}), bf16[8,192,128]{2,1,0:T(8,128)(2,1)}, u32[]{:S(2)}, u32[]{:S(2)}) %all-to-all-start.3) | async-done | bytes 393248 | tf_op jit(solution)/shard_map/all_to_all | solution.py:21
  94.5 4.8 %all-to-all-start.4 = ((bf16[8,2,6208]{2,1,0:T(2,128)(2,1)}), bf16[8,2,6208]{2,1,0:T(2,128)(2,1)S(1)}, u32[]{:S(2)}, u32[]{:S(2)}) async-start(bf16[8,2,6208]{2,1,0:T(2,128)(2,1)} %reshape.273), calls=%async_computation.4 | async-start | bytes 401408 | tf_op jit(solution)/shard_map/all_to_all | solution.py:21
  99.4 1.0 fusion.26
  101.8 2.0 reduce.5
  103.8 1.4 reshape.271
  105.2 7.1 %all-to-all-start.1 = ((bf16[8,2,448]{2,1,0:T(2,128)(2,1)}), bf16[8,2,448]{2,1,0:T(2,128)(2,1)}, u32[]{:S(2)}, u32[]{:S(2)}) async-start(bf16[8,2,448]{2,1,0:T(2,128)(2,1)} %reshape.271), calls=%async_computation.1 | async-start | bytes 32768 | tf_op jit(solution)/shard_map/all_to_all | solution.py:21
  112.3 0.9 reshape.274
  113.3 1.0 copy.65
  115.0 5.6 %all-to-all-done.1 = bf16[8,2,448]{2,1,0:T(2,128)(2,1)} async-done(((bf16[8,2,448]{2,1,0:T(2,128)(2,1)}), bf16[8,2,448]{2,1,0:T(2,128)(2,1)}, u32[]{:S(2)}, u32[]{:S(2)}) %all-to-all-start.1) | async-done | bytes 14368 | tf_op jit(solution)/shard_map/all_to_all | solution.py:21
  120.6 1.4 reshape.272
  124.0 1.3 reshape.266
  125.3 1.1 convert_reduce_fusion
  127.8 1.2 slice.109
  130.3 3.3 %all-to-all-start.5 = ((f32[8,1,768]{2,1,0:T(1,128)}), f32[8,1,768]{2,1,0:T(1,128)S(1)}, u32[]{:S(2)}, u32[]{:S(2)}) async-start(f32[8,1,768]{2,1,0:T(1,128)} %broadcast_in_dim.63), calls=%async_computation.5 | async-start | bytes 49152 | tf_op jit(solution)/shard_map/all_to_all | solution.py:21
  133.7 1.3 dynamic-slice_divide_fusion
  134.9 6.6 %all-to-all-done.5 = f32[8,1,768]{2,1,0:T(1,128)S(1)} async-done(((f32[8,1,768]{2,1,0:T(1,128)}), f32[8,1,768]{2,1,0:T(1,128)S(1)}, u32[]{:S(2)}, u32[]{:S(2)}) %all-to-all-start.5) | async-done | bytes 24608 | tf_op jit(solution)/shard_map/all_to_all | solution.py:21
  142.2 3.3 %all-to-all-start.6 = ((f32[8,1,768]{2,1,0:T(1,128)}), f32[8,1,768]{2,1,0:T(1,128)S(1)}, u32[]{:S(2)}, u32[]{:S(2)}) async-start(f32[8,1,768]{2,1,0:T(1,128)} %broadcast_in_dim.64), calls=%async_computation.6 | async-start | bytes 49152 | tf_op jit(solution)/shard_map/all_to_all | solution.py:21
  150.7 3.0 %all-to-all-done.6 = f32[8,1,768]{2,1,0:T(1,128)S(1)} async-done(((f32[8,1,768]{2,1,0:T(1,128)}), f32[8,1,768]{2,1,0:T(1,128)S(1)}, u32[]{:S(2)}, u32[]{:S(2)}) %all-to-all-start.6) | async-done | bytes 24608 | tf_op jit(solution)/shard_map/all_to_all | solution.py:21
  154.4 4.8 %all-to-all-start.7 = ((f32[8,1,768]{2,1,0:T(1,128)}), f32[8,1,768]{2,1,0:T(1,128)S(1)}, u32[]{:S(2)}, u32[]{:S(2)}) async-start(f32[8,1,768]{2,1,0:T(1,128)} %broadcast_in_dim.65), calls=%async_computation.7 | async-start | bytes 49152 | tf_op jit(solution)/shard_map/all_to_all | solution.py:21
  159.2 1.4 pad_add_fusion.1.span_ref
  160.7 2.5 %all-to-all-done.7 = f32[8,1,768]{2,1,0:T(1,128)S(1)} async-done(((f32[8,1,768]{2,1,0:T(1,128)}), f32[8,1,768]{2,1,0:T(1,128)S(1)}, u32[]{:S(2)}, u32[]{:S(2)}) %all-to-all-start.7) | async-done | bytes 24608 | tf_op jit(solution)/shard_map/all_to_all | solution.py:21
  164.3 2.3 %broadcast_select_fusion.1 = (bf16[96,8192]{1,0:T(8,128)(2,1)}, bf16[96,8192]{1,0:T(8,128)(2,1)}) fusion(bf16[96,8192]{1,0:T(8,128)(2,1)S(1)} %get-tuple-element.19, pred[]{:T(512)S(6)} %and.23, bf16[96,4096]{1,0:T(8,128)(2,1)S(1)} %get-tuple-element.25, bf16[96,4096]{1,0:T(8,128)(2,1)S(1)} %get-tuple-element.24), kind=kLoop, calls=%fused_computation.17 | loop fusion | flops 4718592 | bytes 6291457 | tf_op jit(solution)/shard_map/jit(_where)/select_n | solution.py:41
  166.7 4.2 %fusion.7 = f32[192,256]{1,0:T(8,128)S(1)} fusion(bf16[8192,256]{1,0:T(8,128)(2,1)} %all-gather.6.cloned.1.call-done, bf16[96,8192]{1,0:T(8,128)(2,1)} %get-tuple-element.21, bf16[96,8192]{1,0:T(8,128)(2,1)} %get-tuple-element.20), kind=kOutput, calls=%fused_computation.9 | convolution fusion | flops 811597824 | bytes 7536640 | tf_op jit(solution)/shard_map/dot_general | solution.py:242
  171.8 2.4 %collective-permute-start.2 = (bf16[96,256]{1,0:T(8,128)(2,1)S(1)}, bf16[96,256]{1,0:T(8,128)(2,1)S(1)}, u32[]{:S(2)}, u32[]{:S(2)}) collective-permute-start(bf16[96,256]{1,0:T(8,128)(2,1)S(1)} %bitcast.113), channel_id=1, source_target_pairs={{0,8},{8,0},{1,9},{9,1},{2,10},{10,2},{3,11},{11,3},{4,12},{12,4},... | collective-permute-start | bytes 147464 | tf_op jit(solution)/shard_map/ppermute | solution.py:246
  175.3 2.5 %collective-permute-done.2 = bf16[96,256]{1,0:T(8,128)(2,1)S(1)} collective-permute-done((bf16[96,256]{1,0:T(8,128)(2,1)S(1)}, bf16[96,256]{1,0:T(8,128)(2,1)S(1)}, u32[]{:S(2)}, u32[]{:S(2)}) %collective-permute-start.2) | collective-permute-done | bytes 49184 | tf_op jit(solution)/shard_map/ppermute | solution.py:246
  177.9 1.9 copy-done
  179.8 2.4 %attend.1 = (bf16[96,512]{1,0:T(8,128)(2,1)}, f32[1,512]{1,0:T(1,128)S(1)}) custom-call(s32[4]{0:T(128)S(1)} %pad_add_fusion.1.span_ref, s32[384,2]{1,0:T(8,128)S(1)} %bitcast.80, bf16[384,128]{1,0:T(8,128)(2,1)S(1)} %bitcast.81, bf16[6144,256]{1,0:T(8,128)(2,1)S(1)} %copy-done), custom_call_target="tpu_custom_call" | custom-call | tf_op jit(solution)/shard_map/attend/pallas_call | solution.py:117
  182.9 15.0 %all-to-all-start.8 = ((f32[64,1,512]{2,1,0:T(1,128)}), f32[64,1,512]{2,1,0:T(1,128)S(1)}, u32[]{:S(2)}, u32[]{:S(2)}) async-start(f32[64,1,512]{2,1,0:T(1,128)} %broadcast_in_dim.66), calls=%async_computation.8 | async-start | bytes 262144 | tf_op jit(solution)/shard_map/all_to_all | solution.py:21
  198.1 0.9 copy.54
  200.2 10.3 %all-to-all-done.8 = f32[64,1,512]{2,1,0:T(1,128)S(1)} async-done(((f32[64,1,512]{2,1,0:T(1,128)}), f32[64,1,512]{2,1,0:T(1,128)S(1)}, u32[]{:S(2)}, u32[]{:S(2)}) %all-to-all-start.8) | async-done | bytes 131104 | tf_op jit(solution)/shard_map/all_to_all | solution.py:21
  (108 shorter events, 19.8 us)
Async XLA Ops:
  7.2 25.0 %copy-start.1 = (bf16[96,8192]{1,0:T(8,128)(2,1)S(1)}, bf16[96,8192]{1,0:T(8,128)(2,1)}, u32[]{:S(2)}) copy-start(bf16[96,8192]{1,0:T(8,128)(2,1)} %param.6) | copy-start | bytes 4718596
  7.2 25.0 %copy-start.10 = (f32[8192]{0:T(1024)S(1)}, f32[8192]{0:T(1024)}, u32[]{:S(2)}) copy-start(f32[8192]{0:T(1024)} %param.7) | copy-start | bytes 98308
  7.2 63.3 %all-gather.4.cloned.1.call-start = ((), (), s32[]{:S(2)}) async-start(), calls=%async_computation.9 | async-start | bytes 2359296 | tf_op jit(solution)/shard_map/all_gather | solution.py:154
  32.1 3.2 %copy-start.11 = (s32[96]{0:T(128)S(1)}, s32[96]{0:T(128)}, u32[]{:S(2)}) copy-start(s32[96]{0:T(128)} %param.11) | copy-start | bytes 1156
  32.2 3.3 %copy-start.4 = (bf16[128,512]{1,0:T(8,128)(2,1)S(1)}, bf16[128,512]{1,0:T(8,128)(2,1)}, u32[]{:S(2)}) copy-start(bf16[128,512]{1,0:T(8,128)(2,1)} %param.8) | copy-start | bytes 393220
  32.8 29.1 %copy-start.7 = (bf16[128,128]{1,0:T(8,128)(2,1)S(1)}, bf16[128,128]{1,0:T(8,128)(2,1)}, u32[]{:S(2)}) copy-start(bf16[128,128]{1,0:T(8,128)(2,1)} %param.9) | copy-start | bytes 98308
  32.8 29.2 %copy-start.8 = (bf16[128,128]{1,0:T(8,128)(2,1)S(1)}, bf16[128,128]{1,0:T(8,128)(2,1)}, u32[]{:S(2)}) copy-start(bf16[128,128]{1,0:T(8,128)(2,1)} %param.10) | copy-start | bytes 98308
  32.8 27.2 %collective-permute-start = (bf16[96,4096]{1,0:T(8,128)(2,1)S(1)}, bf16[96,4096]{1,0:T(8,128)(2,1)}, u32[]{:S(2)}, u32[]{:S(2)}) collective-permute-start(bf16[96,4096]{1,0:T(8,128)(2,1)S(1)} %constant_dynamic-slice_fusion), channel_id=1, source_target_pairs={{0,8},{8,0},{1,9},{9,1},{2,10},{10,2},{3,11},{11,3},{4,12},{12,4},... | collective-permute-start | bytes 2359304 | tf_op jit(solution)/shard_map/ppermute | solution.py:162
  36.5 27.6 %all-to-all-start = ((bf16[8,144,256]{2,1,0:T(8,128)(2,1)}), bf16[8,144,256]{2,1,0:T(8,128)(2,1)S(1)}, u32[]{:S(2)}, u32[]{:S(2)}) async-start(bf16[8,144,256]{2,1,0:T(8,128)(2,1)} %maximum_maximum_fusion), calls=%async_computation | async-start | bytes 1179648 | tf_op jit(solution)/shard_map/all_to_all | solution.py:21
  40.1 126.6 %all-gather.6.cloned.1.call-start = ((), (), s32[]{:S(2)}) async-start(), calls=%async_computation.10 | async-start | bytes 4718592 | tf_op jit(solution)/shard_map/all_gather | solution.py:176
  60.0 6.7 %collective-permute-start.1 = (bf16[96,4096]{1,0:T(8,128)(2,1)}, bf16[96,4096]{1,0:T(8,128)(2,1)}, u32[]{:S(2)}, u32[]{:S(2)}) collective-permute-start(bf16[96,4096]{1,0:T(8,128)(2,1)} %collective-permute-done), channel_id=1, source_target_pairs={{0,1},{1,0},{2,3},{3,2},{4,5},{5,4},{6,7},{7,6},{8,9},{9,8},{10,11... | collective-permute-start | bytes 2359304 | tf_op jit(solution)/shard_map/ppermute | solution.py:186
  64.1 2.6 %copy-start.2 = (bf16[8,144,256]{2,1,0:T(8,128)(2,1)}, bf16[8,144,256]{2,1,0:T(8,128)(2,1)S(1)}, u32[]{:S(2)}) copy-start(bf16[8,144,256]{2,1,0:T(8,128)(2,1)S(1)} %all-to-all-done) | copy-start | bytes 1769476
  75.4 19.1 %all-to-all-start.3 = ((bf16[8,192,128]{2,1,0:T(8,128)(2,1)}), bf16[8,192,128]{2,1,0:T(8,128)(2,1)}, u32[]{:S(2)}, u32[]{:S(2)}) async-start(bf16[8,192,128]{2,1,0:T(8,128)(2,1)} %broadcast_in_dim.60), calls=%async_computation.3 | async-start | bytes 786432 | tf_op jit(solution)/shard_map/all_to_all | solution.py:21
  94.5 10.7 %all-to-all-start.4 = ((bf16[8,2,6208]{2,1,0:T(2,128)(2,1)}), bf16[8,2,6208]{2,1,0:T(2,128)(2,1)S(1)}, u32[]{:S(2)}, u32[]{:S(2)}) async-start(bf16[8,2,6208]{2,1,0:T(2,128)(2,1)} %reshape.273), calls=%async_computation.4 | async-start | bytes 401408 | tf_op jit(solution)/shard_map/all_to_all | solution.py:21
  99.4 78.5 %all-gather.8.cloned.1.call-start = ((), (), s32[]{:S(2)}) async-start(), calls=%async_computation.11 | async-start | bytes 3538944 | tf_op jit(solution)/shard_map/all_gather | solution.py:203
  105.2 15.4 %all-to-all-start.1 = ((bf16[8,2,448]{2,1,0:T(2,128)(2,1)}), bf16[8,2,448]{2,1,0:T(2,128)(2,1)}, u32[]{:S(2)}, u32[]{:S(2)}) async-start(bf16[8,2,448]{2,1,0:T(2,128)(2,1)} %reshape.271), calls=%async_computation.1 | async-start | bytes 32768 | tf_op jit(solution)/shard_map/all_to_all | solution.py:21
  122.8 0.6 copy-start.9
  130.3 11.2 %all-to-all-start.5 = ((f32[8,1,768]{2,1,0:T(1,128)}), f32[8,1,768]{2,1,0:T(1,128)S(1)}, u32[]{:S(2)}, u32[]{:S(2)}) async-start(f32[8,1,768]{2,1,0:T(1,128)} %broadcast_in_dim.63), calls=%async_computation.5 | async-start | bytes 49152 | tf_op jit(solution)/shard_map/all_to_all | solution.py:21
  142.2 11.6 %all-to-all-start.6 = ((f32[8,1,768]{2,1,0:T(1,128)}), f32[8,1,768]{2,1,0:T(1,128)S(1)}, u32[]{:S(2)}, u32[]{:S(2)}) async-start(f32[8,1,768]{2,1,0:T(1,128)} %broadcast_in_dim.64), calls=%async_computation.6 | async-start | bytes 49152 | tf_op jit(solution)/shard_map/all_to_all | solution.py:21
  154.4 8.7 %all-to-all-start.7 = ((f32[8,1,768]{2,1,0:T(1,128)}), f32[8,1,768]{2,1,0:T(1,128)S(1)}, u32[]{:S(2)}, u32[]{:S(2)}) async-start(f32[8,1,768]{2,1,0:T(1,128)} %broadcast_in_dim.65), calls=%async_computation.7 | async-start | bytes 49152 | tf_op jit(solution)/shard_map/all_to_all | solution.py:21
  166.6 4.4 %copy-start.5 = (f32[192,64]{1,0:T(8,128)S(1)}, f32[192,64]{1,0:T(8,128)}, u32[]{:S(2)}) copy-start(f32[192,64]{1,0:T(8,128)} %get-tuple-element.40) | copy-start | bytes 147460
  166.7 4.4 %copy-start.6 = (f32[192,64]{1,0:T(8,128)S(1)}, f32[192,64]{1,0:T(8,128)}, u32[]{:S(2)}) copy-start(f32[192,64]{1,0:T(8,128)} %get-tuple-element.41) | copy-start | bytes 147460
  171.8 6.0 %collective-permute-start.2 = (bf16[96,256]{1,0:T(8,128)(2,1)S(1)}, bf16[96,256]{1,0:T(8,128)(2,1)S(1)}, u32[]{:S(2)}, u32[]{:S(2)}) collective-permute-start(bf16[96,256]{1,0:T(8,128)(2,1)S(1)} %bitcast.113), channel_id=1, source_target_pairs={{0,8},{8,0},{1,9},{9,1},{2,10},{10,2},{3,11},{11,3},{4,12},{12,4},... | collective-permute-start | bytes 147464 | tf_op jit(solution)/shard_map/ppermute | solution.py:246
  177.8 20.1 %copy-start.3 = (bf16[8,12288]{1,0:T(8,128)(2,1)S(1)}, bf16[8,12288]{1,0:T(8,128)(2,1)}, u32[]{:S(2)}) copy-start(bf16[8,12288]{1,0:T(8,128)(2,1)} %slice.120) | copy-start | bytes 589828
  177.9 1.9 copy-start
  182.9 27.6 %all-to-all-start.8 = ((f32[64,1,512]{2,1,0:T(1,128)}), f32[64,1,512]{2,1,0:T(1,128)S(1)}, u32[]{:S(2)}, u32[]{:S(2)}) async-start(f32[64,1,512]{2,1,0:T(1,128)} %broadcast_in_dim.66), calls=%async_computation.8 | async-start | bytes 262144 | tf_op jit(solution)/shard_map/all_to_all | solution.py:21
Sparse Core Ops, SparseCore 0:
  30.4 39.2 all-gather.3
  71.8 56.4 all-gather.5
  130.3 47.1 all-gather.7

commit v7 on v5

--- a/solution.py
+++ b/solution.py
@@ -100,22 +100,19 @@
     sent = jnp.broadcast_to(halves, (line // 2, *halves.shape))
     sent = sent.reshape(line, row_count, heads_wide)
     along_z = exchange(jnp.concatenate((sent, peaks, docs, blank), axis=1), LINE)
-    gathered_query = lax.all_gather(
-        along_z[:, :row_count].reshape(-1, heads_wide), "y", axis=0, tiled=True
-    )
+    blocks = {0: along_z[:, :row_count].reshape(-1, heads_wide)}
+    for step in range(1, tall // 2 + 1):
+        for sign in (1, -1):
+            if step < tall // 2 or sign > 0:
+                hop = [(k, (k + sign) % tall) for k in range(tall)]
+                blocks[-sign * step] = lax.ppermute(blocks[-sign * (step - 1)], "y", hop)
     riders = along_z[:, row_count:]
-    peaks = jnp.max(riders[:, :peak_rows], axis=0).reshape(tall, row_count)
-    docs = riders[:, peak_rows, :tok_dev].reshape(line * tok_dev)
-    docs = jnp.broadcast_to(docs, (tall, line * tok_dev))
-    arrived = exchange(jnp.concatenate((peaks, docs), axis=1), "y")
-    input_peak = jnp.max(arrived[:, :row_count], axis=0).astype(jnp.float32)
-    doc_block = arrived[:, row_count:].astype(jnp.int32).reshape(tok_count * tok_dev)
     far = lax.ppermute(near, "core", swap)
     other = jnp.concatenate(
         (jnp.where(core == 0, near, far), jnp.where(core == 0, far, near)), axis=1
     )
 
-    even = (side == 0) & present(along_z)
+    even = (side == 0) & present(blocks[1]) & present(blocks[-1])
     both_rows = in_pair_order(even, normed, other)
     pair_positions = (tok_index - side) * tok_dev + jnp.arange(2 * tok_dev, dtype=jnp.int32)
     pair_positions = pair_positions.astype(jnp.float32)
@@ -129,6 +126,15 @@
     )
     everything = lax.all_gather(sent_y, "y", axis=0, tiled=True)
     key_block, value_block = jnp.split(everything, (HEAD,), axis=1)
+
+    peaks = jnp.max(riders[:, :peak_rows], axis=0).reshape(tall, row_count)
+    ready = present(spread) & present(blocks[2]) & present(blocks[-2])
+    peaks = jnp.where(ready, peaks, 0.0)
+    docs = riders[:, peak_rows, :tok_dev].reshape(line * tok_dev)
+    docs = jnp.broadcast_to(docs, (tall, line * tok_dev))
+    arrived = exchange(jnp.concatenate((peaks, docs), axis=1), "y")
+    input_peak = jnp.max(arrived[:, :row_count], axis=0).astype(jnp.float32)
+    doc_block = arrived[:, row_count:].astype(jnp.int32).reshape(tok_count * tok_dev)
 
     block = jnp.concatenate((w_query, w_key, w_value), axis=1)
     row_peak = jnp.max(jnp.abs(block), axis=1)
@@ -144,30 +150,16 @@
     own_rows = rows[:, : sub_rows * columns].reshape(tp_count, sub_rows, columns)
 
     smoothing = smooth_from(input_peak, weight_peak)
-    column_peak = jnp.max(jnp.abs(smoothing[:, None] * block.astype(jnp.float32)), axis=0)
-    column_peak = jnp.where(present(spread), column_peak, 0.0)
-    column_peak = jnp.max(to_everyone(column_peak, LINE), axis=0)
-    column_peak = jnp.max(to_everyone(column_peak, "y"), axis=0)
-    scale = jnp.maximum(column_peak, 1e-05) / 127.0
-    all_scales = to_everyone(scale, TP)
-    scales = jnp.split(scale, cuts)
-
-    smooth_part = lax.dynamic_slice_in_dim(smoothing, tp_index * sub_rows, sub_rows)
-    gain_part = lax.dynamic_slice_in_dim(
-        norm_gain, tok_index * row_count + tp_index * sub_rows, sub_rows
-    )
-    folded_gain = gain_part / smooth_part
-    coded = (
-        smooth_part[None, :, None] * own_rows.astype(jnp.float32) / all_scales[:, None, :]
-    )
-    codes = tuple(
-        part.transpose(1, 0, 2).reshape(sub_rows, tp_count * part.shape[2])
-        for part in jnp.split(coded, cuts, axis=2)
-    )
-
-    even = (side == 0) & present(all_scales)
-    both_rows = in_pair_order(even, normed, other)
-    turned = jnp.dot(both_rows, gathered_query, preferred_element_type=jnp.float32)
+    y_index = lax.axis_index("y")
+    block_rows = line * row_count
+    turned = 0.0
+    for offset, block_query in blocks.items():
+        first = (y_index + offset) % tall * block_rows
+        turned = turned + jnp.dot(
+            lax.dynamic_slice_in_dim(both_rows, first, block_rows, axis=1),
+            block_query,
+            preferred_element_type=jnp.float32,
+        )
     turned = rotate(turned.reshape(2 * tok_dev, -1, HEAD), pair_positions)
     turned = turned.astype(jnp.bfloat16).reshape(2, tok_dev, half_query)
     mine = jnp.where(side == 0, turned[0], turned[1])
@@ -202,7 +194,28 @@
         .astype(jnp.bfloat16)
     )
     out_peak = jnp.max(jnp.abs(attended), axis=0).astype(jnp.float32)
-    out_scale = jnp.max(to_everyone(out_peak, TOK), axis=0)
+    column_peak = jnp.max(jnp.abs(smoothing[:, None] * block.astype(jnp.float32)), axis=0)
+    largest = jnp.concatenate((column_peak, out_peak))
+    largest = jnp.max(to_everyone(largest, LINE), axis=0)
+    largest = jnp.max(to_everyone(largest, "y"), axis=0)
+    column_peak, out_scale = largest[:columns], largest[columns:]
+    scale = jnp.maximum(column_peak, 1e-05) / 127.0
+    all_scales = to_everyone(scale, TP)
+    scales = jnp.split(scale, cuts)
+
+    smooth_part = lax.dynamic_slice_in_dim(smoothing, tp_index * sub_rows, sub_rows)
+    gain_part = lax.dynamic_slice_in_dim(
+        norm_gain, tok_index * row_count + tp_index * sub_rows, sub_rows
+    )
+    folded_gain = gain_part / smooth_part
+    coded = (
+        smooth_part[None, :, None] * own_rows.astype(jnp.float32) / all_scales[:, None, :]
+    )
+    codes = tuple(
+        part.transpose(1, 0, 2).reshape(sub_rows, tp_count * part.shape[2])
+        for part in jnp.split(coded, cuts, axis=2)
+    )
+
     return (
         attended,
         out_scale,

time: 217 us -> 265 us (1.22)
  the two profiles are of different devices: /device:TPU:2 before, /device:TPU:1 now
where the time goes in v7:
time: 265 us; the launch traced here: 263 us
  waiting for transfers between devices  108 us (41%)
  starting transfers between devices  78.9 us (30%)
  local copies, waits for them, and re-layouts  23.3 us (9%)
  other arithmetic  20.6 us (8%)
  between operations  18.3 us (7%)
  matrix products  13.6 us (5%)
    all_to_all x8, starting transfers between devices, exchange(): return lax.all_to_all(parts, axis, split_axis=0, concat_axis=0, tiled=True)  45.8 us
    ppermute x7, waiting for transfers between devices, on_device(): blocks[-sign * step] = lax.ppermute(blocks[-sign * (step - 1)], 'y', hop)  44.9 us
    all_to_all x8, waiting for transfers between devices, exchange(): return lax.all_to_all(parts, axis, split_axis=0, concat_axis=0, tiled=True)  36 us
    ppermute x1, waiting for transfers between devices, on_device(): lax.ppermute(lax.dynamic_slice_in_dim(normed, core * channels, channels,...  26.9 us
    ppermute x7, starting transfers between devices, on_device(): blocks[-sign * step] = lax.ppermute(blocks[-sign * (step - 1)], 'y', hop)  23.8 us
    unnamed x48, local copies, waits for them, and re-layouts  10.3 us
    dot_general x8, matrix products, on_device(): jnp.dot(lax.dynamic_slice_in_dim(both_rows, first, block_rows, axis=1), b...  6.03 us
  transfers between devices with their start and end apart: 20, of which 13 were waited for; matrix products, arithmetic and copies ran while one was open for 16% of the time, Pallas kernels for 0%

profile of v7, /device:TPU:1, one launch (start us, length us, event | category | flops | bytes accessed | tf_op | source)
XLA Modules:
  0.0 262.7 jit_solution(830487218715889967)
XLA Ops:
  8.8 10.9 %all-to-all-start.1 = ((bf16[8,128,128]{2,1,0:T(8,128)(2,1)}), bf16[8,128,128]{2,1,0:T(8,128)(2,1)}, u32[]{:S(2)}, u32[]{:S(2)}) async-start(bf16[8,128,128]{2,1,0:T(8,128)(2,1)} %bitcast.10), calls=%async_computation.1 | async-start | bytes 524288 | tf_op jit(solution)/shard_map/all_to_all | solution.py:19
  19.7 1.8 fusion.8
  22.4 1.1 maximum_maximum_fusion
  23.6 6.7 %all-to-all-done.1 = bf16[8,128,128]{2,1,0:T(8,128)(2,1)} async-done(((bf16[8,128,128]{2,1,0:T(8,128)(2,1)}), bf16[8,128,128]{2,1,0:T(8,128)(2,1)}, u32[]{:S(2)}, u32[]{:S(2)}) %all-to-all-start.1) | async-done | bytes 262176 | tf_op jit(solution)/shard_map/all_to_all | solution.py:19
  30.3 3.5 %all-to-all-start = ((bf16[8,144,256]{2,1,0:T(8,128)(2,1)}), bf16[8,144,256]{2,1,0:T(8,128)(2,1)S(1)}, u32[]{:S(2)}, u32[]{:S(2)}) async-start(bf16[8,144,256]{2,1,0:T(8,128)(2,1)} %maximum_maximum_fusion), calls=%async_computation | async-start | bytes 1179648 | tf_op jit(solution)/shard_map/all_to_all | solution.py:19
  34.0 3.2 %collective-permute-start.2 = (bf16[96,4096]{1,0:T(8,128)(2,1)S(1)}, bf16[96,4096]{1,0:T(8,128)(2,1)}, u32[]{:S(2)}, u32[]{:S(2)}) collective-permute-start(bf16[96,4096]{1,0:T(8,128)(2,1)S(1)} %constant_dynamic-slice_fusion), channel_id=1, source_target_pairs={{0,8},{8,0},{1,9},{9,1},{2,10},{10,2},{3,11},{11,3},{4,12},{12,4},... | collective-permute-start | bytes 2359304 | tf_op jit(solution)/shard_map/ppermute | solution.py:89
  37.5 26.9 %collective-permute-done.2 = bf16[96,4096]{1,0:T(8,128)(2,1)} collective-permute-done((bf16[96,4096]{1,0:T(8,128)(2,1)S(1)}, bf16[96,4096]{1,0:T(8,128)(2,1)}, u32[]{:S(2)}, u32[]{:S(2)}) %collective-permute-start.2) | collective-permute-done | bytes 786464 | tf_op jit(solution)/shard_map/ppermute | solution.py:89
  64.4 4.1 %collective-permute-start.3 = (bf16[96,4096]{1,0:T(8,128)(2,1)}, bf16[96,4096]{1,0:T(8,128)(2,1)}, u32[]{:S(2)}, u32[]{:S(2)}) collective-permute-start(bf16[96,4096]{1,0:T(8,128)(2,1)} %collective-permute-done.2), channel_id=1, source_target_pairs={{0,1},{1,0},{2,3},{3,2},{4,5},{5,4},{6,7},{7,6},{8,9},{9,8},{10,11... | collective-permute-start | bytes 2359304 | tf_op jit(solution)/shard_map/ppermute | solution.py:110
  68.6 5.1 %collective-permute-start = (bf16[1024,256]{1,0:T(8,128)(2,1)S(1)}, bf16[1024,256]{1,0:T(8,128)(2,1)S(1)}, u32[]{:S(2)}, u32[]{:S(2)}) collective-permute-start(bf16[1024,256]{1,0:T(8,128)(2,1)S(1)} %bitcast.134), channel_id=1, source_target_pairs={{0,448},{64,0},{128,64},{192,128},{256,192},{320,256},{384,320},{4... | collective-permute-start | bytes 1572872 | tf_op jit(solution)/shard_map/ppermute | solution.py:108
  73.7 1.9 collective-permute-start.1
  77.8 4.6 %all-to-all-start.4 = ((bf16[8,2,6208]{2,1,0:T(2,128)(2,1)}), bf16[8,2,6208]{2,1,0:T(2,128)(2,1)S(1)}, u32[]{:S(2)}, u32[]{:S(2)}) async-start(bf16[8,2,6208]{2,1,0:T(2,128)(2,1)} %reshape.305), calls=%async_computation.4 | async-start | bytes 401408 | tf_op jit(solution)/shard_map/all_to_all | solution.py:19
  82.4 8.3 %collective-permute-done = bf16[1024,256]{1,0:T(8,128)(2,1)S(1)} collective-permute-done((bf16[1024,256]{1,0:T(8,128)(2,1)S(1)}, bf16[1024,256]{1,0:T(8,128)(2,1)S(1)}, u32[]{:S(2)}, u32[]{:S(2)}) %collective-permute-start) | collective-permute-done | bytes 524320 | tf_op jit(solution)/shard_map/ppermute | solution.py:108
  94.0 1.5 broadcast_select_fusion.3
  95.5 2.0 broadcast_select_fusion.1
  97.6 2.6 fusion.11
  101.4 1.6 broadcast_in_dim.74
  103.0 7.0 %all-to-all-start.2 = ((bf16[8,192,128]{2,1,0:T(8,128)(2,1)}), bf16[8,192,128]{2,1,0:T(8,128)(2,1)}, u32[]{:S(2)}, u32[]{:S(2)}) async-start(bf16[8,192,128]{2,1,0:T(8,128)(2,1)} %broadcast_in_dim.74), calls=%async_computation.2 | async-start | bytes 786432 | tf_op jit(solution)/shard_map/all_to_all | solution.py:19
  113.7 2.5 collective-permute-start.5
  116.2 8.0 %all-to-all-done.2 = bf16[8,192,128]{2,1,0:T(8,128)(2,1)} async-done(((bf16[8,192,128]{2,1,0:T(8,128)(2,1)}), bf16[8,192,128]{2,1,0:T(8,128)(2,1)}, u32[]{:S(2)}, u32[]{:S(2)}) %all-to-all-start.2) | async-done | bytes 393248 | tf_op jit(solution)/shard_map/all_to_all | solution.py:19
  126.9 5.0 %collective-permute-start.4 = (bf16[1024,256]{1,0:T(8,128)(2,1)}, bf16[1024,256]{1,0:T(8,128)(2,1)}, u32[]{:S(2)}, u32[]{:S(2)}) collective-permute-start(bf16[1024,256]{1,0:T(8,128)(2,1)} %copy-done.3), channel_id=1, source_target_pairs={{0,448},{64,0},{128,64},{192,128},{256,192},{320,256},{384,320},{4... | collective-permute-start | bytes 1572872 | tf_op jit(solution)/shard_map/ppermute | solution.py:108
  132.7 1.4 fusion.39
  134.1 2.1 collective-permute-start.6
  136.5 14.5 %collective-permute-done.4 = bf16[1024,256]{1,0:T(8,128)(2,1)} collective-permute-done((bf16[1024,256]{1,0:T(8,128)(2,1)}, bf16[1024,256]{1,0:T(8,128)(2,1)}, u32[]{:S(2)}, u32[]{:S(2)}) %collective-permute-start.4) | collective-permute-done | bytes 524320 | tf_op jit(solution)/shard_map/ppermute | solution.py:108
  150.9 5.3 %collective-permute-start.7 = (bf16[1024,256]{1,0:T(8,128)(2,1)}, bf16[1024,256]{1,0:T(8,128)(2,1)S(1)}, u32[]{:S(2)}, u32[]{:S(2)}) collective-permute-start(bf16[1024,256]{1,0:T(8,128)(2,1)} %collective-permute-done.4), channel_id=1, source_target_pairs={{0,448},{64,0},{128,64},{192,128},{256,192},{320,256},{384,320},{4... | collective-permute-start | bytes 1572872 | tf_op jit(solution)/shard_map/ppermute | solution.py:108
  156.5 1.3 fusion.37
  157.9 4.7 %collective-permute-done.6 = bf16[1024,256]{1,0:T(8,128)(2,1)S(1)} collective-permute-done((bf16[1024,256]{1,0:T(8,128)(2,1)}, bf16[1024,256]{1,0:T(8,128)(2,1)S(1)}, u32[]{:S(2)}, u32[]{:S(2)}) %collective-permute-start.6) | collective-permute-done | bytes 524320 | tf_op jit(solution)/shard_map/ppermute | solution.py:108
  162.6 1.9 collective-permute-start.8
  164.5 1.3 fusion.13
  165.8 1.5 copy.53
  168.5 1.5 copy.54
  171.1 7.2 %collective-permute-done.7 = bf16[1024,256]{1,0:T(8,128)(2,1)S(1)} collective-permute-done((bf16[1024,256]{1,0:T(8,128)(2,1)}, bf16[1024,256]{1,0:T(8,128)(2,1)S(1)}, u32[]{:S(2)}, u32[]{:S(2)}) %collective-permute-start.7) | collective-permute-done | bytes 524320 | tf_op jit(solution)/shard_map/ppermute | solution.py:108
  178.9 10.1 %collective-permute-done.8 = bf16[1024,256]{1,0:T(8,128)(2,1)S(1)} collective-permute-done((bf16[1024,256]{1,0:T(8,128)(2,1)S(1)}, bf16[1024,256]{1,0:T(8,128)(2,1)S(1)}, u32[]{:S(2)}, u32[]{:S(2)}) %collective-permute-start.8) | collective-permute-done | bytes 524320 | tf_op jit(solution)/shard_map/ppermute | solution.py:108
  191.0 1.3 subtract_convert_fusion
  192.6 1.9 collective-permute-start.9
  194.6 1.2 slice.108
  197.8 3.8 %all-to-all-start.3 = ((bf16[8,2,448]{2,1,0:T(2,128)(2,1)}), bf16[8,2,448]{2,1,0:T(2,128)(2,1)S(1)}, u32[]{:S(2)}, u32[]{:S(2)}) async-start(bf16[8,2,448]{2,1,0:T(2,128)(2,1)} %reshape.303), calls=%async_computation.3 | async-start | bytes 32768 | tf_op jit(solution)/shard_map/all_to_all | solution.py:19
  201.7 6.6 %all-to-all-done.3 = bf16[8,2,448]{2,1,0:T(2,128)(2,1)S(1)} async-done(((bf16[8,2,448]{2,1,0:T(2,128)(2,1)}), bf16[8,2,448]{2,1,0:T(2,128)(2,1)S(1)}, u32[]{:S(2)}, u32[]{:S(2)}) %all-to-all-start.3) | async-done | bytes 14368 | tf_op jit(solution)/shard_map/all_to_all | solution.py:19
  208.6 1.2 fusion.12
  209.8 3.3 %fusion.76 = (f32[4,96]{1,0:T(4,128)S(1)}, f32[1,4,96,6144]{3,2,1,0:T(8,128)S(1)}) fusion(bf16[6144,256]{1,0:T(8,128)(2,1)} %all-gather.5.cloned.1.call-done, pred[96,6144]{1,0:T(8,128)(4,1)S(1)} %fusion.12, bf16[96,256]{1,0:T(8,128)(2,1)S(1)} %get-tuple-element.31, bf16[96,256]{1,0:T(8,128)(2,1)S(1)} %get-tuple-element.30), kind=kOutput, calls=%fused_computation.149 | convolution fusion | flops 611253888 | bytes 11699712 | tf_op jit(solution)/shard_map/tkgd,skd->kgts/dot_general | solution.py:172
  213.1 2.2 fusion
  215.4 1.7 abs_reduce_fusion.3
  217.7 3.3 %all-to-all-start.5 = ((f32[8,1,1280]{2,1,0:T(1,128)}), f32[8,1,1280]{2,1,0:T(1,128)S(1)}, u32[]{:S(2)}, u32[]{:S(2)}) async-start(f32[8,1,1280]{2,1,0:T(1,128)} %broadcast_in_dim.81), calls=%async_computation.5 | async-start | bytes 81920 | tf_op jit(solution)/shard_map/all_to_all | solution.py:19
  221.1 6.8 %all-to-all-done.5 = f32[8,1,1280]{2,1,0:T(1,128)S(1)} async-done(((f32[8,1,1280]{2,1,0:T(1,128)}), f32[8,1,1280]{2,1,0:T(1,128)S(1)}, u32[]{:S(2)}, u32[]{:S(2)}) %all-to-all-start.5) | async-done | bytes 40992 | tf_op jit(solution)/shard_map/all_to_all | solution.py:19
  228.6 3.3 %all-to-all-start.6 = ((f32[8,1,1280]{2,1,0:T(1,128)}), f32[8,1,1280]{2,1,0:T(1,128)S(1)}, u32[]{:S(2)}, u32[]{:S(2)}) async-start(f32[8,1,1280]{2,1,0:T(1,128)} %broadcast_in_dim.82), calls=%async_computation.6 | async-start | bytes 81920 | tf_op jit(solution)/shard_map/all_to_all | solution.py:19
  232.0 1.3 dynamic-slice_divide_fusion
  234.0 4.9 %all-to-all-done.6 = f32[8,1,1280]{2,1,0:T(1,128)S(1)} async-done(((f32[8,1,1280]{2,1,0:T(1,128)}), f32[8,1,1280]{2,1,0:T(1,128)S(1)}, u32[]{:S(2)}, u32[]{:S(2)}) %all-to-all-start.6) | async-done | bytes 40992 | tf_op jit(solution)/shard_map/all_to_all | solution.py:19
  239.5 9.3 %all-to-all-start.7 = ((f32[8,1,768]{2,1,0:T(1,128)}), f32[8,1,768]{2,1,0:T(1,128)S(1)}, u32[]{:S(2)}, u32[]{:S(2)}) async-start(f32[8,1,768]{2,1,0:T(1,128)} %broadcast_in_dim.83), calls=%async_computation.7 | async-start | bytes 49152 | tf_op jit(solution)/shard_map/all_to_all | solution.py:19
  250.5 3.0 %all-to-all-done.7 = f32[8,1,768]{2,1,0:T(1,128)S(1)} async-done(((f32[8,1,768]{2,1,0:T(1,128)}), f32[8,1,768]{2,1,0:T(1,128)S(1)}, u32[]{:S(2)}, u32[]{:S(2)}) %all-to-all-start.7) | async-done | bytes 24608 | tf_op jit(solution)/shard_map/all_to_all | solution.py:19
  (131 shorter events, 28.1 us)
Async XLA Ops:
  7.2 14.4 %copy-start.1 = (bf16[96,8192]{1,0:T(8,128)(2,1)S(1)}, bf16[96,8192]{1,0:T(8,128)(2,1)}, u32[]{:S(2)}) copy-start(bf16[96,8192]{1,0:T(8,128)(2,1)} %param.6) | copy-start | bytes 4718596
  7.2 14.4 %copy-start.11 = (f32[8192]{0:T(1024)S(1)}, f32[8192]{0:T(1024)}, u32[]{:S(2)}) copy-start(f32[8192]{0:T(1024)} %param.7) | copy-start | bytes 98308
  8.8 21.5 %all-to-all-start.1 = ((bf16[8,128,128]{2,1,0:T(8,128)(2,1)}), bf16[8,128,128]{2,1,0:T(8,128)(2,1)}, u32[]{:S(2)}, u32[]{:S(2)}) async-start(bf16[8,128,128]{2,1,0:T(8,128)(2,1)} %bitcast.10), calls=%async_computation.1 | async-start | bytes 524288 | tf_op jit(solution)/shard_map/all_to_all | solution.py:19
  19.7 2.5 copy-start.8
  19.7 2.5 copy-start.12
  22.1 11.8 %copy-start = (bf16[96,8192]{1,0:T(8,128)(2,1)}, bf16[96,8192]{1,0:T(8,128)(2,1)S(1)}, u32[]{:S(2)}) copy-start(bf16[96,8192]{1,0:T(8,128)(2,1)S(1)} %get-tuple-element.15) | copy-start | bytes 4718596
  22.4 14.8 %copy-start.9 = (bf16[128,128]{1,0:T(8,128)(2,1)S(1)}, bf16[128,128]{1,0:T(8,128)(2,1)}, u32[]{:S(2)}) copy-start(bf16[128,128]{1,0:T(8,128)(2,1)} %param.9) | copy-start | bytes 98308
  22.4 14.8 %copy-start.10 = (bf16[128,128]{1,0:T(8,128)(2,1)S(1)}, bf16[128,128]{1,0:T(8,128)(2,1)}, u32[]{:S(2)}) copy-start(bf16[128,128]{1,0:T(8,128)(2,1)} %param.10) | copy-start | bytes 98308
  30.3 38.3 %all-to-all-start = ((bf16[8,144,256]{2,1,0:T(8,128)(2,1)}), bf16[8,144,256]{2,1,0:T(8,128)(2,1)S(1)}, u32[]{:S(2)}, u32[]{:S(2)}) async-start(bf16[8,144,256]{2,1,0:T(8,128)(2,1)} %maximum_maximum_fusion), calls=%async_computation | async-start | bytes 1179648 | tf_op jit(solution)/shard_map/all_to_all | solution.py:19
  33.8 63.7 %all-gather.3.cloned.1.call-start = ((), (), s32[]{:S(2)}) async-start(), calls=%async_computation.8 | async-start | bytes 2359296 | tf_op jit(solution)/shard_map/all_gather | solution.py:81
  34.0 30.5 %collective-permute-start.2 = (bf16[96,4096]{1,0:T(8,128)(2,1)S(1)}, bf16[96,4096]{1,0:T(8,128)(2,1)}, u32[]{:S(2)}, u32[]{:S(2)}) collective-permute-start(bf16[96,4096]{1,0:T(8,128)(2,1)S(1)} %constant_dynamic-slice_fusion), channel_id=1, source_target_pairs={{0,8},{8,0},{1,9},{9,1},{2,10},{10,2},{3,11},{11,3},{4,12},{12,4},... | collective-permute-start | bytes 2359304 | tf_op jit(solution)/shard_map/ppermute | solution.py:89
  64.4 29.6 %collective-permute-start.3 = (bf16[96,4096]{1,0:T(8,128)(2,1)}, bf16[96,4096]{1,0:T(8,128)(2,1)}, u32[]{:S(2)}, u32[]{:S(2)}) collective-permute-start(bf16[96,4096]{1,0:T(8,128)(2,1)} %collective-permute-done.2), channel_id=1, source_target_pairs={{0,1},{1,0},{2,3},{3,2},{4,5},{5,4},{6,7},{7,6},{8,9},{9,8},{10,11... | collective-permute-start | bytes 2359304 | tf_op jit(solution)/shard_map/ppermute | solution.py:110
  68.6 23.6 %copy-start.2 = (bf16[8,144,256]{2,1,0:T(8,128)(2,1)}, bf16[8,144,256]{2,1,0:T(8,128)(2,1)S(1)}, u32[]{:S(2)}) copy-start(bf16[8,144,256]{2,1,0:T(8,128)(2,1)S(1)} %all-to-all-done) | copy-start | bytes 1769476
  68.6 26.9 %copy-start.7 = (bf16[8,128,256]{2,1,0:T(8,128)(2,1)}, bf16[8,128,256]{2,1,0:T(8,128)(2,1)S(1)}, u32[]{:S(2)}) copy-start(bf16[8,128,256]{2,1,0:T(8,128)(2,1)S(1)} %slice.103) | copy-start | bytes 1572868
  68.6 22.1 %collective-permute-start = (bf16[1024,256]{1,0:T(8,128)(2,1)S(1)}, bf16[1024,256]{1,0:T(8,128)(2,1)S(1)}, u32[]{:S(2)}, u32[]{:S(2)}) collective-permute-start(bf16[1024,256]{1,0:T(8,128)(2,1)S(1)} %bitcast.134), channel_id=1, source_target_pairs={{0,448},{64,0},{128,64},{192,128},{256,192},{320,256},{384,320},{4... | collective-permute-start | bytes 1572872 | tf_op jit(solution)/shard_map/ppermute | solution.py:108
  73.7 18.0 %collective-permute-start.1 = (bf16[1024,256]{1,0:T(8,128)(2,1)S(1)}, bf16[1024,256]{1,0:T(8,128)(2,1)S(1)}, u32[]{:S(2)}, u32[]{:S(2)}) collective-permute-start(bf16[1024,256]{1,0:T(8,128)(2,1)S(1)} %bitcast.135), channel_id=1, source_target_pairs={{0,64},{64,128},{128,192},{192,256},{256,320},{320,384},{384,448},... | collective-permute-start | bytes 1572872 | tf_op jit(solution)/shard_map/ppermute | solution.py:108
  77.8 23.5 %all-to-all-start.4 = ((bf16[8,2,6208]{2,1,0:T(2,128)(2,1)}), bf16[8,2,6208]{2,1,0:T(2,128)(2,1)S(1)}, u32[]{:S(2)}, u32[]{:S(2)}) async-start(bf16[8,2,6208]{2,1,0:T(2,128)(2,1)} %reshape.305), calls=%async_computation.4 | async-start | bytes 401408 | tf_op jit(solution)/shard_map/all_to_all | solution.py:19
  90.7 4.8 %copy-start.3 = (bf16[1024,256]{1,0:T(8,128)(2,1)}, bf16[1024,256]{1,0:T(8,128)(2,1)S(1)}, u32[]{:S(2)}) copy-start(bf16[1024,256]{1,0:T(8,128)(2,1)S(1)} %collective-permute-done) | copy-start | bytes 1572868
  91.8 3.8 %copy-start.5 = (bf16[1024,256]{1,0:T(8,128)(2,1)}, bf16[1024,256]{1,0:T(8,128)(2,1)S(1)}, u32[]{:S(2)}) copy-start(bf16[1024,256]{1,0:T(8,128)(2,1)S(1)} %collective-permute-done.1) | copy-start | bytes 1572868
  103.0 21.2 %all-to-all-start.2 = ((bf16[8,192,128]{2,1,0:T(8,128)(2,1)}), bf16[8,192,128]{2,1,0:T(8,128)(2,1)}, u32[]{:S(2)}, u32[]{:S(2)}) async-start(bf16[8,192,128]{2,1,0:T(8,128)(2,1)} %broadcast_in_dim.74), calls=%async_computation.2 | async-start | bytes 786432 | tf_op jit(solution)/shard_map/all_to_all | solution.py:19
  109.9 99.9 %all-gather.5.cloned.1.call-start = ((), (), s32[]{:S(2)}) async-start(), calls=%async_computation.9 | async-start | bytes 3538944 | tf_op jit(solution)/shard_map/all_gather | solution.py:127
  113.7 20.4 %collective-permute-start.5 = (bf16[1024,256]{1,0:T(8,128)(2,1)}, bf16[1024,256]{1,0:T(8,128)(2,1)}, u32[]{:S(2)}, u32[]{:S(2)}) collective-permute-start(bf16[1024,256]{1,0:T(8,128)(2,1)} %copy-done.5), channel_id=1, source_target_pairs={{0,64},{64,128},{128,192},{192,256},{256,320},{320,384},{384,448},... | collective-permute-start | bytes 1572872 | tf_op jit(solution)/shard_map/ppermute | solution.py:108
  126.9 24.1 %collective-permute-start.4 = (bf16[1024,256]{1,0:T(8,128)(2,1)}, bf16[1024,256]{1,0:T(8,128)(2,1)}, u32[]{:S(2)}, u32[]{:S(2)}) collective-permute-start(bf16[1024,256]{1,0:T(8,128)(2,1)} %copy-done.3), channel_id=1, source_target_pairs={{0,448},{64,0},{128,64},{192,128},{256,192},{320,256},{384,320},{4... | collective-permute-start | bytes 1572872 | tf_op jit(solution)/shard_map/ppermute | solution.py:108
  132.7 3.5 %copy-start.6 = (bf16[1024,256]{1,0:T(8,128)(2,1)S(1)}, bf16[1024,256]{1,0:T(8,128)(2,1)}, u32[]{:S(2)}) copy-start(bf16[1024,256]{1,0:T(8,128)(2,1)} %copy-done.5) | copy-start | bytes 1572868
  134.1 22.1 %copy-start.4 = (bf16[1024,256]{1,0:T(8,128)(2,1)S(1)}, bf16[1024,256]{1,0:T(8,128)(2,1)}, u32[]{:S(2)}) copy-start(bf16[1024,256]{1,0:T(8,128)(2,1)} %copy-done.3) | copy-start | bytes 1572868
  134.1 28.5 %collective-permute-start.6 = (bf16[1024,256]{1,0:T(8,128)(2,1)}, bf16[1024,256]{1,0:T(8,128)(2,1)S(1)}, u32[]{:S(2)}, u32[]{:S(2)}) collective-permute-start(bf16[1024,256]{1,0:T(8,128)(2,1)} %collective-permute-done.5), channel_id=1, source_target_pairs={{0,64},{64,128},{128,192},{192,256},{256,320},{320,384},{384,448},... | collective-permute-start | bytes 1572872 | tf_op jit(solution)/shard_map/ppermute | solution.py:108
  150.9 27.4 %collective-permute-start.7 = (bf16[1024,256]{1,0:T(8,128)(2,1)}, bf16[1024,256]{1,0:T(8,128)(2,1)S(1)}, u32[]{:S(2)}, u32[]{:S(2)}) collective-permute-start(bf16[1024,256]{1,0:T(8,128)(2,1)} %collective-permute-done.4), channel_id=1, source_target_pairs={{0,448},{64,0},{128,64},{192,128},{256,192},{320,256},{384,320},{4... | collective-permute-start | bytes 1572872 | tf_op jit(solution)/shard_map/ppermute | solution.py:108
  162.6 26.4 %collective-permute-start.8 = (bf16[1024,256]{1,0:T(8,128)(2,1)S(1)}, bf16[1024,256]{1,0:T(8,128)(2,1)S(1)}, u32[]{:S(2)}, u32[]{:S(2)}) collective-permute-start(bf16[1024,256]{1,0:T(8,128)(2,1)S(1)} %collective-permute-done.6), channel_id=1, source_target_pairs={{0,64},{64,128},{128,192},{192,256},{256,320},{320,384},{384,448},... | collective-permute-start | bytes 1572872 | tf_op jit(solution)/shard_map/ppermute | solution.py:108
  178.9 29.7 %copy-start.13 = (s32[96]{0:T(128)S(1)}, s32[96]{0:T(128)}, u32[]{:S(2)}) copy-start(s32[96]{0:T(128)} %param.11) | copy-start | bytes 1156
  192.6 9.0 %collective-permute-start.9 = (bf16[96,256]{1,0:T(8,128)(2,1)S(1)}, bf16[96,256]{1,0:T(8,128)(2,1)S(1)}, u32[]{:S(2)}, u32[]{:S(2)}) collective-permute-start(bf16[96,256]{1,0:T(8,128)(2,1)S(1)} %bitcast.166), channel_id=1, source_target_pairs={{0,8},{8,0},{1,9},{9,1},{2,10},{10,2},{3,11},{11,3},{4,12},{12,4},... | collective-permute-start | bytes 147464 | tf_op jit(solution)/shard_map/ppermute | solution.py:166
  197.8 10.5 %all-to-all-start.3 = ((bf16[8,2,448]{2,1,0:T(2,128)(2,1)}), bf16[8,2,448]{2,1,0:T(2,128)(2,1)S(1)}, u32[]{:S(2)}, u32[]{:S(2)}) async-start(bf16[8,2,448]{2,1,0:T(2,128)(2,1)} %reshape.303), calls=%async_computation.3 | async-start | bytes 32768 | tf_op jit(solution)/shard_map/all_to_all | solution.py:19
  213.1 2.2 copy-start.14
  217.7 10.2 %all-to-all-start.5 = ((f32[8,1,1280]{2,1,0:T(1,128)}), f32[8,1,1280]{2,1,0:T(1,128)S(1)}, u32[]{:S(2)}, u32[]{:S(2)}) async-start(f32[8,1,1280]{2,1,0:T(1,128)} %broadcast_in_dim.81), calls=%async_computation.5 | async-start | bytes 81920 | tf_op jit(solution)/shard_map/all_to_all | solution.py:19
  228.6 10.2 %all-to-all-start.6 = ((f32[8,1,1280]{2,1,0:T(1,128)}), f32[8,1,1280]{2,1,0:T(1,128)S(1)}, u32[]{:S(2)}, u32[]{:S(2)}) async-start(f32[8,1,1280]{2,1,0:T(1,128)} %broadcast_in_dim.82), calls=%async_computation.6 | async-start | bytes 81920 | tf_op jit(solution)/shard_map/all_to_all | solution.py:19
  239.5 14.0 %all-to-all-start.7 = ((f32[8,1,768]{2,1,0:T(1,128)}), f32[8,1,768]{2,1,0:T(1,128)S(1)}, u32[]{:S(2)}, u32[]{:S(2)}) async-start(f32[8,1,768]{2,1,0:T(1,128)} %broadcast_in_dim.83), calls=%async_computation.7 | async-start | bytes 49152 | tf_op jit(solution)/shard_map/all_to_all | solution.py:19
Sparse Core Ops, SparseCore 0:
  37.6 45.7 all-gather.2
  126.2 60.8 all-gather.4

commit v8 on v5

--- a/solution.py
+++ b/solution.py
@@ -9,6 +9,7 @@
 HEAD = 128
 KVH = 8
 QHEADS = 32
+DOC_MOST = 4608
 LINE = ("z", "pair")
 TOK = ("y", "z", "pair")
 TP = ("x", "core")
@@ -128,7 +129,6 @@
         (spread[:, 0].reshape(-1, HEAD), spread[:, 1].reshape(-1, HEAD)), axis=1
     )
     everything = lax.all_gather(sent_y, "y", axis=0, tiled=True)
-    key_block, value_block = jnp.split(everything, (HEAD,), axis=1)
 
     block = jnp.concatenate((w_query, w_key, w_value), axis=1)
     row_peak = jnp.max(jnp.abs(block), axis=1)
@@ -176,18 +176,25 @@
         (jnp.where(side == 0, mine, swapped), jnp.where(side == 0, swapped, mine)), axis=1
     ).reshape(tok_dev, 1, group_size, HEAD)
 
-    length = key_block.shape[0]
+    query_positions = tok_index * tok_dev + jnp.arange(tok_dev, dtype=jnp.int32)
+    length = doc_block.shape[0]
+    window = min(length, -(-(DOC_MOST - 1 + tok_dev + 127) // 256) * 256)
+    start = jnp.sum((doc_block < doc_ids[0]).astype(jnp.int32)) // 128 * 128
+    start = jnp.minimum(start, length - window)
+    doc_window = lax.dynamic_slice_in_dim(doc_block, start, window)
+    key_positions = start + jnp.arange(window, dtype=jnp.int32)
+    allowed = (doc_ids[:, None] == doc_window[None, :]) & (
+        key_positions[None, :] <= query_positions[:, None]
+    )
+    seen = lax.dynamic_slice_in_dim(everything, start, window)
+    key_block, value_block = jnp.split(seen, (HEAD,), axis=1)
+
     scores = jnp.einsum(
         "tkgd,skd->kgts", query, key_block[:, None, :], preferred_element_type=jnp.float32
     ) * (1.0 / math.sqrt(HEAD))
-    query_positions = tok_index * tok_dev + jnp.arange(tok_dev, dtype=jnp.int32)
-    key_positions = jnp.arange(length, dtype=jnp.int32)
-    allowed = (doc_ids[:, None] == doc_block[None, :]) & (
-        key_positions[None, :] <= query_positions[:, None]
-    )
     scores = jnp.where(allowed, scores, -1e30)
     highest = jnp.max(scores, axis=3, keepdims=True)
-    weights = jnp.where(allowed, jnp.exp(scores - highest), 0.0)
+    weights = jnp.exp(scores - highest)
     totals = jnp.sum(weights, axis=3)
     accumulated = jnp.einsum(
         "kgts,skd->kgtd",

time: 217 us -> 219 us (level)
  waiting for transfers between devices: 64.3 us -> 60.8 us
  between operations: 16.3 us -> 18.9 us
    all_gather x1, waiting for transfers between devices: 6.5 us -> 1.8 us  [on_device(): everything = lax.all_gather(sent_y, 'y', axis=0, tiled=True)]
    unnamed x49 -> x47, local copies, waits for them, and re-layouts: 11.1 us -> 11.1 us
  transfers between devices with their start and end apart: 14 -> 14, of which waited for: 10 -> 10; matrix products, arithmetic and copies ran while one was open for 23% -> 24% of each run, Pallas kernels for 0% -> 0%
where the time goes in v8:
time: 219 us; the launch traced here: 217 us
  waiting for transfers between devices  60.8 us (28%)
  starting transfers between devices  51.7 us (24%)
  other arithmetic  25.8 us (12%)
  local copies, waits for them, and re-layouts  23.1 us (11%)
  blocking collectives  22.1 us (10%)
  between operations  18.9 us (9%)
  matrix products  14.5 us (7%)
    all_to_all x8, waiting for transfers between devices, exchange(): return lax.all_to_all(parts, axis, split_axis=0, concat_axis=0, tiled=True)  53.5 us
    all_to_all x8, starting transfers between devices, exchange(): return lax.all_to_all(parts, axis, split_axis=0, concat_axis=0, tiled=True)  43.4 us
    all_to_all x1, blocking collectives, exchange(): return lax.all_to_all(parts, axis, split_axis=0, concat_axis=0, tiled=True)  22.1 us
    unnamed x47, local copies, waits for them, and re-layouts  11.1 us
    select_n x2, other arithmetic, in_pair_order(): jnp.where(even, own, other)  4.59 us
  transfers between devices with their start and end apart: 14, of which 10 were waited for; matrix products, arithmetic and copies ran while one was open for 24% of the time, Pallas kernels for 0%

profile of v8, /device:TPU:2, one launch (start us, length us, event | category | flops | bytes accessed | tf_op | source)
XLA Modules:
  0.0 216.9 jit_solution(2588125635619746552)
XLA Ops:
  7.3 0.9 pad_maximum_fusion.3
  8.2 22.1 %all_to_all.63 = bf16[8,128,128]{2,1,0:T(8,128)(2,1)} all-to-all(bf16[8,128,128]{2,1,0:T(8,128)(2,1)S(1)} %bitcast.124), channel_id=1, replica_groups=mesh['y'=8,'z'=4,'pair'=2,'x'=4,'core'=2] {'z','pair'}, dimensions={0} | all-to-all | bytes 524288 | tf_op jit(solution)/shard_map/all_to_all | solution.py:20
  30.3 1.8 fusion.9
  32.2 1.3 abs_reduce_fusion
  33.8 1.0 maximum_maximum_fusion
  34.7 3.5 %all-to-all-start = ((bf16[8,144,256]{2,1,0:T(8,128)(2,1)}), bf16[8,144,256]{2,1,0:T(8,128)(2,1)S(1)}, u32[]{:S(2)}, u32[]{:S(2)}) async-start(bf16[8,144,256]{2,1,0:T(8,128)(2,1)} %maximum_maximum_fusion), calls=%async_computation | async-start | bytes 1179648 | tf_op jit(solution)/shard_map/all_to_all | solution.py:20
  38.4 3.8 %collective-permute-start = (bf16[96,4096]{1,0:T(8,128)(2,1)S(1)}, bf16[96,4096]{1,0:T(8,128)(2,1)}, u32[]{:S(2)}, u32[]{:S(2)}) collective-permute-start(bf16[96,4096]{1,0:T(8,128)(2,1)S(1)} %constant_dynamic-slice_fusion), channel_id=1, source_target_pairs={{0,8},{8,0},{1,9},{9,1},{2,10},{10,2},{3,11},{11,3},{4,12},{12,4},... | collective-permute-start | bytes 2359304 | tf_op jit(solution)/shard_map/ppermute | solution.py:90
  43.1 13.9 %all-to-all-done = bf16[8,144,256]{2,1,0:T(8,128)(2,1)S(1)} async-done(((bf16[8,144,256]{2,1,0:T(8,128)(2,1)}), bf16[8,144,256]{2,1,0:T(8,128)(2,1)S(1)}, u32[]{:S(2)}, u32[]{:S(2)}) %all-to-all-start) | async-done | bytes 589856 | tf_op jit(solution)/shard_map/all_to_all | solution.py:20
  57.1 0.8 slice.103
  57.9 0.8 maximum_bitcast_fusion
  60.0 0.9 reshape.303
  60.9 4.8 %all-to-all-start.4 = ((bf16[8,2,6208]{2,1,0:T(2,128)(2,1)}), bf16[8,2,6208]{2,1,0:T(2,128)(2,1)}, u32[]{:S(2)}, u32[]{:S(2)}) async-start(bf16[8,2,6208]{2,1,0:T(2,128)(2,1)} %reshape.303), calls=%async_computation.4 | async-start | bytes 401408 | tf_op jit(solution)/shard_map/all_to_all | solution.py:20
  65.7 3.1 %collective-permute-done = bf16[96,4096]{1,0:T(8,128)(2,1)} collective-permute-done((bf16[96,4096]{1,0:T(8,128)(2,1)S(1)}, bf16[96,4096]{1,0:T(8,128)(2,1)}, u32[]{:S(2)}, u32[]{:S(2)}) %collective-permute-start) | collective-permute-done | bytes 786464 | tf_op jit(solution)/shard_map/ppermute | solution.py:90
  68.7 1.9 collective-permute-start.1
  74.5 1.5 broadcast_select_fusion.5
  75.9 2.3 %broadcast_select_fusion.3 = (bf16[96,8192]{1,0:T(8,128)(2,1)}, bf16[96,8192]{1,0:T(8,128)(2,1)}) fusion(bf16[96,8192]{1,0:T(8,128)(2,1)S(1)} %get-tuple-element.15, pred[]{:T(512)S(6)} %and.21, bf16[96,4096]{1,0:T(8,128)(2,1)S(1)} %get-tuple-element.21, bf16[96,4096]{1,0:T(8,128)(2,1)S(1)} %get-tuple-element.20), kind=kLoop, calls=%fused_computation.30 | loop fusion | flops 4718592 | bytes 6291457 | tf_op jit(solution)/shard_map/jit(_where)/select_n | solution.py:40
  78.2 3.5 %fusion.12 = f32[192,128]{1,0:T(8,128)S(1)} fusion(bf16[8192,128]{1,0:T(8,128)(2,1)} %all-gather.4.cloned.1.call-done, bf16[96,8192]{1,0:T(8,128)(2,1)} %get-tuple-element.19, bf16[96,8192]{1,0:T(8,128)(2,1)} %get-tuple-element.18), kind=kOutput, calls=%fused_computation.16 | convolution fusion | flops 408944640 | bytes 5341184 | tf_op jit(solution)/shard_map/dot_general | solution.py:123
  82.2 7.1 %all-to-all-start.1 = ((bf16[8,2,448]{2,1,0:T(2,128)(2,1)}), bf16[8,2,448]{2,1,0:T(2,128)(2,1)S(1)}, u32[]{:S(2)}, u32[]{:S(2)}) async-start(bf16[8,2,448]{2,1,0:T(2,128)(2,1)} %reshape.301), calls=%async_computation.1 | async-start | bytes 32768 | tf_op jit(solution)/shard_map/all_to_all | solution.py:20
  90.1 7.4 %all-to-all-done.1 = bf16[8,2,448]{2,1,0:T(2,128)(2,1)S(1)} async-done(((bf16[8,2,448]{2,1,0:T(2,128)(2,1)}), bf16[8,2,448]{2,1,0:T(2,128)(2,1)S(1)}, u32[]{:S(2)}, u32[]{:S(2)}) %all-to-all-start.1) | async-done | bytes 14368 | tf_op jit(solution)/shard_map/all_to_all | solution.py:20
  97.5 1.6 broadcast_in_dim.76
  99.1 5.8 %all-to-all-start.3 = ((bf16[8,192,128]{2,1,0:T(8,128)(2,1)}), bf16[8,192,128]{2,1,0:T(8,128)(2,1)}, u32[]{:S(2)}, u32[]{:S(2)}) async-start(bf16[8,192,128]{2,1,0:T(8,128)(2,1)} %broadcast_in_dim.76), calls=%async_computation.3 | async-start | bytes 786432 | tf_op jit(solution)/shard_map/all_to_all | solution.py:20
  105.0 1.8 multiply_cosine_fusion
  106.8 2.3 %reshape.304 = bf16[8,1,12416]{2,1,0:T(2,128)(2,1)} reshape(bf16[8,2,6208]{2,1,0:T(2,128)(2,1)} %all-to-all-done.4) | data formatting | bytes 397312
  109.1 1.1 copy.73
  110.8 1.4 reshape.302
  113.7 5.2 %all-to-all-done.3 = bf16[8,192,128]{2,1,0:T(8,128)(2,1)} async-done(((bf16[8,192,128]{2,1,0:T(8,128)(2,1)}), bf16[8,192,128]{2,1,0:T(8,128)(2,1)}, u32[]{:S(2)}, u32[]{:S(2)}) %all-to-all-start.3) | async-done | bytes 393248 | tf_op jit(solution)/shard_map/all_to_all | solution.py:20
  118.9 1.1 fusion.45
  120.8 1.4 convert_reduce_fusion
  125.5 1.1 slice.99
  128.0 3.3 %all-to-all-start.5 = ((f32[8,1,768]{2,1,0:T(1,128)}), f32[8,1,768]{2,1,0:T(1,128)S(1)}, u32[]{:S(2)}, u32[]{:S(2)}) async-start(f32[8,1,768]{2,1,0:T(1,128)} %broadcast_in_dim.79), calls=%async_computation.5 | async-start | bytes 49152 | tf_op jit(solution)/shard_map/all_to_all | solution.py:20
  131.4 7.7 %all-to-all-done.5 = f32[8,1,768]{2,1,0:T(1,128)S(1)} async-done(((f32[8,1,768]{2,1,0:T(1,128)}), f32[8,1,768]{2,1,0:T(1,128)S(1)}, u32[]{:S(2)}, u32[]{:S(2)}) %all-to-all-start.5) | async-done | bytes 24608 | tf_op jit(solution)/shard_map/all_to_all | solution.py:20
  139.8 3.3 %all-to-all-start.6 = ((f32[8,1,768]{2,1,0:T(1,128)}), f32[8,1,768]{2,1,0:T(1,128)S(1)}, u32[]{:S(2)}, u32[]{:S(2)}) async-start(f32[8,1,768]{2,1,0:T(1,128)} %broadcast_in_dim.80), calls=%async_computation.6 | async-start | bytes 49152 | tf_op jit(solution)/shard_map/all_to_all | solution.py:20
  143.2 1.2 compare_and_fusion
  144.4 6.9 %all-to-all-done.6 = f32[8,1,768]{2,1,0:T(1,128)S(1)} async-done(((f32[8,1,768]{2,1,0:T(1,128)}), f32[8,1,768]{2,1,0:T(1,128)S(1)}, u32[]{:S(2)}, u32[]{:S(2)}) %all-to-all-start.6) | async-done | bytes 24608 | tf_op jit(solution)/shard_map/all_to_all | solution.py:20
  152.0 4.8 %all-to-all-start.7 = ((f32[8,1,768]{2,1,0:T(1,128)}), f32[8,1,768]{2,1,0:T(1,128)S(1)}, u32[]{:S(2)}, u32[]{:S(2)}) async-start(f32[8,1,768]{2,1,0:T(1,128)} %broadcast_in_dim.81), calls=%async_computation.7 | async-start | bytes 49152 | tf_op jit(solution)/shard_map/all_to_all | solution.py:20
  156.8 1.3 dynamic-slice_divide_fusion
  158.1 2.7 %all-to-all-done.7 = f32[8,1,768]{2,1,0:T(1,128)S(1)} async-done(((f32[8,1,768]{2,1,0:T(1,128)}), f32[8,1,768]{2,1,0:T(1,128)S(1)}, u32[]{:S(2)}, u32[]{:S(2)}) %all-to-all-start.7) | async-done | bytes 24608 | tf_op jit(solution)/shard_map/all_to_all | solution.py:20
  161.9 2.3 %broadcast_select_fusion.1 = (bf16[96,8192]{1,0:T(8,128)(2,1)}, bf16[96,8192]{1,0:T(8,128)(2,1)}) fusion(bf16[96,8192]{1,0:T(8,128)(2,1)S(1)} %get-tuple-element.15, pred[]{:T(512)S(6)} %and.22, bf16[96,4096]{1,0:T(8,128)(2,1)S(1)} %get-tuple-element.21, bf16[96,4096]{1,0:T(8,128)(2,1)S(1)} %get-tuple-element.20), kind=kLoop, calls=%fused_computation.28 | loop fusion | flops 4718592 | bytes 6291457 | tf_op jit(solution)/shard_map/jit(_where)/select_n | solution.py:40
  164.2 4.3 %fusion.16 = f32[192,256]{1,0:T(8,128)S(1)} fusion(bf16[8192,256]{1,0:T(8,128)(2,1)} %all-gather.8.cloned.1.call-done, bf16[96,8192]{1,0:T(8,128)(2,1)} %get-tuple-element.17, bf16[96,8192]{1,0:T(8,128)(2,1)} %get-tuple-element.16), kind=kOutput, calls=%fused_computation.20 | convolution fusion | flops 811597824 | bytes 7536640 | tf_op jit(solution)/shard_map/dot_general | solution.py:170
  169.4 2.5 %collective-permute-start.2 = (bf16[96,256]{1,0:T(8,128)(2,1)S(1)}, bf16[96,256]{1,0:T(8,128)(2,1)S(1)}, u32[]{:S(2)}, u32[]{:S(2)}) collective-permute-start(bf16[96,256]{1,0:T(8,128)(2,1)S(1)} %bitcast.154), channel_id=1, source_target_pairs={{0,8},{8,0},{1,9},{9,1},{2,10},{10,2},{3,11},{11,3},{4,12},{12,4},... | collective-permute-start | bytes 147464 | tf_op jit(solution)/shard_map/ppermute | solution.py:174
  173.0 2.4 %collective-permute-done.2 = bf16[96,256]{1,0:T(8,128)(2,1)S(1)} collective-permute-done((bf16[96,256]{1,0:T(8,128)(2,1)S(1)}, bf16[96,256]{1,0:T(8,128)(2,1)S(1)}, u32[]{:S(2)}, u32[]{:S(2)}) %collective-permute-start.2) | collective-permute-done | bytes 49184 | tf_op jit(solution)/shard_map/ppermute | solution.py:174
  175.4 1.8 all-gather.6.cloned.1.call-done
  177.2 3.3 %select_reduce_fusion = (f32[4,96]{1,0:T(4,128)S(1)}, f32[1,4,96,4864]{3,2,1,0:T(8,128)S(1)}) fusion(pred[96,4864]{1,0:T(8,128)(4,1)S(1)} %copy-done.1, bf16[6144,256]{1,0:T(8,128)(2,1)} %all-gather.6.cloned.1.call-done, s32[]{:T(128)S(6)} %select_n.101, bf16[96,256]{1,0:T(8,128)(2,1)S(1)} %get-tuple-element.33, bf16[96,256]{1,0:T(8,128)(2,1)S(1)} %get-tuple-element.32), kind=kOutput, calls=%fused_computation.3 | convolution fusion | flops 483950208 | bytes 9283076 | tf_op jit(solution)/shard_map/tkgd,skd->kgts/dot_general | solution.py:192
  180.4 1.8 fusion.1
  182.2 3.5 %abs_reduce_fusion.3 = (bf16[4,128]{1,0:T(4,128)(2,1)S(1)}, bf16[4,96,128]{2,1,0:T(8,128)(2,1)S(1)}) fusion(f32[4,96]{1,0:T(4,128)S(1)} %fusion.1, bf16[6144,256]{1,0:T(8,128)(2,1)} %all-gather.6.cloned.1.call-done, s32[]{:T(128)S(6)} %select_n.101, s32[]{:T(128)S(6)} %add.94, f32[1,4,96,4864]{3,2,1,0:T(8,128)S(1)} %get-tuple-element.39, ...), kind=kOutput, calls=%fused_computation.67 | convolution fusion | flops 483950080 | bytes 9285640 | tf_op jit(solution)/shard_map/kgts,skd->kgtd/dot_general | solution.py:199
  186.5 10.6 %all-to-all-start.8 = ((f32[64,1,512]{2,1,0:T(1,128)}), f32[64,1,512]{2,1,0:T(1,128)S(1)}, u32[]{:S(2)}, u32[]{:S(2)}) async-start(f32[64,1,512]{2,1,0:T(1,128)} %broadcast_in_dim.83), calls=%async_computation.8 | async-start | bytes 262144 | tf_op jit(solution)/shard_map/all_to_all | solution.py:20
  197.3 0.9 copy.55
  200.1 9.6 %all-to-all-done.8 = f32[64,1,512]{2,1,0:T(1,128)S(1)} async-done(((f32[64,1,512]{2,1,0:T(1,128)}), f32[64,1,512]{2,1,0:T(1,128)S(1)}, u32[]{:S(2)}, u32[]{:S(2)}) %all-to-all-start.8) | async-done | bytes 131104 | tf_op jit(solution)/shard_map/all_to_all | solution.py:20
  (115 shorter events, 18.6 us)
Async XLA Ops:
  7.2 25.0 %copy-start = (bf16[96,8192]{1,0:T(8,128)(2,1)S(1)}, bf16[96,8192]{1,0:T(8,128)(2,1)}, u32[]{:S(2)}) copy-start(bf16[96,8192]{1,0:T(8,128)(2,1)} %param.6) | copy-start | bytes 4718596
  7.2 26.4 %copy-start.13 = (s32[96]{0:T(128)S(1)}, s32[96]{0:T(128)}, u32[]{:S(2)}) copy-start(s32[96]{0:T(128)} %param.11) | copy-start | bytes 1156
  7.2 26.5 %copy-start.3 = (bf16[128,512]{1,0:T(8,128)(2,1)S(1)}, bf16[128,512]{1,0:T(8,128)(2,1)}, u32[]{:S(2)}) copy-start(bf16[128,512]{1,0:T(8,128)(2,1)} %param.8) | copy-start | bytes 393220
  7.2 71.0 %all-gather.4.cloned.1.call-start = ((), (), s32[]{:S(2)}) async-start(), calls=%async_computation.9 | async-start | bytes 2359296 | tf_op jit(solution)/shard_map/all_gather | solution.py:82
  33.5 8.7 %copy-start.4 = (bf16[128,512]{1,0:T(8,128)(2,1)S(1)}, bf16[128,512]{1,0:T(8,128)(2,1)}, u32[]{:S(2)}) copy-start(bf16[128,512]{1,0:T(8,128)(2,1)} %param.8) | copy-start | bytes 393220
  33.5 8.7 %copy-start.7 = (bf16[128,128]{1,0:T(8,128)(2,1)S(1)}, bf16[128,128]{1,0:T(8,128)(2,1)}, u32[]{:S(2)}) copy-start(bf16[128,128]{1,0:T(8,128)(2,1)} %param.9) | copy-start | bytes 98308
  33.5 8.7 %copy-start.8 = (bf16[128,128]{1,0:T(8,128)(2,1)S(1)}, bf16[128,128]{1,0:T(8,128)(2,1)}, u32[]{:S(2)}) copy-start(bf16[128,128]{1,0:T(8,128)(2,1)} %param.10) | copy-start | bytes 98308
  34.7 22.3 %all-to-all-start = ((bf16[8,144,256]{2,1,0:T(8,128)(2,1)}), bf16[8,144,256]{2,1,0:T(8,128)(2,1)S(1)}, u32[]{:S(2)}, u32[]{:S(2)}) async-start(bf16[8,144,256]{2,1,0:T(8,128)(2,1)} %maximum_maximum_fusion), calls=%async_computation | async-start | bytes 1179648 | tf_op jit(solution)/shard_map/all_to_all | solution.py:20
  38.3 125.9 %all-gather.8.cloned.1.call-start = ((), (), s32[]{:S(2)}) async-start(), calls=%async_computation.11 | async-start | bytes 4718592 | tf_op jit(solution)/shard_map/all_gather | solution.py:104
  38.4 30.3 %collective-permute-start = (bf16[96,4096]{1,0:T(8,128)(2,1)S(1)}, bf16[96,4096]{1,0:T(8,128)(2,1)}, u32[]{:S(2)}, u32[]{:S(2)}) collective-permute-start(bf16[96,4096]{1,0:T(8,128)(2,1)S(1)} %constant_dynamic-slice_fusion), channel_id=1, source_target_pairs={{0,8},{8,0},{1,9},{9,1},{2,10},{10,2},{3,11},{11,3},{4,12},{12,4},... | collective-permute-start | bytes 2359304 | tf_op jit(solution)/shard_map/ppermute | solution.py:90
  60.9 21.4 %all-to-all-start.4 = ((bf16[8,2,6208]{2,1,0:T(2,128)(2,1)}), bf16[8,2,6208]{2,1,0:T(2,128)(2,1)}, u32[]{:S(2)}, u32[]{:S(2)}) async-start(bf16[8,2,6208]{2,1,0:T(2,128)(2,1)} %reshape.303), calls=%async_computation.4 | async-start | bytes 401408 | tf_op jit(solution)/shard_map/all_to_all | solution.py:20
  68.7 5.7 %collective-permute-start.1 = (bf16[96,4096]{1,0:T(8,128)(2,1)}, bf16[96,4096]{1,0:T(8,128)(2,1)}, u32[]{:S(2)}, u32[]{:S(2)}) collective-permute-start(bf16[96,4096]{1,0:T(8,128)(2,1)} %collective-permute-done), channel_id=1, source_target_pairs={{0,1},{1,0},{2,3},{3,2},{4,5},{5,4},{6,7},{7,6},{8,9},{9,8},{10,11... | collective-permute-start | bytes 2359304 | tf_op jit(solution)/shard_map/ppermute | solution.py:114
  70.7 11.1 %copy-start.12 = (f32[64]{0:T(128)}, f32[64]{0:T(128)S(1)}, u32[]{:S(2)}) copy-start(f32[64]{0:T(128)S(1)} %multiply_exponential_fusion) | copy-start | bytes 772
  71.2 10.6 %copy-start.11 = (f32[192]{0:T(256)}, f32[192]{0:T(256)S(1)}, u32[]{:S(2)}) copy-start(f32[192]{0:T(256)S(1)} %add_convert_fusion.1) | copy-start | bytes 2308
  82.2 15.3 %all-to-all-start.1 = ((bf16[8,2,448]{2,1,0:T(2,128)(2,1)}), bf16[8,2,448]{2,1,0:T(2,128)(2,1)S(1)}, u32[]{:S(2)}, u32[]{:S(2)}) async-start(bf16[8,2,448]{2,1,0:T(2,128)(2,1)} %reshape.301), calls=%async_computation.1 | async-start | bytes 32768 | tf_op jit(solution)/shard_map/all_to_all | solution.py:20
  97.5 9.2 %copy-start.10 = (bf16[8,2,448]{2,1,0:T(2,128)(2,1)}, bf16[8,2,448]{2,1,0:T(2,128)(2,1)S(1)}, u32[]{:S(2)}) copy-start(bf16[8,2,448]{2,1,0:T(2,128)(2,1)S(1)} %all-to-all-done.1) | copy-start | bytes 43012
  99.1 19.8 %all-to-all-start.3 = ((bf16[8,192,128]{2,1,0:T(8,128)(2,1)}), bf16[8,192,128]{2,1,0:T(8,128)(2,1)}, u32[]{:S(2)}, u32[]{:S(2)}) async-start(bf16[8,192,128]{2,1,0:T(8,128)(2,1)} %broadcast_in_dim.76), calls=%async_computation.3 | async-start | bytes 786432 | tf_op jit(solution)/shard_map/all_to_all | solution.py:20
  104.9 72.3 %all-gather.6.cloned.1.call-start = ((), (), s32[]{:S(2)}) async-start(), calls=%async_computation.10 | async-start | bytes 3538944 | tf_op jit(solution)/shard_map/all_gather | solution.py:131
  109.1 11.7 %copy-start.14 = (s32[96]{0:T(128)S(1)}, s32[96]{0:T(128)}, u32[]{:S(2)}) copy-start(s32[96]{0:T(128)} %param.11) | copy-start | bytes 1156
  109.1 34.1 %copy-start.15 = (s32[96]{0:T(128)S(1)}, s32[96]{0:T(128)}, u32[]{:S(2)}) copy-start(s32[96]{0:T(128)} %iota_add_fusion.1) | copy-start | bytes 1156
  113.0 0.6 copy-start.9
  128.0 11.2 %all-to-all-start.5 = ((f32[8,1,768]{2,1,0:T(1,128)}), f32[8,1,768]{2,1,0:T(1,128)S(1)}, u32[]{:S(2)}, u32[]{:S(2)}) async-start(f32[8,1,768]{2,1,0:T(1,128)} %broadcast_in_dim.79), calls=%async_computation.5 | async-start | bytes 49152 | tf_op jit(solution)/shard_map/all_to_all | solution.py:20
  139.8 11.5 %all-to-all-start.6 = ((f32[8,1,768]{2,1,0:T(1,128)}), f32[8,1,768]{2,1,0:T(1,128)S(1)}, u32[]{:S(2)}, u32[]{:S(2)}) async-start(f32[8,1,768]{2,1,0:T(1,128)} %broadcast_in_dim.80), calls=%async_computation.6 | async-start | bytes 49152 | tf_op jit(solution)/shard_map/all_to_all | solution.py:20
  152.0 8.8 %all-to-all-start.7 = ((f32[8,1,768]{2,1,0:T(1,128)}), f32[8,1,768]{2,1,0:T(1,128)S(1)}, u32[]{:S(2)}, u32[]{:S(2)}) async-start(f32[8,1,768]{2,1,0:T(1,128)} %broadcast_in_dim.81), calls=%async_computation.7 | async-start | bytes 49152 | tf_op jit(solution)/shard_map/all_to_all | solution.py:20
  164.2 4.4 %copy-start.5 = (f32[192,64]{1,0:T(8,128)S(1)}, f32[192,64]{1,0:T(8,128)}, u32[]{:S(2)}) copy-start(f32[192,64]{1,0:T(8,128)} %get-tuple-element.36) | copy-start | bytes 147460
  164.2 4.4 %copy-start.6 = (f32[192,64]{1,0:T(8,128)S(1)}, f32[192,64]{1,0:T(8,128)}, u32[]{:S(2)}) copy-start(f32[192,64]{1,0:T(8,128)} %get-tuple-element.37) | copy-start | bytes 147460
  164.2 13.0 %copy-start.1 = (pred[96,4864]{1,0:T(8,128)(4,1)S(1)}, pred[96,4864]{1,0:T(8,128)(4,1)}, u32[]{:S(2)}) copy-start(pred[96,4864]{1,0:T(8,128)(4,1)} %compare_and_fusion) | copy-start | bytes 1400836
  169.4 6.0 %collective-permute-start.2 = (bf16[96,256]{1,0:T(8,128)(2,1)S(1)}, bf16[96,256]{1,0:T(8,128)(2,1)S(1)}, u32[]{:S(2)}, u32[]{:S(2)}) collective-permute-start(bf16[96,256]{1,0:T(8,128)(2,1)S(1)} %bitcast.154), channel_id=1, source_target_pairs={{0,8},{8,0},{1,9},{9,1},{2,10},{10,2},{3,11},{11,3},{4,12},{12,4},... | collective-permute-start | bytes 147464 | tf_op jit(solution)/shard_map/ppermute | solution.py:174
  182.2 14.9 %copy-start.2 = (bf16[8,12288]{1,0:T(8,128)(2,1)S(1)}, bf16[8,12288]{1,0:T(8,128)(2,1)}, u32[]{:S(2)}) copy-start(bf16[8,12288]{1,0:T(8,128)(2,1)} %slice.108) | copy-start | bytes 589828
  186.5 23.2 %all-to-all-start.8 = ((f32[64,1,512]{2,1,0:T(1,128)}), f32[64,1,512]{2,1,0:T(1,128)S(1)}, u32[]{:S(2)}, u32[]{:S(2)}) async-start(f32[64,1,512]{2,1,0:T(1,128)} %broadcast_in_dim.83), calls=%async_computation.8 | async-start | bytes 262144 | tf_op jit(solution)/shard_map/all_to_all | solution.py:20
Sparse Core Ops, SparseCore 0:
  30.4 39.6 all-gather.3
  72.2 56.0 all-gather.7
  130.4 46.7 all-gather.5

commit v9 on v5

--- a/solution.py
+++ b/solution.py
@@ -23,10 +23,13 @@
     return exchange(jnp.broadcast_to(shard, (lax.axis_size(axis), *shard.shape)), axis)
 
 
+def by_parity(even, odd):
+    receiver = lax.broadcasted_iota(jnp.int32, (lax.axis_size(LINE), 1, 1), 0)
+    return jnp.where(receiver % 2 == 0, even[None], odd[None])
+
+
 def to_sides(even, odd):
-    halves = jnp.stack((even, odd))
-    sent = jnp.broadcast_to(halves, (lax.axis_size("z"), *halves.shape))
-    return exchange(sent.reshape(-1, *even.shape), LINE).reshape(-1, even.shape[1])
+    return exchange(by_parity(even, odd), LINE).reshape(-1, even.shape[1])
 
 
 def present(array):
@@ -96,9 +99,7 @@
     docs = jnp.broadcast_to(docs, (line, 1, heads_wide))
     peak_rows = peaks.shape[1]
     blank = jnp.zeros((line, 15 - peak_rows, heads_wide), jnp.bfloat16)
-    halves = jnp.stack((w_query[:, :half_query], w_query[:, half_query:]))
-    sent = jnp.broadcast_to(halves, (line // 2, *halves.shape))
-    sent = sent.reshape(line, row_count, heads_wide)
+    sent = by_parity(w_query[:, :half_query], w_query[:, half_query:])
     along_z = exchange(jnp.concatenate((sent, peaks, docs, blank), axis=1), LINE)
     gathered_query = lax.all_gather(
         along_z[:, :row_count].reshape(-1, heads_wide), "y", axis=0, tiled=True
@@ -187,7 +188,7 @@
     )
     scores = jnp.where(allowed, scores, -1e30)
     highest = jnp.max(scores, axis=3, keepdims=True)
-    weights = jnp.where(allowed, jnp.exp(scores - highest), 0.0)
+    weights = jnp.exp(scores - highest)
     totals = jnp.sum(weights, axis=3)
     accumulated = jnp.einsum(
         "kgts,skd->kgtd",

time: 217 us -> 217 us (level)
  transfers between devices with their start and end apart: 14 -> 14, of which waited for: 10 -> 10; matrix products, arithmetic and copies ran while one was open for 23% -> 24% of each run, Pallas kernels for 0% -> 0%
where the time goes in v9:
time: 217 us; the launch traced here: 215 us
  waiting for transfers between devices  64.3 us (30%)
  starting transfers between devices  52.1 us (24%)
  other arithmetic  24.4 us (11%)
  local copies, waits for them, and re-layouts  23.4 us (11%)
  blocking collectives  22.1 us (10%)
  between operations  16.3 us (8%)
  matrix products  12.5 us (6%)
    all_to_all x8, waiting for transfers between devices, exchange(): return lax.all_to_all(parts, axis, split_axis=0, concat_axis=0, tiled=True)  52.4 us
    all_to_all x8, starting transfers between devices, exchange(): return lax.all_to_all(parts, axis, split_axis=0, concat_axis=0, tiled=True)  43.7 us
    all_to_all x1, blocking collectives, exchange(): return lax.all_to_all(parts, axis, split_axis=0, concat_axis=0, tiled=True)  22.1 us
    unnamed x49, local copies, waits for them, and re-layouts  11.6 us
    all_gather x1, waiting for transfers between devices, on_device(): everything = lax.all_gather(sent_y, 'y', axis=0, tiled=True)  6.47 us
    select_n x2, other arithmetic, in_pair_order(): jnp.where(even, own, other)  4.6 us
  transfers between devices with their start and end apart: 14, of which 10 were waited for; matrix products, arithmetic and copies ran while one was open for 24% of the time, Pallas kernels for 0%

profile of v9, /device:TPU:2, one launch (start us, length us, event | category | flops | bytes accessed | tf_op | source)
XLA Modules:
  0.0 215.1 jit_solution(1245934125846843113)
XLA Ops:
  7.3 1.0 broadcast_select_fusion.7
  8.2 22.1 %all_to_all.63 = bf16[8,128,128]{2,1,0:T(8,128)(2,1)} all-to-all(bf16[8,128,128]{2,1,0:T(8,128)(2,1)S(1)} %broadcast_select_fusion.7), channel_id=1, replica_groups=mesh['y'=8,'z'=4,'pair'=2,'x'=4,'core'=2] {'z','pair'}, dimensions={0} | all-to-all | bytes 524288 | tf_op jit(solution)/shard_map/all_to_all | solution.py:19
  30.4 1.8 fusion.6
  32.2 1.3 abs_reduce_fusion
  33.9 1.0 maximum_maximum_fusion
  34.8 3.5 %all-to-all-start = ((bf16[8,144,256]{2,1,0:T(8,128)(2,1)}), bf16[8,144,256]{2,1,0:T(8,128)(2,1)S(1)}, u32[]{:S(2)}, u32[]{:S(2)}) async-start(bf16[8,144,256]{2,1,0:T(8,128)(2,1)} %maximum_maximum_fusion), calls=%async_computation | async-start | bytes 1179648 | tf_op jit(solution)/shard_map/all_to_all | solution.py:19
  38.5 3.8 %collective-permute-start = (bf16[96,4096]{1,0:T(8,128)(2,1)S(1)}, bf16[96,4096]{1,0:T(8,128)(2,1)}, u32[]{:S(2)}, u32[]{:S(2)}) collective-permute-start(bf16[96,4096]{1,0:T(8,128)(2,1)S(1)} %constant_dynamic-slice_fusion), channel_id=1, source_target_pairs={{0,8},{8,0},{1,9},{9,1},{2,10},{10,2},{3,11},{11,3},{4,12},{12,4},... | collective-permute-start | bytes 2359304 | tf_op jit(solution)/shard_map/ppermute | solution.py:92
  43.2 13.9 %all-to-all-done = bf16[8,144,256]{2,1,0:T(8,128)(2,1)S(1)} async-done(((bf16[8,144,256]{2,1,0:T(8,128)(2,1)}), bf16[8,144,256]{2,1,0:T(8,128)(2,1)S(1)}, u32[]{:S(2)}, u32[]{:S(2)}) %all-to-all-start) | async-done | bytes 589856 | tf_op jit(solution)/shard_map/all_to_all | solution.py:19
  57.2 0.8 slice.99
  58.0 0.8 maximum_bitcast_fusion
  60.1 0.9 reshape.309
  61.0 4.8 %all-to-all-start.4 = ((bf16[8,2,6208]{2,1,0:T(2,128)(2,1)}), bf16[8,2,6208]{2,1,0:T(2,128)(2,1)}, u32[]{:S(2)}, u32[]{:S(2)}) async-start(bf16[8,2,6208]{2,1,0:T(2,128)(2,1)} %reshape.309), calls=%async_computation.4 | async-start | bytes 401408 | tf_op jit(solution)/shard_map/all_to_all | solution.py:19
  65.8 3.1 %collective-permute-done = bf16[96,4096]{1,0:T(8,128)(2,1)} collective-permute-done((bf16[96,4096]{1,0:T(8,128)(2,1)S(1)}, bf16[96,4096]{1,0:T(8,128)(2,1)}, u32[]{:S(2)}, u32[]{:S(2)}) %collective-permute-start) | collective-permute-done | bytes 786464 | tf_op jit(solution)/shard_map/ppermute | solution.py:92
  68.9 1.9 collective-permute-start.1
  74.6 1.5 broadcast_select_fusion.5
  76.1 2.3 %broadcast_select_fusion.3 = (bf16[96,8192]{1,0:T(8,128)(2,1)}, bf16[96,8192]{1,0:T(8,128)(2,1)}) fusion(bf16[96,8192]{1,0:T(8,128)(2,1)S(1)} %get-tuple-element.15, pred[]{:T(512)S(6)} %and.32, bf16[96,4096]{1,0:T(8,128)(2,1)S(1)} %get-tuple-element.21, bf16[96,4096]{1,0:T(8,128)(2,1)S(1)} %get-tuple-element.20), kind=kLoop, calls=%fused_computation.29 | loop fusion | flops 4718592 | bytes 6291457 | tf_op jit(solution)/shard_map/jit(_where)/select_n | solution.py:42
  78.4 3.5 %fusion.9 = f32[192,128]{1,0:T(8,128)S(1)} fusion(bf16[8192,128]{1,0:T(8,128)(2,1)} %all-gather.4.cloned.1.call-done, bf16[96,8192]{1,0:T(8,128)(2,1)} %get-tuple-element.19, bf16[96,8192]{1,0:T(8,128)(2,1)} %get-tuple-element.18), kind=kOutput, calls=%fused_computation.12 | convolution fusion | flops 408944640 | bytes 5341184 | tf_op jit(solution)/shard_map/dot_general | solution.py:123
  82.4 7.1 %all-to-all-start.1 = ((bf16[8,2,448]{2,1,0:T(2,128)(2,1)}), bf16[8,2,448]{2,1,0:T(2,128)(2,1)S(1)}, u32[]{:S(2)}, u32[]{:S(2)}) async-start(bf16[8,2,448]{2,1,0:T(2,128)(2,1)} %reshape.307), calls=%async_computation.1 | async-start | bytes 32768 | tf_op jit(solution)/shard_map/all_to_all | solution.py:19
  90.2 7.4 %all-to-all-done.1 = bf16[8,2,448]{2,1,0:T(2,128)(2,1)S(1)} async-done(((bf16[8,2,448]{2,1,0:T(2,128)(2,1)}), bf16[8,2,448]{2,1,0:T(2,128)(2,1)S(1)}, u32[]{:S(2)}, u32[]{:S(2)}) %all-to-all-start.1) | async-done | bytes 14368 | tf_op jit(solution)/shard_map/all_to_all | solution.py:19
  97.6 1.6 broadcast_in_dim.125
  99.2 5.8 %all-to-all-start.3 = ((bf16[8,192,128]{2,1,0:T(8,128)(2,1)}), bf16[8,192,128]{2,1,0:T(8,128)(2,1)}, u32[]{:S(2)}, u32[]{:S(2)}) async-start(bf16[8,192,128]{2,1,0:T(8,128)(2,1)} %broadcast_in_dim.125), calls=%async_computation.3 | async-start | bytes 786432 | tf_op jit(solution)/shard_map/all_to_all | solution.py:19
  105.1 1.8 multiply_cosine_fusion
  106.9 2.3 %reshape.310 = bf16[8,1,12416]{2,1,0:T(2,128)(2,1)} reshape(bf16[8,2,6208]{2,1,0:T(2,128)(2,1)} %all-to-all-done.4) | data formatting | bytes 397312
  109.2 1.1 copy.72
  110.9 1.4 reshape.308
  113.8 5.2 %all-to-all-done.3 = bf16[8,192,128]{2,1,0:T(8,128)(2,1)} async-done(((bf16[8,192,128]{2,1,0:T(8,128)(2,1)}), bf16[8,192,128]{2,1,0:T(8,128)(2,1)}, u32[]{:S(2)}, u32[]{:S(2)}) %all-to-all-start.3) | async-done | bytes 393248 | tf_op jit(solution)/shard_map/all_to_all | solution.py:19
  119.0 1.2 slice.95
  120.9 1.1 fusion.42
  121.9 0.8 pad_maximum_fusion.1
  123.4 3.3 %all-to-all-start.5 = ((f32[8,1,768]{2,1,0:T(1,128)}), f32[8,1,768]{2,1,0:T(1,128)S(1)}, u32[]{:S(2)}, u32[]{:S(2)}) async-start(f32[8,1,768]{2,1,0:T(1,128)} %broadcast_in_dim.128), calls=%async_computation.5 | async-start | bytes 49152 | tf_op jit(solution)/shard_map/all_to_all | solution.py:19
  127.5 7.1 %all-to-all-done.5 = f32[8,1,768]{2,1,0:T(1,128)S(1)} async-done(((f32[8,1,768]{2,1,0:T(1,128)}), f32[8,1,768]{2,1,0:T(1,128)S(1)}, u32[]{:S(2)}, u32[]{:S(2)}) %all-to-all-start.5) | async-done | bytes 24608 | tf_op jit(solution)/shard_map/all_to_all | solution.py:19
  135.2 3.3 %all-to-all-start.6 = ((f32[8,1,768]{2,1,0:T(1,128)}), f32[8,1,768]{2,1,0:T(1,128)S(1)}, u32[]{:S(2)}, u32[]{:S(2)}) async-start(f32[8,1,768]{2,1,0:T(1,128)} %broadcast_in_dim.129), calls=%async_computation.6 | async-start | bytes 49152 | tf_op jit(solution)/shard_map/all_to_all | solution.py:19
  138.6 1.4 fusion.17
  140.0 6.5 %all-to-all-done.6 = f32[8,1,768]{2,1,0:T(1,128)S(1)} async-done(((f32[8,1,768]{2,1,0:T(1,128)}), f32[8,1,768]{2,1,0:T(1,128)S(1)}, u32[]{:S(2)}, u32[]{:S(2)}) %all-to-all-start.6) | async-done | bytes 24608 | tf_op jit(solution)/shard_map/all_to_all | solution.py:19
  147.1 4.8 %all-to-all-start.7 = ((f32[8,1,768]{2,1,0:T(1,128)}), f32[8,1,768]{2,1,0:T(1,128)S(1)}, u32[]{:S(2)}, u32[]{:S(2)}) async-start(f32[8,1,768]{2,1,0:T(1,128)} %broadcast_in_dim.130), calls=%async_computation.7 | async-start | bytes 49152 | tf_op jit(solution)/shard_map/all_to_all | solution.py:19
  151.9 1.3 dynamic-slice_divide_fusion
  153.2 2.7 %all-to-all-done.7 = f32[8,1,768]{2,1,0:T(1,128)S(1)} async-done(((f32[8,1,768]{2,1,0:T(1,128)}), f32[8,1,768]{2,1,0:T(1,128)S(1)}, u32[]{:S(2)}, u32[]{:S(2)}) %all-to-all-start.7) | async-done | bytes 24608 | tf_op jit(solution)/shard_map/all_to_all | solution.py:19
  157.1 2.3 %broadcast_select_fusion.1 = (bf16[96,8192]{1,0:T(8,128)(2,1)}, bf16[96,8192]{1,0:T(8,128)(2,1)}) fusion(bf16[96,8192]{1,0:T(8,128)(2,1)S(1)} %get-tuple-element.15, pred[]{:T(512)S(6)} %and.33, bf16[96,4096]{1,0:T(8,128)(2,1)S(1)} %get-tuple-element.21, bf16[96,4096]{1,0:T(8,128)(2,1)S(1)} %get-tuple-element.20), kind=kLoop, calls=%fused_computation.27 | loop fusion | flops 4718592 | bytes 6291457 | tf_op jit(solution)/shard_map/jit(_where)/select_n | solution.py:42
  159.4 4.3 %fusion.13 = f32[192,256]{1,0:T(8,128)S(1)} fusion(bf16[8192,256]{1,0:T(8,128)(2,1)} %all-gather.8.cloned.1.call-done, bf16[96,8192]{1,0:T(8,128)(2,1)} %get-tuple-element.17, bf16[96,8192]{1,0:T(8,128)(2,1)} %get-tuple-element.16), kind=kOutput, calls=%fused_computation.16 | convolution fusion | flops 811597824 | bytes 7536640 | tf_op jit(solution)/shard_map/dot_general | solution.py:171
  164.5 2.6 %collective-permute-start.2 = (bf16[96,256]{1,0:T(8,128)(2,1)S(1)}, bf16[96,256]{1,0:T(8,128)(2,1)S(1)}, u32[]{:S(2)}, u32[]{:S(2)}) collective-permute-start(bf16[96,256]{1,0:T(8,128)(2,1)S(1)} %bitcast.139), channel_id=1, source_target_pairs={{0,8},{8,0},{1,9},{9,1},{2,10},{10,2},{3,11},{11,3},{4,12},{12,4},... | collective-permute-start | bytes 147464 | tf_op jit(solution)/shard_map/ppermute | solution.py:175
  168.2 2.3 %collective-permute-done.2 = bf16[96,256]{1,0:T(8,128)(2,1)S(1)} collective-permute-done((bf16[96,256]{1,0:T(8,128)(2,1)S(1)}, bf16[96,256]{1,0:T(8,128)(2,1)S(1)}, u32[]{:S(2)}, u32[]{:S(2)}) %collective-permute-start.2) | collective-permute-done | bytes 49184 | tf_op jit(solution)/shard_map/ppermute | solution.py:175
  170.5 6.5 %all-gather.6.cloned.1.call-done = bf16[6144,256]{1,0:T(8,128)(2,1)} async-done(((bf16[768,256]{1,0:T(8,128)(2,1)}), bf16[6144,256]{1,0:T(8,128)(2,1)}) %all-gather.6.cloned.1.call-update) | async-done | bytes 3145744 | tf_op jit(solution)/shard_map/all_gather | solution.py:131
  177.0 3.3 %fusion.45 = (f32[4,96]{1,0:T(4,128)S(1)}, f32[1,4,96,6144]{3,2,1,0:T(8,128)S(1)}) fusion(bf16[6144,256]{1,0:T(8,128)(2,1)} %all-gather.6.cloned.1.call-done, pred[96,6144]{1,0:T(8,128)(4,1)S(1)} %copy-done.3, bf16[96,256]{1,0:T(8,128)(2,1)S(1)} %get-tuple-element.33, bf16[96,256]{1,0:T(8,128)(2,1)S(1)} %get-tuple-element.32), kind=kOutput, calls=%fused_computation.104 | convolution fusion | flops 611253888 | bytes 11699712 | tf_op jit(solution)/shard_map/tkgd,skd->kgts/dot_general | solution.py:181
  180.3 1.4 fusion
  182.2 1.4 abs_reduce_fusion.3
  184.4 10.9 %all-to-all-start.8 = ((f32[64,1,512]{2,1,0:T(1,128)}), f32[64,1,512]{2,1,0:T(1,128)S(1)}, u32[]{:S(2)}, u32[]{:S(2)}) async-start(f32[64,1,512]{2,1,0:T(1,128)} %broadcast_in_dim.132), calls=%async_computation.8 | async-start | bytes 262144 | tf_op jit(solution)/shard_map/all_to_all | solution.py:19
  195.4 0.9 copy.54
  198.3 9.6 %all-to-all-done.8 = f32[64,1,512]{2,1,0:T(1,128)S(1)} async-done(((f32[64,1,512]{2,1,0:T(1,128)}), f32[64,1,512]{2,1,0:T(1,128)S(1)}, u32[]{:S(2)}, u32[]{:S(2)}) %all-to-all-start.8) | async-done | bytes 131104 | tf_op jit(solution)/shard_map/all_to_all | solution.py:19
  (113 shorter events, 18.2 us)
Async XLA Ops:
  7.2 25.0 %copy-start = (bf16[96,8192]{1,0:T(8,128)(2,1)S(1)}, bf16[96,8192]{1,0:T(8,128)(2,1)}, u32[]{:S(2)}) copy-start(bf16[96,8192]{1,0:T(8,128)(2,1)} %param.6) | copy-start | bytes 4718596
  7.2 26.4 %copy-start.14 = (s32[96]{0:T(128)S(1)}, s32[96]{0:T(128)}, u32[]{:S(2)}) copy-start(s32[96]{0:T(128)} %param.11) | copy-start | bytes 1156
  7.2 26.5 %copy-start.4 = (bf16[128,512]{1,0:T(8,128)(2,1)S(1)}, bf16[128,512]{1,0:T(8,128)(2,1)}, u32[]{:S(2)}) copy-start(bf16[128,512]{1,0:T(8,128)(2,1)} %param.8) | copy-start | bytes 393220
  7.2 71.1 %all-gather.4.cloned.1.call-start = ((), (), s32[]{:S(2)}) async-start(), calls=%async_computation.9 | async-start | bytes 2359296 | tf_op jit(solution)/shard_map/all_gather | solution.py:84
  33.5 8.8 %copy-start.5 = (bf16[128,512]{1,0:T(8,128)(2,1)S(1)}, bf16[128,512]{1,0:T(8,128)(2,1)}, u32[]{:S(2)}) copy-start(bf16[128,512]{1,0:T(8,128)(2,1)} %param.8) | copy-start | bytes 393220
  33.5 8.8 %copy-start.8 = (bf16[128,128]{1,0:T(8,128)(2,1)S(1)}, bf16[128,128]{1,0:T(8,128)(2,1)}, u32[]{:S(2)}) copy-start(bf16[128,128]{1,0:T(8,128)(2,1)} %param.9) | copy-start | bytes 98308
  33.5 8.8 %copy-start.9 = (bf16[128,128]{1,0:T(8,128)(2,1)S(1)}, bf16[128,128]{1,0:T(8,128)(2,1)}, u32[]{:S(2)}) copy-start(bf16[128,128]{1,0:T(8,128)(2,1)} %param.10) | copy-start | bytes 98308
  34.8 22.3 %all-to-all-start = ((bf16[8,144,256]{2,1,0:T(8,128)(2,1)}), bf16[8,144,256]{2,1,0:T(8,128)(2,1)S(1)}, u32[]{:S(2)}, u32[]{:S(2)}) async-start(bf16[8,144,256]{2,1,0:T(8,128)(2,1)} %maximum_maximum_fusion), calls=%async_computation | async-start | bytes 1179648 | tf_op jit(solution)/shard_map/all_to_all | solution.py:19
  38.4 121.0 %all-gather.8.cloned.1.call-start = ((), (), s32[]{:S(2)}) async-start(), calls=%async_computation.11 | async-start | bytes 4718592 | tf_op jit(solution)/shard_map/all_gather | solution.py:104
  38.5 30.3 %collective-permute-start = (bf16[96,4096]{1,0:T(8,128)(2,1)S(1)}, bf16[96,4096]{1,0:T(8,128)(2,1)}, u32[]{:S(2)}, u32[]{:S(2)}) collective-permute-start(bf16[96,4096]{1,0:T(8,128)(2,1)S(1)} %constant_dynamic-slice_fusion), channel_id=1, source_target_pairs={{0,8},{8,0},{1,9},{9,1},{2,10},{10,2},{3,11},{11,3},{4,12},{12,4},... | collective-permute-start | bytes 2359304 | tf_op jit(solution)/shard_map/ppermute | solution.py:92
  61.0 21.4 %all-to-all-start.4 = ((bf16[8,2,6208]{2,1,0:T(2,128)(2,1)}), bf16[8,2,6208]{2,1,0:T(2,128)(2,1)}, u32[]{:S(2)}, u32[]{:S(2)}) async-start(bf16[8,2,6208]{2,1,0:T(2,128)(2,1)} %reshape.309), calls=%async_computation.4 | async-start | bytes 401408 | tf_op jit(solution)/shard_map/all_to_all | solution.py:19
  68.9 5.7 %collective-permute-start.1 = (bf16[96,4096]{1,0:T(8,128)(2,1)}, bf16[96,4096]{1,0:T(8,128)(2,1)}, u32[]{:S(2)}, u32[]{:S(2)}) collective-permute-start(bf16[96,4096]{1,0:T(8,128)(2,1)} %collective-permute-done), channel_id=1, source_target_pairs={{0,1},{1,0},{2,3},{3,2},{4,5},{5,4},{6,7},{7,6},{8,9},{9,8},{10,11... | collective-permute-start | bytes 2359304 | tf_op jit(solution)/shard_map/ppermute | solution.py:114
  70.8 11.1 %copy-start.13 = (f32[64]{0:T(128)}, f32[64]{0:T(128)S(1)}, u32[]{:S(2)}) copy-start(f32[64]{0:T(128)S(1)} %multiply_exponential_fusion) | copy-start | bytes 772
  71.3 10.6 %copy-start.12 = (f32[192]{0:T(256)}, f32[192]{0:T(256)S(1)}, u32[]{:S(2)}) copy-start(f32[192]{0:T(256)S(1)} %add_convert_fusion.1) | copy-start | bytes 2308
  82.4 15.3 %all-to-all-start.1 = ((bf16[8,2,448]{2,1,0:T(2,128)(2,1)}), bf16[8,2,448]{2,1,0:T(2,128)(2,1)S(1)}, u32[]{:S(2)}, u32[]{:S(2)}) async-start(bf16[8,2,448]{2,1,0:T(2,128)(2,1)} %reshape.307), calls=%async_computation.1 | async-start | bytes 32768 | tf_op jit(solution)/shard_map/all_to_all | solution.py:19
  97.6 9.2 %copy-start.10 = (bf16[8,2,448]{2,1,0:T(2,128)(2,1)}, bf16[8,2,448]{2,1,0:T(2,128)(2,1)S(1)}, u32[]{:S(2)}) copy-start(bf16[8,2,448]{2,1,0:T(2,128)(2,1)S(1)} %all-to-all-done.1) | copy-start | bytes 43012
  99.2 19.8 %all-to-all-start.3 = ((bf16[8,192,128]{2,1,0:T(8,128)(2,1)}), bf16[8,192,128]{2,1,0:T(8,128)(2,1)}, u32[]{:S(2)}, u32[]{:S(2)}) async-start(bf16[8,192,128]{2,1,0:T(8,128)(2,1)} %broadcast_in_dim.125), calls=%async_computation.3 | async-start | bytes 786432 | tf_op jit(solution)/shard_map/all_to_all | solution.py:19
  105.0 72.0 %all-gather.6.cloned.1.call-start = ((), (), s32[]{:S(2)}) async-start(), calls=%async_computation.10 | async-start | bytes 3538944 | tf_op jit(solution)/shard_map/all_gather | solution.py:131
  109.2 29.4 %copy-start.15 = (s32[96]{0:T(128)S(1)}, s32[96]{0:T(128)}, u32[]{:S(2)}) copy-start(s32[96]{0:T(128)} %param.11) | copy-start | bytes 1156
  109.2 29.4 %copy-start.16 = (s32[96]{0:T(128)S(1)}, s32[96]{0:T(128)}, u32[]{:S(2)}) copy-start(s32[96]{0:T(128)} %iota_add_fusion) | copy-start | bytes 1156
  113.1 0.6 copy-start.11
  123.4 11.2 %all-to-all-start.5 = ((f32[8,1,768]{2,1,0:T(1,128)}), f32[8,1,768]{2,1,0:T(1,128)S(1)}, u32[]{:S(2)}, u32[]{:S(2)}) async-start(f32[8,1,768]{2,1,0:T(1,128)} %broadcast_in_dim.128), calls=%async_computation.5 | async-start | bytes 49152 | tf_op jit(solution)/shard_map/all_to_all | solution.py:19
  135.2 11.2 %all-to-all-start.6 = ((f32[8,1,768]{2,1,0:T(1,128)}), f32[8,1,768]{2,1,0:T(1,128)S(1)}, u32[]{:S(2)}, u32[]{:S(2)}) async-start(f32[8,1,768]{2,1,0:T(1,128)} %broadcast_in_dim.129), calls=%async_computation.6 | async-start | bytes 49152 | tf_op jit(solution)/shard_map/all_to_all | solution.py:19
  147.1 8.8 %all-to-all-start.7 = ((f32[8,1,768]{2,1,0:T(1,128)}), f32[8,1,768]{2,1,0:T(1,128)S(1)}, u32[]{:S(2)}, u32[]{:S(2)}) async-start(f32[8,1,768]{2,1,0:T(1,128)} %broadcast_in_dim.130), calls=%async_computation.7 | async-start | bytes 49152 | tf_op jit(solution)/shard_map/all_to_all | solution.py:19
  159.4 4.4 %copy-start.6 = (f32[192,64]{1,0:T(8,128)S(1)}, f32[192,64]{1,0:T(8,128)}, u32[]{:S(2)}) copy-start(f32[192,64]{1,0:T(8,128)} %get-tuple-element.36) | copy-start | bytes 147460
  159.4 4.4 %copy-start.7 = (f32[192,64]{1,0:T(8,128)S(1)}, f32[192,64]{1,0:T(8,128)}, u32[]{:S(2)}) copy-start(f32[192,64]{1,0:T(8,128)} %get-tuple-element.37) | copy-start | bytes 147460
  159.4 17.6 %copy-start.3 = (pred[96,6144]{1,0:T(8,128)(4,1)S(1)}, pred[96,6144]{1,0:T(8,128)(4,1)}, u32[]{:S(2)}) copy-start(pred[96,6144]{1,0:T(8,128)(4,1)} %fusion.17) | copy-start | bytes 1769476
  164.5 6.0 %collective-permute-start.2 = (bf16[96,256]{1,0:T(8,128)(2,1)S(1)}, bf16[96,256]{1,0:T(8,128)(2,1)S(1)}, u32[]{:S(2)}, u32[]{:S(2)}) collective-permute-start(bf16[96,256]{1,0:T(8,128)(2,1)S(1)} %bitcast.139), channel_id=1, source_target_pairs={{0,8},{8,0},{1,9},{9,1},{2,10},{10,2},{3,11},{11,3},{4,12},{12,4},... | collective-permute-start | bytes 147464 | tf_op jit(solution)/shard_map/ppermute | solution.py:175
  180.3 1.9 copy-start.2
  182.2 13.1 %copy-start.1 = (bf16[8,12288]{1,0:T(8,128)(2,1)S(1)}, bf16[8,12288]{1,0:T(8,128)(2,1)}, u32[]{:S(2)}) copy-start(bf16[8,12288]{1,0:T(8,128)(2,1)} %slice.104) | copy-start | bytes 589828
  184.4 23.5 %all-to-all-start.8 = ((f32[64,1,512]{2,1,0:T(1,128)}), f32[64,1,512]{2,1,0:T(1,128)S(1)}, u32[]{:S(2)}, u32[]{:S(2)}) async-start(f32[64,1,512]{2,1,0:T(1,128)} %broadcast_in_dim.132), calls=%async_computation.8 | async-start | bytes 262144 | tf_op jit(solution)/shard_map/all_to_all | solution.py:19
Sparse Core Ops, SparseCore 0:
  30.5 39.6 all-gather.3
  72.2 56.0 all-gather.7
  130.4 46.5 all-gather.5

commit v10 on v9

--- a/solution.py
+++ b/solution.py
@@ -180,7 +180,7 @@
     length = key_block.shape[0]
     scores = jnp.einsum(
         "tkgd,skd->kgts", query, key_block[:, None, :], preferred_element_type=jnp.float32
-    ) * (1.0 / math.sqrt(HEAD))
+    )
     query_positions = tok_index * tok_dev + jnp.arange(tok_dev, dtype=jnp.int32)
     key_positions = jnp.arange(length, dtype=jnp.int32)
     allowed = (doc_ids[:, None] == doc_block[None, :]) & (
@@ -188,7 +188,7 @@
     )
     scores = jnp.where(allowed, scores, -1e30)
     highest = jnp.max(scores, axis=3, keepdims=True)
-    weights = jnp.exp(scores - highest)
+    weights = jnp.exp((scores - highest) * (1.0 / math.sqrt(HEAD)))
     totals = jnp.sum(weights, axis=3)
     accumulated = jnp.einsum(
         "kgts,skd->kgtd",

time: 217 us -> 216 us (level)
  no operation moved by 1% of the time
where the time goes in v10:
time: 216 us; the launch traced here: 215 us
  waiting for transfers between devices  64.3 us (30%)
  starting transfers between devices  52.1 us (24%)
  other arithmetic  24.7 us (11%)
  local copies, waits for them, and re-layouts  23.2 us (11%)
  blocking collectives  22.1 us (10%)
  between operations  16.3 us (8%)
  matrix products  12.3 us (6%)
    all_to_all x8, waiting for transfers between devices, exchange(): return lax.all_to_all(parts, axis, split_axis=0, concat_axis=0, tiled=True)  52.4 us
    all_to_all x8, starting transfers between devices, exchange(): return lax.all_to_all(parts, axis, split_axis=0, concat_axis=0, tiled=True)  43.7 us
    all_to_all x1, blocking collectives, exchange(): return lax.all_to_all(parts, axis, split_axis=0, concat_axis=0, tiled=True)  22.1 us
    unnamed x49, local copies, waits for them, and re-layouts  11.3 us
    all_gather x1, waiting for transfers between devices, on_device(): everything = lax.all_gather(sent_y, 'y', axis=0, tiled=True)  6.47 us
    select_n x2, other arithmetic, in_pair_order(): jnp.where(even, own, other)  4.6 us
  transfers between devices with their start and end apart: 14, of which 10 were waited for; matrix products, arithmetic and copies ran while one was open for 24% of the time, Pallas kernels for 0%

profile of v10, /device:TPU:2, one launch (start us, length us, event | category | flops | bytes accessed | tf_op | source)
XLA Modules:
  0.0 214.9 jit_solution(16683080491729649125)
XLA Ops:
  7.3 1.0 broadcast_select_fusion.7
  8.2 22.1 %all_to_all.63 = bf16[8,128,128]{2,1,0:T(8,128)(2,1)} all-to-all(bf16[8,128,128]{2,1,0:T(8,128)(2,1)S(1)} %broadcast_select_fusion.7), channel_id=1, replica_groups=mesh['y'=8,'z'=4,'pair'=2,'x'=4,'core'=2] {'z','pair'}, dimensions={0} | all-to-all | bytes 524288 | tf_op jit(solution)/shard_map/all_to_all | solution.py:19
  30.4 1.8 fusion.7
  32.2 1.3 abs_reduce_fusion
  33.9 1.0 maximum_maximum_fusion
  34.8 3.5 %all-to-all-start = ((bf16[8,144,256]{2,1,0:T(8,128)(2,1)}), bf16[8,144,256]{2,1,0:T(8,128)(2,1)S(1)}, u32[]{:S(2)}, u32[]{:S(2)}) async-start(bf16[8,144,256]{2,1,0:T(8,128)(2,1)} %maximum_maximum_fusion), calls=%async_computation | async-start | bytes 1179648 | tf_op jit(solution)/shard_map/all_to_all | solution.py:19
  38.5 3.8 %collective-permute-start = (bf16[96,4096]{1,0:T(8,128)(2,1)S(1)}, bf16[96,4096]{1,0:T(8,128)(2,1)}, u32[]{:S(2)}, u32[]{:S(2)}) collective-permute-start(bf16[96,4096]{1,0:T(8,128)(2,1)S(1)} %constant_dynamic-slice_fusion), channel_id=1, source_target_pairs={{0,8},{8,0},{1,9},{9,1},{2,10},{10,2},{3,11},{11,3},{4,12},{12,4},... | collective-permute-start | bytes 2359304 | tf_op jit(solution)/shard_map/ppermute | solution.py:92
  43.2 13.9 %all-to-all-done = bf16[8,144,256]{2,1,0:T(8,128)(2,1)S(1)} async-done(((bf16[8,144,256]{2,1,0:T(8,128)(2,1)}), bf16[8,144,256]{2,1,0:T(8,128)(2,1)S(1)}, u32[]{:S(2)}, u32[]{:S(2)}) %all-to-all-start) | async-done | bytes 589856 | tf_op jit(solution)/shard_map/all_to_all | solution.py:19
  57.2 0.8 slice.99
  58.0 0.8 maximum_bitcast_fusion
  60.1 0.9 reshape.307
  61.0 4.8 %all-to-all-start.4 = ((bf16[8,2,6208]{2,1,0:T(2,128)(2,1)}), bf16[8,2,6208]{2,1,0:T(2,128)(2,1)}, u32[]{:S(2)}, u32[]{:S(2)}) async-start(bf16[8,2,6208]{2,1,0:T(2,128)(2,1)} %reshape.307), calls=%async_computation.4 | async-start | bytes 401408 | tf_op jit(solution)/shard_map/all_to_all | solution.py:19
  65.8 3.1 %collective-permute-done = bf16[96,4096]{1,0:T(8,128)(2,1)} collective-permute-done((bf16[96,4096]{1,0:T(8,128)(2,1)S(1)}, bf16[96,4096]{1,0:T(8,128)(2,1)}, u32[]{:S(2)}, u32[]{:S(2)}) %collective-permute-start) | collective-permute-done | bytes 786464 | tf_op jit(solution)/shard_map/ppermute | solution.py:92
  68.9 1.9 collective-permute-start.1
  74.6 1.5 broadcast_select_fusion.5
  76.1 2.3 %broadcast_select_fusion.3 = (bf16[96,8192]{1,0:T(8,128)(2,1)}, bf16[96,8192]{1,0:T(8,128)(2,1)}) fusion(bf16[96,8192]{1,0:T(8,128)(2,1)S(1)} %get-tuple-element.15, pred[]{:T(512)S(6)} %and.32, bf16[96,4096]{1,0:T(8,128)(2,1)S(1)} %get-tuple-element.21, bf16[96,4096]{1,0:T(8,128)(2,1)S(1)} %get-tuple-element.20), kind=kLoop, calls=%fused_computation.30 | loop fusion | flops 4718592 | bytes 6291457 | tf_op jit(solution)/shard_map/jit(_where)/select_n | solution.py:42
  78.4 3.5 %fusion.10 = f32[192,128]{1,0:T(8,128)S(1)} fusion(bf16[8192,128]{1,0:T(8,128)(2,1)} %all-gather.4.cloned.1.call-done, bf16[96,8192]{1,0:T(8,128)(2,1)} %get-tuple-element.19, bf16[96,8192]{1,0:T(8,128)(2,1)} %get-tuple-element.18), kind=kOutput, calls=%fused_computation.13 | convolution fusion | flops 408944640 | bytes 5341184 | tf_op jit(solution)/shard_map/dot_general | solution.py:123
  82.4 7.1 %all-to-all-start.1 = ((bf16[8,2,448]{2,1,0:T(2,128)(2,1)}), bf16[8,2,448]{2,1,0:T(2,128)(2,1)S(1)}, u32[]{:S(2)}, u32[]{:S(2)}) async-start(bf16[8,2,448]{2,1,0:T(2,128)(2,1)} %reshape.305), calls=%async_computation.1 | async-start | bytes 32768 | tf_op jit(solution)/shard_map/all_to_all | solution.py:19
  90.2 7.4 %all-to-all-done.1 = bf16[8,2,448]{2,1,0:T(2,128)(2,1)S(1)} async-done(((bf16[8,2,448]{2,1,0:T(2,128)(2,1)}), bf16[8,2,448]{2,1,0:T(2,128)(2,1)S(1)}, u32[]{:S(2)}, u32[]{:S(2)}) %all-to-all-start.1) | async-done | bytes 14368 | tf_op jit(solution)/shard_map/all_to_all | solution.py:19
  97.6 1.6 broadcast_in_dim.125
  99.2 5.8 %all-to-all-start.3 = ((bf16[8,192,128]{2,1,0:T(8,128)(2,1)}), bf16[8,192,128]{2,1,0:T(8,128)(2,1)}, u32[]{:S(2)}, u32[]{:S(2)}) async-start(bf16[8,192,128]{2,1,0:T(8,128)(2,1)} %broadcast_in_dim.125), calls=%async_computation.3 | async-start | bytes 786432 | tf_op jit(solution)/shard_map/all_to_all | solution.py:19
  105.1 1.8 multiply_cosine_fusion
  106.9 2.3 %reshape.308 = bf16[8,1,12416]{2,1,0:T(2,128)(2,1)} reshape(bf16[8,2,6208]{2,1,0:T(2,128)(2,1)} %all-to-all-done.4) | data formatting | bytes 397312
  109.2 1.1 copy.72
  110.9 1.4 reshape.306
  113.8 5.2 %all-to-all-done.3 = bf16[8,192,128]{2,1,0:T(8,128)(2,1)} async-done(((bf16[8,192,128]{2,1,0:T(8,128)(2,1)}), bf16[8,192,128]{2,1,0:T(8,128)(2,1)}, u32[]{:S(2)}, u32[]{:S(2)}) %all-to-all-start.3) | async-done | bytes 393248 | tf_op jit(solution)/shard_map/all_to_all | solution.py:19
  119.0 1.2 slice.95
  120.9 1.1 fusion.44
  121.9 0.8 pad_maximum_fusion.1
  123.4 3.3 %all-to-all-start.5 = ((f32[8,1,768]{2,1,0:T(1,128)}), f32[8,1,768]{2,1,0:T(1,128)S(1)}, u32[]{:S(2)}, u32[]{:S(2)}) async-start(f32[8,1,768]{2,1,0:T(1,128)} %broadcast_in_dim.128), calls=%async_computation.5 | async-start | bytes 49152 | tf_op jit(solution)/shard_map/all_to_all | solution.py:19
  127.5 7.1 %all-to-all-done.5 = f32[8,1,768]{2,1,0:T(1,128)S(1)} async-done(((f32[8,1,768]{2,1,0:T(1,128)}), f32[8,1,768]{2,1,0:T(1,128)S(1)}, u32[]{:S(2)}, u32[]{:S(2)}) %all-to-all-start.5) | async-done | bytes 24608 | tf_op jit(solution)/shard_map/all_to_all | solution.py:19
  135.2 3.3 %all-to-all-start.6 = ((f32[8,1,768]{2,1,0:T(1,128)}), f32[8,1,768]{2,1,0:T(1,128)S(1)}, u32[]{:S(2)}, u32[]{:S(2)}) async-start(f32[8,1,768]{2,1,0:T(1,128)} %broadcast_in_dim.129), calls=%async_computation.6 | async-start | bytes 49152 | tf_op jit(solution)/shard_map/all_to_all | solution.py:19
  138.6 1.4 fusion.18
  140.0 6.5 %all-to-all-done.6 = f32[8,1,768]{2,1,0:T(1,128)S(1)} async-done(((f32[8,1,768]{2,1,0:T(1,128)}), f32[8,1,768]{2,1,0:T(1,128)S(1)}, u32[]{:S(2)}, u32[]{:S(2)}) %all-to-all-start.6) | async-done | bytes 24608 | tf_op jit(solution)/shard_map/all_to_all | solution.py:19
  147.1 4.8 %all-to-all-start.7 = ((f32[8,1,768]{2,1,0:T(1,128)}), f32[8,1,768]{2,1,0:T(1,128)S(1)}, u32[]{:S(2)}, u32[]{:S(2)}) async-start(f32[8,1,768]{2,1,0:T(1,128)} %broadcast_in_dim.130), calls=%async_computation.7 | async-start | bytes 49152 | tf_op jit(solution)/shard_map/all_to_all | solution.py:19
  151.9 1.3 dynamic-slice_divide_fusion
  153.2 2.7 %all-to-all-done.7 = f32[8,1,768]{2,1,0:T(1,128)S(1)} async-done(((f32[8,1,768]{2,1,0:T(1,128)}), f32[8,1,768]{2,1,0:T(1,128)S(1)}, u32[]{:S(2)}, u32[]{:S(2)}) %all-to-all-start.7) | async-done | bytes 24608 | tf_op jit(solution)/shard_map/all_to_all | solution.py:19
  157.1 2.3 %broadcast_select_fusion.1 = (bf16[96,8192]{1,0:T(8,128)(2,1)}, bf16[96,8192]{1,0:T(8,128)(2,1)}) fusion(bf16[96,8192]{1,0:T(8,128)(2,1)S(1)} %get-tuple-element.15, pred[]{:T(512)S(6)} %and.33, bf16[96,4096]{1,0:T(8,128)(2,1)S(1)} %get-tuple-element.21, bf16[96,4096]{1,0:T(8,128)(2,1)S(1)} %get-tuple-element.20), kind=kLoop, calls=%fused_computation.28 | loop fusion | flops 4718592 | bytes 6291457 | tf_op jit(solution)/shard_map/jit(_where)/select_n | solution.py:42
  159.4 4.3 %fusion.14 = f32[192,256]{1,0:T(8,128)S(1)} fusion(bf16[8192,256]{1,0:T(8,128)(2,1)} %all-gather.8.cloned.1.call-done, bf16[96,8192]{1,0:T(8,128)(2,1)} %get-tuple-element.17, bf16[96,8192]{1,0:T(8,128)(2,1)} %get-tuple-element.16), kind=kOutput, calls=%fused_computation.17 | convolution fusion | flops 811597824 | bytes 7536640 | tf_op jit(solution)/shard_map/dot_general | solution.py:171
  164.5 2.6 %collective-permute-start.2 = (bf16[96,256]{1,0:T(8,128)(2,1)S(1)}, bf16[96,256]{1,0:T(8,128)(2,1)S(1)}, u32[]{:S(2)}, u32[]{:S(2)}) collective-permute-start(bf16[96,256]{1,0:T(8,128)(2,1)S(1)} %bitcast.139), channel_id=1, source_target_pairs={{0,8},{8,0},{1,9},{9,1},{2,10},{10,2},{3,11},{11,3},{4,12},{12,4},... | collective-permute-start | bytes 147464 | tf_op jit(solution)/shard_map/ppermute | solution.py:175
  168.2 2.3 %collective-permute-done.2 = bf16[96,256]{1,0:T(8,128)(2,1)S(1)} collective-permute-done((bf16[96,256]{1,0:T(8,128)(2,1)S(1)}, bf16[96,256]{1,0:T(8,128)(2,1)S(1)}, u32[]{:S(2)}, u32[]{:S(2)}) %collective-permute-start.2) | collective-permute-done | bytes 49184 | tf_op jit(solution)/shard_map/ppermute | solution.py:175
  170.5 6.5 %all-gather.6.cloned.1.call-done = bf16[6144,256]{1,0:T(8,128)(2,1)} async-done(((bf16[768,256]{1,0:T(8,128)(2,1)}), bf16[6144,256]{1,0:T(8,128)(2,1)}) %all-gather.6.cloned.1.call-update) | async-done | bytes 3145744 | tf_op jit(solution)/shard_map/all_gather | solution.py:131
  177.0 3.0 %fusion.47 = (f32[4,96]{1,0:T(4,128)S(1)}, f32[1,4,96,6144]{3,2,1,0:T(8,128)S(1)}) fusion(bf16[6144,256]{1,0:T(8,128)(2,1)} %all-gather.6.cloned.1.call-done, pred[96,6144]{1,0:T(8,128)(4,1)S(1)} %copy-done.1, bf16[96,256]{1,0:T(8,128)(2,1)S(1)} %get-tuple-element.33, bf16[96,256]{1,0:T(8,128)(2,1)S(1)} %get-tuple-element.32), kind=kOutput, calls=%fused_computation.106 | convolution fusion | flops 608894592 | bytes 11699712 | tf_op jit(solution)/shard_map/tkgd,skd->kgts/dot_general | solution.py:181
  180.0 1.7 fusion
  181.9 1.6 abs_reduce_fusion.3
  184.2 10.9 %all-to-all-start.8 = ((f32[64,1,512]{2,1,0:T(1,128)}), f32[64,1,512]{2,1,0:T(1,128)S(1)}, u32[]{:S(2)}, u32[]{:S(2)}) async-start(f32[64,1,512]{2,1,0:T(1,128)} %broadcast_in_dim.132), calls=%async_computation.8 | async-start | bytes 262144 | tf_op jit(solution)/shard_map/all_to_all | solution.py:19
  195.2 0.9 copy.54
  198.1 9.6 %all-to-all-done.8 = f32[64,1,512]{2,1,0:T(1,128)S(1)} async-done(((f32[64,1,512]{2,1,0:T(1,128)}), f32[64,1,512]{2,1,0:T(1,128)S(1)}, u32[]{:S(2)}, u32[]{:S(2)}) %all-to-all-start.8) | async-done | bytes 131104 | tf_op jit(solution)/shard_map/all_to_all | solution.py:19
  (113 shorter events, 18.0 us)
Async XLA Ops:
  7.2 25.0 %copy-start = (bf16[96,8192]{1,0:T(8,128)(2,1)S(1)}, bf16[96,8192]{1,0:T(8,128)(2,1)}, u32[]{:S(2)}) copy-start(bf16[96,8192]{1,0:T(8,128)(2,1)} %param.6) | copy-start | bytes 4718596
  7.2 26.4 %copy-start.14 = (s32[96]{0:T(128)S(1)}, s32[96]{0:T(128)}, u32[]{:S(2)}) copy-start(s32[96]{0:T(128)} %param.11) | copy-start | bytes 1156
  7.2 26.5 %copy-start.4 = (bf16[128,512]{1,0:T(8,128)(2,1)S(1)}, bf16[128,512]{1,0:T(8,128)(2,1)}, u32[]{:S(2)}) copy-start(bf16[128,512]{1,0:T(8,128)(2,1)} %param.8) | copy-start | bytes 393220
  7.2 71.1 %all-gather.4.cloned.1.call-start = ((), (), s32[]{:S(2)}) async-start(), calls=%async_computation.9 | async-start | bytes 2359296 | tf_op jit(solution)/shard_map/all_gather | solution.py:84
  33.5 8.8 %copy-start.5 = (bf16[128,512]{1,0:T(8,128)(2,1)S(1)}, bf16[128,512]{1,0:T(8,128)(2,1)}, u32[]{:S(2)}) copy-start(bf16[128,512]{1,0:T(8,128)(2,1)} %param.8) | copy-start | bytes 393220
  33.5 8.8 %copy-start.8 = (bf16[128,128]{1,0:T(8,128)(2,1)S(1)}, bf16[128,128]{1,0:T(8,128)(2,1)}, u32[]{:S(2)}) copy-start(bf16[128,128]{1,0:T(8,128)(2,1)} %param.9) | copy-start | bytes 98308
  33.5 8.8 %copy-start.9 = (bf16[128,128]{1,0:T(8,128)(2,1)S(1)}, bf16[128,128]{1,0:T(8,128)(2,1)}, u32[]{:S(2)}) copy-start(bf16[128,128]{1,0:T(8,128)(2,1)} %param.10) | copy-start | bytes 98308
  34.8 22.3 %all-to-all-start = ((bf16[8,144,256]{2,1,0:T(8,128)(2,1)}), bf16[8,144,256]{2,1,0:T(8,128)(2,1)S(1)}, u32[]{:S(2)}, u32[]{:S(2)}) async-start(bf16[8,144,256]{2,1,0:T(8,128)(2,1)} %maximum_maximum_fusion), calls=%async_computation | async-start | bytes 1179648 | tf_op jit(solution)/shard_map/all_to_all | solution.py:19
  38.4 121.0 %all-gather.8.cloned.1.call-start = ((), (), s32[]{:S(2)}) async-start(), calls=%async_computation.11 | async-start | bytes 4718592 | tf_op jit(solution)/shard_map/all_gather | solution.py:104
  38.5 30.3 %collective-permute-start = (bf16[96,4096]{1,0:T(8,128)(2,1)S(1)}, bf16[96,4096]{1,0:T(8,128)(2,1)}, u32[]{:S(2)}, u32[]{:S(2)}) collective-permute-start(bf16[96,4096]{1,0:T(8,128)(2,1)S(1)} %constant_dynamic-slice_fusion), channel_id=1, source_target_pairs={{0,8},{8,0},{1,9},{9,1},{2,10},{10,2},{3,11},{11,3},{4,12},{12,4},... | collective-permute-start | bytes 2359304 | tf_op jit(solution)/shard_map/ppermute | solution.py:92
  61.0 21.4 %all-to-all-start.4 = ((bf16[8,2,6208]{2,1,0:T(2,128)(2,1)}), bf16[8,2,6208]{2,1,0:T(2,128)(2,1)}, u32[]{:S(2)}, u32[]{:S(2)}) async-start(bf16[8,2,6208]{2,1,0:T(2,128)(2,1)} %reshape.307), calls=%async_computation.4 | async-start | bytes 401408 | tf_op jit(solution)/shard_map/all_to_all | solution.py:19
  68.9 5.7 %collective-permute-start.1 = (bf16[96,4096]{1,0:T(8,128)(2,1)}, bf16[96,4096]{1,0:T(8,128)(2,1)}, u32[]{:S(2)}, u32[]{:S(2)}) collective-permute-start(bf16[96,4096]{1,0:T(8,128)(2,1)} %collective-permute-done), channel_id=1, source_target_pairs={{0,1},{1,0},{2,3},{3,2},{4,5},{5,4},{6,7},{7,6},{8,9},{9,8},{10,11... | collective-permute-start | bytes 2359304 | tf_op jit(solution)/shard_map/ppermute | solution.py:114
  70.8 11.1 %copy-start.13 = (f32[64]{0:T(128)}, f32[64]{0:T(128)S(1)}, u32[]{:S(2)}) copy-start(f32[64]{0:T(128)S(1)} %multiply_exponential_fusion.1) | copy-start | bytes 772
  71.3 10.6 %copy-start.12 = (f32[192]{0:T(256)}, f32[192]{0:T(256)S(1)}, u32[]{:S(2)}) copy-start(f32[192]{0:T(256)S(1)} %add_convert_fusion.1) | copy-start | bytes 2308
  82.4 15.3 %all-to-all-start.1 = ((bf16[8,2,448]{2,1,0:T(2,128)(2,1)}), bf16[8,2,448]{2,1,0:T(2,128)(2,1)S(1)}, u32[]{:S(2)}, u32[]{:S(2)}) async-start(bf16[8,2,448]{2,1,0:T(2,128)(2,1)} %reshape.305), calls=%async_computation.1 | async-start | bytes 32768 | tf_op jit(solution)/shard_map/all_to_all | solution.py:19
  97.6 9.2 %copy-start.10 = (bf16[8,2,448]{2,1,0:T(2,128)(2,1)}, bf16[8,2,448]{2,1,0:T(2,128)(2,1)S(1)}, u32[]{:S(2)}) copy-start(bf16[8,2,448]{2,1,0:T(2,128)(2,1)S(1)} %all-to-all-done.1) | copy-start | bytes 43012
  99.2 19.8 %all-to-all-start.3 = ((bf16[8,192,128]{2,1,0:T(8,128)(2,1)}), bf16[8,192,128]{2,1,0:T(8,128)(2,1)}, u32[]{:S(2)}, u32[]{:S(2)}) async-start(bf16[8,192,128]{2,1,0:T(8,128)(2,1)} %broadcast_in_dim.125), calls=%async_computation.3 | async-start | bytes 786432 | tf_op jit(solution)/shard_map/all_to_all | solution.py:19
  105.0 72.0 %all-gather.6.cloned.1.call-start = ((), (), s32[]{:S(2)}) async-start(), calls=%async_computation.10 | async-start | bytes 3538944 | tf_op jit(solution)/shard_map/all_gather | solution.py:131
  109.2 29.4 %copy-start.15 = (s32[96]{0:T(128)S(1)}, s32[96]{0:T(128)}, u32[]{:S(2)}) copy-start(s32[96]{0:T(128)} %param.11) | copy-start | bytes 1156
  109.2 29.4 %copy-start.16 = (s32[96]{0:T(128)S(1)}, s32[96]{0:T(128)}, u32[]{:S(2)}) copy-start(s32[96]{0:T(128)} %iota_add_fusion) | copy-start | bytes 1156
  113.1 0.6 copy-start.11
  123.4 11.2 %all-to-all-start.5 = ((f32[8,1,768]{2,1,0:T(1,128)}), f32[8,1,768]{2,1,0:T(1,128)S(1)}, u32[]{:S(2)}, u32[]{:S(2)}) async-start(f32[8,1,768]{2,1,0:T(1,128)} %broadcast_in_dim.128), calls=%async_computation.5 | async-start | bytes 49152 | tf_op jit(solution)/shard_map/all_to_all | solution.py:19
  135.2 11.2 %all-to-all-start.6 = ((f32[8,1,768]{2,1,0:T(1,128)}), f32[8,1,768]{2,1,0:T(1,128)S(1)}, u32[]{:S(2)}, u32[]{:S(2)}) async-start(f32[8,1,768]{2,1,0:T(1,128)} %broadcast_in_dim.129), calls=%async_computation.6 | async-start | bytes 49152 | tf_op jit(solution)/shard_map/all_to_all | solution.py:19
  147.1 8.8 %all-to-all-start.7 = ((f32[8,1,768]{2,1,0:T(1,128)}), f32[8,1,768]{2,1,0:T(1,128)S(1)}, u32[]{:S(2)}, u32[]{:S(2)}) async-start(f32[8,1,768]{2,1,0:T(1,128)} %broadcast_in_dim.130), calls=%async_computation.7 | async-start | bytes 49152 | tf_op jit(solution)/shard_map/all_to_all | solution.py:19
  159.4 4.4 %copy-start.6 = (f32[192,64]{1,0:T(8,128)S(1)}, f32[192,64]{1,0:T(8,128)}, u32[]{:S(2)}) copy-start(f32[192,64]{1,0:T(8,128)} %get-tuple-element.36) | copy-start | bytes 147460
  159.4 4.4 %copy-start.7 = (f32[192,64]{1,0:T(8,128)S(1)}, f32[192,64]{1,0:T(8,128)}, u32[]{:S(2)}) copy-start(f32[192,64]{1,0:T(8,128)} %get-tuple-element.37) | copy-start | bytes 147460
  159.4 17.6 %copy-start.1 = (pred[96,6144]{1,0:T(8,128)(4,1)S(1)}, pred[96,6144]{1,0:T(8,128)(4,1)}, u32[]{:S(2)}) copy-start(pred[96,6144]{1,0:T(8,128)(4,1)} %fusion.18) | copy-start | bytes 1769476
  164.5 6.0 %collective-permute-start.2 = (bf16[96,256]{1,0:T(8,128)(2,1)S(1)}, bf16[96,256]{1,0:T(8,128)(2,1)S(1)}, u32[]{:S(2)}, u32[]{:S(2)}) collective-permute-start(bf16[96,256]{1,0:T(8,128)(2,1)S(1)} %bitcast.139), channel_id=1, source_target_pairs={{0,8},{8,0},{1,9},{9,1},{2,10},{10,2},{3,11},{11,3},{4,12},{12,4},... | collective-permute-start | bytes 147464 | tf_op jit(solution)/shard_map/ppermute | solution.py:175
  180.0 1.9 copy-start.2
  181.9 13.2 %copy-start.3 = (bf16[8,12288]{1,0:T(8,128)(2,1)S(1)}, bf16[8,12288]{1,0:T(8,128)(2,1)}, u32[]{:S(2)}) copy-start(bf16[8,12288]{1,0:T(8,128)(2,1)} %slice.104) | copy-start | bytes 589828
  184.2 23.5 %all-to-all-start.8 = ((f32[64,1,512]{2,1,0:T(1,128)}), f32[64,1,512]{2,1,0:T(1,128)S(1)}, u32[]{:S(2)}, u32[]{:S(2)}) async-start(f32[64,1,512]{2,1,0:T(1,128)} %broadcast_in_dim.132), calls=%async_computation.8 | async-start | bytes 262144 | tf_op jit(solution)/shard_map/all_to_all | solution.py:19
Sparse Core Ops, SparseCore 0:
  30.5 39.6 all-gather.3
  72.2 56.0 all-gather.7
  130.4 46.5 all-gather.5

commit v11 on v9

--- a/solution.py
+++ b/solution.py
@@ -186,7 +186,8 @@
     allowed = (doc_ids[:, None] == doc_block[None, :]) & (
         key_positions[None, :] <= query_positions[:, None]
     )
-    scores = jnp.where(allowed, scores, -1e30)
+    bias = lax.optimization_barrier(jnp.where(allowed, 0.0, -1e30))
+    scores = scores + bias
     highest = jnp.max(scores, axis=3, keepdims=True)
     weights = jnp.exp(scores - highest)
     totals = jnp.sum(weights, axis=3)

time: 217 us -> 216 us (level)
  waiting for transfers between devices: 64.3 us -> 75.2 us
  local copies, waits for them, and re-layouts: 23.4 us -> 14.7 us
  other arithmetic: 24.4 us -> 22.2 us
    all_to_all x8, waiting for transfers between devices: 52.4 us -> 60.9 us  [exchange(): return lax.all_to_all(parts, axis, split_axis=0, concat_axis=0, tiled=True)]
    unnamed x49 -> x37, local copies, waits for them, and re-layouts: 11.6 us -> 5.75 us
  transfers between devices with their start and end apart: 14 -> 14, of which waited for: 10 -> 10; matrix products, arithmetic and copies ran while one was open for 24% -> 19% of each run, Pallas kernels for 0% -> 0%
where the time goes in v11:
time: 216 us; the launch traced here: 215 us
  waiting for transfers between devices  75.2 us (35%)
  starting transfers between devices  52 us (24%)
  other arithmetic  22.2 us (10%)
  blocking collectives  22.1 us (10%)
  between operations  16.3 us (8%)
  local copies, waits for them, and re-layouts  14.7 us (7%)
  matrix products  12.1 us (6%)
    all_to_all x8, waiting for transfers between devices, exchange(): return lax.all_to_all(parts, axis, split_axis=0, concat_axis=0, tiled=True)  60.9 us
    all_to_all x8, starting transfers between devices, exchange(): return lax.all_to_all(parts, axis, split_axis=0, concat_axis=0, tiled=True)  43.7 us
    all_to_all x1, blocking collectives, exchange(): return lax.all_to_all(parts, axis, split_axis=0, concat_axis=0, tiled=True)  22.1 us
    all_gather x1, waiting for transfers between devices, on_device(): everything = lax.all_gather(sent_y, 'y', axis=0, tiled=True)  8.22 us
    select_n x2, other arithmetic, in_pair_order(): jnp.where(even, own, other)  6.13 us
    unnamed x37, local copies, waits for them, and re-layouts  5.75 us
  transfers between devices with their start and end apart: 14, of which 10 were waited for; matrix products, arithmetic and copies ran while one was open for 19% of the time, Pallas kernels for 0%

profile of v11, /device:TPU:2, one launch (start us, length us, event | category | flops | bytes accessed | tf_op | source)
XLA Modules:
  0.0 214.7 jit_solution(11751529130930098960)
XLA Ops:
  7.3 1.0 broadcast_select_fusion.7
  8.2 22.1 %all_to_all.63 = bf16[8,128,128]{2,1,0:T(8,128)(2,1)} all-to-all(bf16[8,128,128]{2,1,0:T(8,128)(2,1)S(1)} %broadcast_select_fusion.7), channel_id=1, replica_groups=mesh['y'=8,'z'=4,'pair'=2,'x'=4,'core'=2] {'z','pair'}, dimensions={0} | all-to-all | bytes 524288 | tf_op jit(solution)/shard_map/all_to_all | solution.py:19
  30.4 1.8 fusion.6
  33.1 1.0 maximum_maximum_fusion
  34.2 3.5 %all-to-all-start = ((bf16[8,144,256]{2,1,0:T(8,128)(2,1)}), bf16[8,144,256]{2,1,0:T(8,128)(2,1)S(1)}, u32[]{:S(2)}, u32[]{:S(2)}) async-start(bf16[8,144,256]{2,1,0:T(8,128)(2,1)} %maximum_maximum_fusion), calls=%async_computation | async-start | bytes 1179648 | tf_op jit(solution)/shard_map/all_to_all | solution.py:19
  37.8 1.0 constant_dynamic-slice_fusion
  38.8 3.8 %collective-permute-start = (bf16[96,4096]{1,0:T(8,128)(2,1)}, bf16[96,4096]{1,0:T(8,128)(2,1)}, u32[]{:S(2)}, u32[]{:S(2)}) collective-permute-start(bf16[96,4096]{1,0:T(8,128)(2,1)} %constant_dynamic-slice_fusion), channel_id=1, source_target_pairs={{0,8},{8,0},{1,9},{9,1},{2,10},{10,2},{3,11},{11,3},{4,12},{12,4},... | collective-permute-start | bytes 2359304 | tf_op jit(solution)/shard_map/ppermute | solution.py:92
  42.8 13.7 %all-to-all-done = bf16[8,144,256]{2,1,0:T(8,128)(2,1)S(1)} async-done(((bf16[8,144,256]{2,1,0:T(8,128)(2,1)}), bf16[8,144,256]{2,1,0:T(8,128)(2,1)S(1)}, u32[]{:S(2)}, u32[]{:S(2)}) %all-to-all-start) | async-done | bytes 589856 | tf_op jit(solution)/shard_map/all_to_all | solution.py:19
  56.5 0.9 slice.98
  58.0 0.8 reduce.11
  58.7 0.9 reshape.312
  59.6 4.8 %all-to-all-start.4 = ((bf16[8,2,6208]{2,1,0:T(2,128)(2,1)}), bf16[8,2,6208]{2,1,0:T(2,128)(2,1)S(1)}, u32[]{:S(2)}, u32[]{:S(2)}) async-start(bf16[8,2,6208]{2,1,0:T(2,128)(2,1)} %reshape.312), calls=%async_computation.4 | async-start | bytes 401408 | tf_op jit(solution)/shard_map/all_to_all | solution.py:19
  64.4 3.8 %collective-permute-done = bf16[96,4096]{1,0:T(8,128)(2,1)} collective-permute-done((bf16[96,4096]{1,0:T(8,128)(2,1)}, bf16[96,4096]{1,0:T(8,128)(2,1)}, u32[]{:S(2)}, u32[]{:S(2)}) %collective-permute-start) | collective-permute-done | bytes 786464 | tf_op jit(solution)/shard_map/ppermute | solution.py:92
  68.2 1.9 collective-permute-start.1
  71.9 0.7 reduce.10
  72.5 0.7 reshape.310
  73.9 1.5 broadcast_select_fusion.5
  75.4 2.2 %broadcast_select_fusion.3 = (bf16[96,8192]{1,0:T(8,128)(2,1)}, bf16[96,8192]{1,0:T(8,128)(2,1)}) fusion(bf16[96,8192]{1,0:T(8,128)(2,1)S(1)} %get-tuple-element.15, pred[]{:T(512)S(6)} %and.31, bf16[96,4096]{1,0:T(8,128)(2,1)S(1)} %get-tuple-element.21, bf16[96,4096]{1,0:T(8,128)(2,1)S(1)} %get-tuple-element.20), kind=kLoop, calls=%fused_computation.30 | loop fusion | flops 4718592 | bytes 6291457 | tf_op jit(solution)/shard_map/jit(_where)/select_n | solution.py:42
  77.6 3.5 %fusion.9 = f32[192,128]{1,0:T(8,128)S(1)} fusion(bf16[8192,128]{1,0:T(8,128)(2,1)} %all-gather.4.cloned.1.call-done, bf16[96,8192]{1,0:T(8,128)(2,1)} %get-tuple-element.19, bf16[96,8192]{1,0:T(8,128)(2,1)} %get-tuple-element.18), kind=kOutput, calls=%fused_computation.12 | convolution fusion | flops 408944640 | bytes 5341184 | tf_op jit(solution)/shard_map/dot_general | solution.py:123
  81.6 7.1 %all-to-all-start.3 = ((bf16[8,2,448]{2,1,0:T(2,128)(2,1)}), bf16[8,2,448]{2,1,0:T(2,128)(2,1)S(1)}, u32[]{:S(2)}, u32[]{:S(2)}) async-start(bf16[8,2,448]{2,1,0:T(2,128)(2,1)} %reshape.310), calls=%async_computation.3 | async-start | bytes 32768 | tf_op jit(solution)/shard_map/all_to_all | solution.py:19
  88.8 8.1 %all-to-all-done.3 = bf16[8,2,448]{2,1,0:T(2,128)(2,1)S(1)} async-done(((bf16[8,2,448]{2,1,0:T(2,128)(2,1)}), bf16[8,2,448]{2,1,0:T(2,128)(2,1)S(1)}, u32[]{:S(2)}, u32[]{:S(2)}) %all-to-all-start.3) | async-done | bytes 14368 | tf_op jit(solution)/shard_map/all_to_all | solution.py:19
  96.9 0.8 broadcast_in_dim.124
  97.7 5.8 %all-to-all-start.2 = ((bf16[8,192,128]{2,1,0:T(8,128)(2,1)}), bf16[8,192,128]{2,1,0:T(8,128)(2,1)S(1)}, u32[]{:S(2)}, u32[]{:S(2)}) async-start(bf16[8,192,128]{2,1,0:T(8,128)(2,1)} %broadcast_in_dim.124), calls=%async_computation.2 | async-start | bytes 786432 | tf_op jit(solution)/shard_map/all_to_all | solution.py:19
  103.5 1.1 multiply_cosine_fusion
  105.1 12.3 %all-to-all-done.2 = bf16[8,192,128]{2,1,0:T(8,128)(2,1)S(1)} async-done(((bf16[8,192,128]{2,1,0:T(8,128)(2,1)}), bf16[8,192,128]{2,1,0:T(8,128)(2,1)S(1)}, u32[]{:S(2)}, u32[]{:S(2)}) %all-to-all-start.2) | async-done | bytes 393248 | tf_op jit(solution)/shard_map/all_to_all | solution.py:19
  118.6 0.8 pad_maximum_fusion.1
  120.0 3.3 %all-to-all-start.5 = ((f32[8,1,768]{2,1,0:T(1,128)}), f32[8,1,768]{2,1,0:T(1,128)S(1)}, u32[]{:S(2)}, u32[]{:S(2)}) async-start(f32[8,1,768]{2,1,0:T(1,128)} %broadcast_in_dim.128), calls=%async_computation.5 | async-start | bytes 49152 | tf_op jit(solution)/shard_map/all_to_all | solution.py:19
  123.4 7.8 %all-to-all-done.5 = f32[8,1,768]{2,1,0:T(1,128)S(1)} async-done(((f32[8,1,768]{2,1,0:T(1,128)}), f32[8,1,768]{2,1,0:T(1,128)S(1)}, u32[]{:S(2)}, u32[]{:S(2)}) %all-to-all-start.5) | async-done | bytes 24608 | tf_op jit(solution)/shard_map/all_to_all | solution.py:19
  131.9 3.3 %all-to-all-start.6 = ((f32[8,1,768]{2,1,0:T(1,128)}), f32[8,1,768]{2,1,0:T(1,128)S(1)}, u32[]{:S(2)}, u32[]{:S(2)}) async-start(f32[8,1,768]{2,1,0:T(1,128)} %broadcast_in_dim.129), calls=%async_computation.6 | async-start | bytes 49152 | tf_op jit(solution)/shard_map/all_to_all | solution.py:19
  135.2 1.0 fusion.18
  136.3 6.8 %all-to-all-done.6 = f32[8,1,768]{2,1,0:T(1,128)S(1)} async-done(((f32[8,1,768]{2,1,0:T(1,128)}), f32[8,1,768]{2,1,0:T(1,128)S(1)}, u32[]{:S(2)}, u32[]{:S(2)}) %all-to-all-start.6) | async-done | bytes 24608 | tf_op jit(solution)/shard_map/all_to_all | solution.py:19
  143.8 4.8 %all-to-all-start.7 = ((f32[8,1,768]{2,1,0:T(1,128)}), f32[8,1,768]{2,1,0:T(1,128)S(1)}, u32[]{:S(2)}, u32[]{:S(2)}) async-start(f32[8,1,768]{2,1,0:T(1,128)} %broadcast_in_dim.130), calls=%async_computation.7 | async-start | bytes 49152 | tf_op jit(solution)/shard_map/all_to_all | solution.py:19
  148.6 1.3 dynamic-slice_divide_fusion
  149.9 2.7 %all-to-all-done.7 = f32[8,1,768]{2,1,0:T(1,128)S(1)} async-done(((f32[8,1,768]{2,1,0:T(1,128)}), f32[8,1,768]{2,1,0:T(1,128)S(1)}, u32[]{:S(2)}, u32[]{:S(2)}) %all-to-all-start.7) | async-done | bytes 24608 | tf_op jit(solution)/shard_map/all_to_all | solution.py:19
  153.7 3.9 %broadcast_select_fusion.1 = (bf16[96,8192]{1,0:T(8,128)(2,1)}, bf16[96,8192]{1,0:T(8,128)(2,1)}) fusion(bf16[96,8192]{1,0:T(8,128)(2,1)} %copy-done, pred[]{:T(512)S(6)} %and.32, bf16[96,4096]{1,0:T(8,128)(2,1)} %copy-done.1, bf16[96,4096]{1,0:T(8,128)(2,1)S(1)} %get-tuple-element.20), kind=kLoop, calls=%fused_computation.28 | loop fusion | flops 4718592 | bytes 6291457 | tf_op jit(solution)/shard_map/jit(_where)/select_n | solution.py:42
  157.6 4.2 %fusion.13 = f32[192,256]{1,0:T(8,128)S(1)} fusion(bf16[8192,256]{1,0:T(8,128)(2,1)} %all-gather.8.cloned.1.call-done, bf16[96,8192]{1,0:T(8,128)(2,1)} %get-tuple-element.17, bf16[96,8192]{1,0:T(8,128)(2,1)} %get-tuple-element.16), kind=kOutput, calls=%fused_computation.16 | convolution fusion | flops 811597824 | bytes 7536640 | tf_op jit(solution)/shard_map/dot_general | solution.py:171
  162.8 2.6 %collective-permute-start.2 = (bf16[96,256]{1,0:T(8,128)(2,1)S(1)}, bf16[96,256]{1,0:T(8,128)(2,1)S(1)}, u32[]{:S(2)}, u32[]{:S(2)}) collective-permute-start(bf16[96,256]{1,0:T(8,128)(2,1)S(1)} %bitcast.141), channel_id=1, source_target_pairs={{0,8},{8,0},{1,9},{9,1},{2,10},{10,2},{3,11},{11,3},{4,12},{12,4},... | collective-permute-start | bytes 147464 | tf_op jit(solution)/shard_map/ppermute | solution.py:175
  166.5 2.3 %collective-permute-done.2 = bf16[96,256]{1,0:T(8,128)(2,1)S(1)} collective-permute-done((bf16[96,256]{1,0:T(8,128)(2,1)S(1)}, bf16[96,256]{1,0:T(8,128)(2,1)S(1)}, u32[]{:S(2)}, u32[]{:S(2)}) %collective-permute-start.2) | collective-permute-done | bytes 49184 | tf_op jit(solution)/shard_map/ppermute | solution.py:175
  168.8 8.2 %all-gather.6.cloned.1.call-done = bf16[6144,256]{1,0:T(8,128)(2,1)} async-done(((bf16[768,256]{1,0:T(8,128)(2,1)}), bf16[6144,256]{1,0:T(8,128)(2,1)}) %all-gather.6.cloned.1.call-update) | async-done | bytes 3145744 | tf_op jit(solution)/shard_map/all_gather | solution.py:131
  177.0 2.9 %fusion.46 = (f32[4,96]{1,0:T(4,128)S(1)}, f32[1,4,96,6144]{3,2,1,0:T(8,128)S(1)}) fusion(f32[96,6144]{1,0:T(8,128)S(1)} %fusion.18, bf16[6144,256]{1,0:T(8,128)(2,1)} %all-gather.6.cloned.1.call-done, bf16[96,256]{1,0:T(8,128)(2,1)S(1)} %get-tuple-element.33, bf16[96,256]{1,0:T(8,128)(2,1)S(1)} %get-tuple-element.32), kind=kOutput, calls=%fused_computation.105 | convolution fusion | flops 611253888 | bytes 13469184 | tf_op jit(solution)/shard_map/tkgd,skd->kgts/dot_general | solution.py:181
  179.9 1.4 fusion
  181.8 1.4 abs_reduce_fusion.3
  183.3 0.7 broadcast_in_dim.133
  184.0 10.9 %all-to-all-start.8 = ((f32[64,1,512]{2,1,0:T(1,128)}), f32[64,1,512]{2,1,0:T(1,128)S(1)}, u32[]{:S(2)}, u32[]{:S(2)}) async-start(f32[64,1,512]{2,1,0:T(1,128)} %broadcast_in_dim.133), calls=%async_computation.8 | async-start | bytes 262144 | tf_op jit(solution)/shard_map/all_to_all | solution.py:19
  195.0 0.9 copy.54
  197.2 0.7 copy.73
  197.9 9.6 %all-to-all-done.8 = f32[64,1,512]{2,1,0:T(1,128)S(1)} async-done(((f32[64,1,512]{2,1,0:T(1,128)}), f32[64,1,512]{2,1,0:T(1,128)S(1)}, u32[]{:S(2)}, u32[]{:S(2)}) %all-to-all-start.8) | async-done | bytes 131104 | tf_op jit(solution)/shard_map/all_to_all | solution.py:19
  207.5 0.7 reduce_max.109
  (101 shorter events, 11.5 us)
Async XLA Ops:
  7.2 25.1 %copy-start.2 = (bf16[96,8192]{1,0:T(8,128)(2,1)S(1)}, bf16[96,8192]{1,0:T(8,128)(2,1)}, u32[]{:S(2)}) copy-start(bf16[96,8192]{1,0:T(8,128)(2,1)} %param.6) | copy-start | bytes 4718596
  7.2 25.1 %copy-start.9 = (f32[8192]{0:T(1024)S(1)}, f32[8192]{0:T(1024)}, u32[]{:S(2)}) copy-start(f32[8192]{0:T(1024)} %param.7) | copy-start | bytes 98308
  7.2 70.4 %all-gather.4.cloned.1.call-start = ((), (), s32[]{:S(2)}) async-start(), calls=%async_computation.9 | async-start | bytes 2359296 | tf_op jit(solution)/shard_map/all_gather | solution.py:84
  30.4 2.5 %copy-start.10 = (s32[96]{0:T(128)S(1)}, s32[96]{0:T(128)}, u32[]{:S(2)}) copy-start(s32[96]{0:T(128)} %param.11) | copy-start | bytes 1156
  30.4 2.6 %copy-start.4 = (bf16[128,512]{1,0:T(8,128)(2,1)S(1)}, bf16[128,512]{1,0:T(8,128)(2,1)}, u32[]{:S(2)}) copy-start(bf16[128,512]{1,0:T(8,128)(2,1)} %param.8) | copy-start | bytes 393220
  32.8 42.6 %copy-start = (bf16[96,8192]{1,0:T(8,128)(2,1)}, bf16[96,8192]{1,0:T(8,128)(2,1)S(1)}, u32[]{:S(2)}) copy-start(bf16[96,8192]{1,0:T(8,128)(2,1)S(1)} %get-tuple-element.15) | copy-start | bytes 4718596
  33.0 9.6 %copy-start.7 = (bf16[128,128]{1,0:T(8,128)(2,1)S(1)}, bf16[128,128]{1,0:T(8,128)(2,1)}, u32[]{:S(2)}) copy-start(bf16[128,128]{1,0:T(8,128)(2,1)} %param.9) | copy-start | bytes 98308
  33.0 9.6 %copy-start.8 = (bf16[128,128]{1,0:T(8,128)(2,1)S(1)}, bf16[128,128]{1,0:T(8,128)(2,1)}, u32[]{:S(2)}) copy-start(bf16[128,128]{1,0:T(8,128)(2,1)} %param.10) | copy-start | bytes 98308
  34.2 22.3 %all-to-all-start = ((bf16[8,144,256]{2,1,0:T(8,128)(2,1)}), bf16[8,144,256]{2,1,0:T(8,128)(2,1)S(1)}, u32[]{:S(2)}, u32[]{:S(2)}) async-start(bf16[8,144,256]{2,1,0:T(8,128)(2,1)} %maximum_maximum_fusion), calls=%async_computation | async-start | bytes 1179648 | tf_op jit(solution)/shard_map/all_to_all | solution.py:19
  37.7 119.9 %all-gather.8.cloned.1.call-start = ((), (), s32[]{:S(2)}) async-start(), calls=%async_computation.11 | async-start | bytes 4718592 | tf_op jit(solution)/shard_map/all_gather | solution.py:104
  38.8 29.4 %collective-permute-start = (bf16[96,4096]{1,0:T(8,128)(2,1)}, bf16[96,4096]{1,0:T(8,128)(2,1)}, u32[]{:S(2)}, u32[]{:S(2)}) collective-permute-start(bf16[96,4096]{1,0:T(8,128)(2,1)} %constant_dynamic-slice_fusion), channel_id=1, source_target_pairs={{0,8},{8,0},{1,9},{9,1},{2,10},{10,2},{3,11},{11,3},{4,12},{12,4},... | collective-permute-start | bytes 2359304 | tf_op jit(solution)/shard_map/ppermute | solution.py:92
  59.6 22.0 %all-to-all-start.4 = ((bf16[8,2,6208]{2,1,0:T(2,128)(2,1)}), bf16[8,2,6208]{2,1,0:T(2,128)(2,1)S(1)}, u32[]{:S(2)}, u32[]{:S(2)}) async-start(bf16[8,2,6208]{2,1,0:T(2,128)(2,1)} %reshape.312), calls=%async_computation.4 | async-start | bytes 401408 | tf_op jit(solution)/shard_map/all_to_all | solution.py:19
  68.2 5.7 %collective-permute-start.1 = (bf16[96,4096]{1,0:T(8,128)(2,1)}, bf16[96,4096]{1,0:T(8,128)(2,1)}, u32[]{:S(2)}, u32[]{:S(2)}) collective-permute-start(bf16[96,4096]{1,0:T(8,128)(2,1)} %collective-permute-done), channel_id=1, source_target_pairs={{0,1},{1,0},{2,3},{3,2},{4,5},{5,4},{6,7},{7,6},{8,9},{9,8},{10,11... | collective-permute-start | bytes 2359304 | tf_op jit(solution)/shard_map/ppermute | solution.py:114
  75.4 5.8 %copy-start.1 = (bf16[96,4096]{1,0:T(8,128)(2,1)}, bf16[96,4096]{1,0:T(8,128)(2,1)S(1)}, u32[]{:S(2)}) copy-start(bf16[96,4096]{1,0:T(8,128)(2,1)S(1)} %get-tuple-element.21) | copy-start | bytes 2359300
  81.6 15.3 %all-to-all-start.3 = ((bf16[8,2,448]{2,1,0:T(2,128)(2,1)}), bf16[8,2,448]{2,1,0:T(2,128)(2,1)S(1)}, u32[]{:S(2)}, u32[]{:S(2)}) async-start(bf16[8,2,448]{2,1,0:T(2,128)(2,1)} %reshape.310), calls=%async_computation.3 | async-start | bytes 32768 | tf_op jit(solution)/shard_map/all_to_all | solution.py:19
  97.7 19.7 %all-to-all-start.2 = ((bf16[8,192,128]{2,1,0:T(8,128)(2,1)}), bf16[8,192,128]{2,1,0:T(8,128)(2,1)S(1)}, u32[]{:S(2)}, u32[]{:S(2)}) async-start(bf16[8,192,128]{2,1,0:T(8,128)(2,1)} %broadcast_in_dim.124), calls=%async_computation.2 | async-start | bytes 786432 | tf_op jit(solution)/shard_map/all_to_all | solution.py:19
  103.4 73.5 %all-gather.6.cloned.1.call-start = ((), (), s32[]{:S(2)}) async-start(), calls=%async_computation.10 | async-start | bytes 3538944 | tf_op jit(solution)/shard_map/all_gather | solution.py:131
  120.0 11.2 %all-to-all-start.5 = ((f32[8,1,768]{2,1,0:T(1,128)}), f32[8,1,768]{2,1,0:T(1,128)S(1)}, u32[]{:S(2)}, u32[]{:S(2)}) async-start(f32[8,1,768]{2,1,0:T(1,128)} %broadcast_in_dim.128), calls=%async_computation.5 | async-start | bytes 49152 | tf_op jit(solution)/shard_map/all_to_all | solution.py:19
  131.9 11.2 %all-to-all-start.6 = ((f32[8,1,768]{2,1,0:T(1,128)}), f32[8,1,768]{2,1,0:T(1,128)S(1)}, u32[]{:S(2)}, u32[]{:S(2)}) async-start(f32[8,1,768]{2,1,0:T(1,128)} %broadcast_in_dim.129), calls=%async_computation.6 | async-start | bytes 49152 | tf_op jit(solution)/shard_map/all_to_all | solution.py:19
  143.8 8.8 %all-to-all-start.7 = ((f32[8,1,768]{2,1,0:T(1,128)}), f32[8,1,768]{2,1,0:T(1,128)S(1)}, u32[]{:S(2)}, u32[]{:S(2)}) async-start(f32[8,1,768]{2,1,0:T(1,128)} %broadcast_in_dim.130), calls=%async_computation.7 | async-start | bytes 49152 | tf_op jit(solution)/shard_map/all_to_all | solution.py:19
  157.6 4.4 %copy-start.5 = (f32[192,64]{1,0:T(8,128)S(1)}, f32[192,64]{1,0:T(8,128)}, u32[]{:S(2)}) copy-start(f32[192,64]{1,0:T(8,128)} %get-tuple-element.36) | copy-start | bytes 147460
  157.6 4.4 %copy-start.6 = (f32[192,64]{1,0:T(8,128)S(1)}, f32[192,64]{1,0:T(8,128)}, u32[]{:S(2)}) copy-start(f32[192,64]{1,0:T(8,128)} %get-tuple-element.37) | copy-start | bytes 147460
  162.8 6.0 %collective-permute-start.2 = (bf16[96,256]{1,0:T(8,128)(2,1)S(1)}, bf16[96,256]{1,0:T(8,128)(2,1)S(1)}, u32[]{:S(2)}, u32[]{:S(2)}) collective-permute-start(bf16[96,256]{1,0:T(8,128)(2,1)S(1)} %bitcast.141), channel_id=1, source_target_pairs={{0,8},{8,0},{1,9},{9,1},{2,10},{10,2},{3,11},{11,3},{4,12},{12,4},... | collective-permute-start | bytes 147464 | tf_op jit(solution)/shard_map/ppermute | solution.py:175
  179.9 1.9 copy-start.3
  184.0 23.5 %all-to-all-start.8 = ((f32[64,1,512]{2,1,0:T(1,128)}), f32[64,1,512]{2,1,0:T(1,128)S(1)}, u32[]{:S(2)}, u32[]{:S(2)}) async-start(f32[64,1,512]{2,1,0:T(1,128)} %broadcast_in_dim.133), calls=%async_computation.8 | async-start | bytes 262144 | tf_op jit(solution)/shard_map/all_to_all | solution.py:19
Sparse Core Ops, SparseCore 0:
  30.5 39.6 all-gather.3
  72.2 56.0 all-gather.7
  130.4 46.5 all-gather.5

commit v12 on v10

--- a/solution.py
+++ b/solution.py
@@ -186,7 +186,8 @@
     allowed = (doc_ids[:, None] == doc_block[None, :]) & (
         key_positions[None, :] <= query_positions[:, None]
     )
-    scores = jnp.where(allowed, scores, -1e30)
+    bias = lax.optimization_barrier(jnp.where(allowed, 0.0, -1e30))
+    scores = scores + bias
     highest = jnp.max(scores, axis=3, keepdims=True)
     weights = jnp.exp((scores - highest) * (1.0 / math.sqrt(HEAD)))
     totals = jnp.sum(weights, axis=3)

time: 216 us -> 216 us (level)
  waiting for transfers between devices: 64.3 us -> 74.3 us
  local copies, waits for them, and re-layouts: 23.2 us -> 14.5 us
    all_to_all x8, waiting for transfers between devices: 52.4 us -> 60.9 us  [exchange(): return lax.all_to_all(parts, axis, split_axis=0, concat_axis=0, tiled=True)]
    unnamed x49 -> x35, local copies, waits for them, and re-layouts: 11.3 us -> 5.48 us
  transfers between devices with their start and end apart: 14 -> 14, of which waited for: 10 -> 10; matrix products, arithmetic and copies ran while one was open for 24% -> 19% of each run, Pallas kernels for 0% -> 0%
where the time goes in v12:
time: 216 us; the launch traced here: 215 us
  waiting for transfers between devices  74.3 us (34%)
  starting transfers between devices  52 us (24%)
  other arithmetic  23.2 us (11%)
  blocking collectives  22.1 us (10%)
  between operations  16.3 us (8%)
  local copies, waits for them, and re-layouts  14.5 us (7%)
  matrix products  12.2 us (6%)
    all_to_all x8, waiting for transfers between devices, exchange(): return lax.all_to_all(parts, axis, split_axis=0, concat_axis=0, tiled=True)  60.9 us
    all_to_all x8, starting transfers between devices, exchange(): return lax.all_to_all(parts, axis, split_axis=0, concat_axis=0, tiled=True)  43.6 us
    all_to_all x1, blocking collectives, exchange(): return lax.all_to_all(parts, axis, split_axis=0, concat_axis=0, tiled=True)  22.1 us
    all_gather x1, waiting for transfers between devices, on_device(): everything = lax.all_gather(sent_y, 'y', axis=0, tiled=True)  7.36 us
    select_n x2, other arithmetic, in_pair_order(): jnp.where(even, own, other)  6.12 us
    unnamed x35, local copies, waits for them, and re-layouts  5.48 us
  transfers between devices with their start and end apart: 14, of which 10 were waited for; matrix products, arithmetic and copies ran while one was open for 19% of the time, Pallas kernels for 0%

profile of v12, /device:TPU:2, one launch (start us, length us, event | category | flops | bytes accessed | tf_op | source)
XLA Modules:
  0.0 214.6 jit_solution(18233953292709831897)
XLA Ops:
  7.3 1.0 broadcast_select_fusion.7
  8.2 22.1 %all_to_all.63 = bf16[8,128,128]{2,1,0:T(8,128)(2,1)} all-to-all(bf16[8,128,128]{2,1,0:T(8,128)(2,1)S(1)} %broadcast_select_fusion.7), channel_id=1, replica_groups=mesh['y'=8,'z'=4,'pair'=2,'x'=4,'core'=2] {'z','pair'}, dimensions={0} | all-to-all | bytes 524288 | tf_op jit(solution)/shard_map/all_to_all | solution.py:19
  30.4 1.8 fusion.7
  32.2 1.3 abs_reduce_fusion
  33.9 1.0 maximum_maximum_fusion
  34.9 3.5 %all-to-all-start = ((bf16[8,144,256]{2,1,0:T(8,128)(2,1)}), bf16[8,144,256]{2,1,0:T(8,128)(2,1)S(1)}, u32[]{:S(2)}, u32[]{:S(2)}) async-start(bf16[8,144,256]{2,1,0:T(8,128)(2,1)} %maximum_maximum_fusion), calls=%async_computation | async-start | bytes 1179648 | tf_op jit(solution)/shard_map/all_to_all | solution.py:19
  38.5 1.0 constant_dynamic-slice_fusion
  39.5 3.8 %collective-permute-start = (bf16[96,4096]{1,0:T(8,128)(2,1)}, bf16[96,4096]{1,0:T(8,128)(2,1)}, u32[]{:S(2)}, u32[]{:S(2)}) collective-permute-start(bf16[96,4096]{1,0:T(8,128)(2,1)} %constant_dynamic-slice_fusion), channel_id=1, source_target_pairs={{0,8},{8,0},{1,9},{9,1},{2,10},{10,2},{3,11},{11,3},{4,12},{12,4},... | collective-permute-start | bytes 2359304 | tf_op jit(solution)/shard_map/ppermute | solution.py:92
  43.5 13.7 %all-to-all-done = bf16[8,144,256]{2,1,0:T(8,128)(2,1)S(1)} async-done(((bf16[8,144,256]{2,1,0:T(8,128)(2,1)}), bf16[8,144,256]{2,1,0:T(8,128)(2,1)S(1)}, u32[]{:S(2)}, u32[]{:S(2)}) %all-to-all-start) | async-done | bytes 589856 | tf_op jit(solution)/shard_map/all_to_all | solution.py:19
  57.2 0.9 slice.98
  58.7 0.8 reduce.11
  59.4 0.9 reshape.310
  60.3 4.8 %all-to-all-start.4 = ((bf16[8,2,6208]{2,1,0:T(2,128)(2,1)}), bf16[8,2,6208]{2,1,0:T(2,128)(2,1)S(1)}, u32[]{:S(2)}, u32[]{:S(2)}) async-start(bf16[8,2,6208]{2,1,0:T(2,128)(2,1)} %reshape.310), calls=%async_computation.4 | async-start | bytes 401408 | tf_op jit(solution)/shard_map/all_to_all | solution.py:19
  65.1 3.8 %collective-permute-done = bf16[96,4096]{1,0:T(8,128)(2,1)} collective-permute-done((bf16[96,4096]{1,0:T(8,128)(2,1)}, bf16[96,4096]{1,0:T(8,128)(2,1)}, u32[]{:S(2)}, u32[]{:S(2)}) %collective-permute-start) | collective-permute-done | bytes 786464 | tf_op jit(solution)/shard_map/ppermute | solution.py:92
  68.9 1.9 collective-permute-start.1
  73.2 0.7 reshape.308
  74.6 1.5 broadcast_select_fusion.5
  76.1 2.2 %broadcast_select_fusion.3 = (bf16[96,8192]{1,0:T(8,128)(2,1)}, bf16[96,8192]{1,0:T(8,128)(2,1)}) fusion(bf16[96,8192]{1,0:T(8,128)(2,1)S(1)} %get-tuple-element.15, pred[]{:T(512)S(6)} %and.31, bf16[96,4096]{1,0:T(8,128)(2,1)S(1)} %get-tuple-element.21, bf16[96,4096]{1,0:T(8,128)(2,1)S(1)} %get-tuple-element.20), kind=kLoop, calls=%fused_computation.31 | loop fusion | flops 4718592 | bytes 6291457 | tf_op jit(solution)/shard_map/jit(_where)/select_n | solution.py:42
  78.3 3.5 %fusion.10 = f32[192,128]{1,0:T(8,128)S(1)} fusion(bf16[8192,128]{1,0:T(8,128)(2,1)} %all-gather.4.cloned.1.call-done, bf16[96,8192]{1,0:T(8,128)(2,1)} %get-tuple-element.19, bf16[96,8192]{1,0:T(8,128)(2,1)} %get-tuple-element.18), kind=kOutput, calls=%fused_computation.13 | convolution fusion | flops 408944640 | bytes 5341184 | tf_op jit(solution)/shard_map/dot_general | solution.py:123
  82.3 7.1 %all-to-all-start.3 = ((bf16[8,2,448]{2,1,0:T(2,128)(2,1)}), bf16[8,2,448]{2,1,0:T(2,128)(2,1)S(1)}, u32[]{:S(2)}, u32[]{:S(2)}) async-start(bf16[8,2,448]{2,1,0:T(2,128)(2,1)} %reshape.308), calls=%async_computation.3 | async-start | bytes 32768 | tf_op jit(solution)/shard_map/all_to_all | solution.py:19
  89.5 8.1 %all-to-all-done.3 = bf16[8,2,448]{2,1,0:T(2,128)(2,1)S(1)} async-done(((bf16[8,2,448]{2,1,0:T(2,128)(2,1)}), bf16[8,2,448]{2,1,0:T(2,128)(2,1)S(1)}, u32[]{:S(2)}, u32[]{:S(2)}) %all-to-all-start.3) | async-done | bytes 14368 | tf_op jit(solution)/shard_map/all_to_all | solution.py:19
  97.6 0.8 broadcast_in_dim.124
  98.4 5.8 %all-to-all-start.2 = ((bf16[8,192,128]{2,1,0:T(8,128)(2,1)}), bf16[8,192,128]{2,1,0:T(8,128)(2,1)S(1)}, u32[]{:S(2)}, u32[]{:S(2)}) async-start(bf16[8,192,128]{2,1,0:T(8,128)(2,1)} %broadcast_in_dim.124), calls=%async_computation.2 | async-start | bytes 786432 | tf_op jit(solution)/shard_map/all_to_all | solution.py:19
  104.2 1.1 multiply_cosine_fusion
  105.8 12.2 %all-to-all-done.2 = bf16[8,192,128]{2,1,0:T(8,128)(2,1)S(1)} async-done(((bf16[8,192,128]{2,1,0:T(8,128)(2,1)}), bf16[8,192,128]{2,1,0:T(8,128)(2,1)S(1)}, u32[]{:S(2)}, u32[]{:S(2)}) %all-to-all-start.2) | async-done | bytes 393248 | tf_op jit(solution)/shard_map/all_to_all | solution.py:19
  119.3 0.8 pad_maximum_fusion.1
  120.7 3.3 %all-to-all-start.5 = ((f32[8,1,768]{2,1,0:T(1,128)}), f32[8,1,768]{2,1,0:T(1,128)S(1)}, u32[]{:S(2)}, u32[]{:S(2)}) async-start(f32[8,1,768]{2,1,0:T(1,128)} %broadcast_in_dim.128), calls=%async_computation.5 | async-start | bytes 49152 | tf_op jit(solution)/shard_map/all_to_all | solution.py:19
  124.1 7.8 %all-to-all-done.5 = f32[8,1,768]{2,1,0:T(1,128)S(1)} async-done(((f32[8,1,768]{2,1,0:T(1,128)}), f32[8,1,768]{2,1,0:T(1,128)S(1)}, u32[]{:S(2)}, u32[]{:S(2)}) %all-to-all-start.5) | async-done | bytes 24608 | tf_op jit(solution)/shard_map/all_to_all | solution.py:19
  132.6 3.3 %all-to-all-start.6 = ((f32[8,1,768]{2,1,0:T(1,128)}), f32[8,1,768]{2,1,0:T(1,128)S(1)}, u32[]{:S(2)}, u32[]{:S(2)}) async-start(f32[8,1,768]{2,1,0:T(1,128)} %broadcast_in_dim.129), calls=%async_computation.6 | async-start | bytes 49152 | tf_op jit(solution)/shard_map/all_to_all | solution.py:19
  135.9 1.0 fusion.19
  137.0 6.8 %all-to-all-done.6 = f32[8,1,768]{2,1,0:T(1,128)S(1)} async-done(((f32[8,1,768]{2,1,0:T(1,128)}), f32[8,1,768]{2,1,0:T(1,128)S(1)}, u32[]{:S(2)}, u32[]{:S(2)}) %all-to-all-start.6) | async-done | bytes 24608 | tf_op jit(solution)/shard_map/all_to_all | solution.py:19
  144.5 4.8 %all-to-all-start.7 = ((f32[8,1,768]{2,1,0:T(1,128)}), f32[8,1,768]{2,1,0:T(1,128)S(1)}, u32[]{:S(2)}, u32[]{:S(2)}) async-start(f32[8,1,768]{2,1,0:T(1,128)} %broadcast_in_dim.130), calls=%async_computation.7 | async-start | bytes 49152 | tf_op jit(solution)/shard_map/all_to_all | solution.py:19
  149.3 1.3 dynamic-slice_divide_fusion
  150.6 2.7 %all-to-all-done.7 = f32[8,1,768]{2,1,0:T(1,128)S(1)} async-done(((f32[8,1,768]{2,1,0:T(1,128)}), f32[8,1,768]{2,1,0:T(1,128)S(1)}, u32[]{:S(2)}, u32[]{:S(2)}) %all-to-all-start.7) | async-done | bytes 24608 | tf_op jit(solution)/shard_map/all_to_all | solution.py:19
  154.4 3.9 %broadcast_select_fusion.1 = (bf16[96,8192]{1,0:T(8,128)(2,1)}, bf16[96,8192]{1,0:T(8,128)(2,1)}) fusion(bf16[96,8192]{1,0:T(8,128)(2,1)} %copy-done, pred[]{:T(512)S(6)} %and.32, bf16[96,4096]{1,0:T(8,128)(2,1)} %copy-done.1, bf16[96,4096]{1,0:T(8,128)(2,1)S(1)} %get-tuple-element.20), kind=kLoop, calls=%fused_computation.29 | loop fusion | flops 4718592 | bytes 6291457 | tf_op jit(solution)/shard_map/jit(_where)/select_n | solution.py:42
  158.3 4.2 %fusion.14 = f32[192,256]{1,0:T(8,128)S(1)} fusion(bf16[8192,256]{1,0:T(8,128)(2,1)} %all-gather.8.cloned.1.call-done, bf16[96,8192]{1,0:T(8,128)(2,1)} %get-tuple-element.17, bf16[96,8192]{1,0:T(8,128)(2,1)} %get-tuple-element.16), kind=kOutput, calls=%fused_computation.17 | convolution fusion | flops 811597824 | bytes 7536640 | tf_op jit(solution)/shard_map/dot_general | solution.py:171
  163.4 2.6 %collective-permute-start.2 = (bf16[96,256]{1,0:T(8,128)(2,1)S(1)}, bf16[96,256]{1,0:T(8,128)(2,1)S(1)}, u32[]{:S(2)}, u32[]{:S(2)}) collective-permute-start(bf16[96,256]{1,0:T(8,128)(2,1)S(1)} %bitcast.141), channel_id=1, source_target_pairs={{0,8},{8,0},{1,9},{9,1},{2,10},{10,2},{3,11},{11,3},{4,12},{12,4},... | collective-permute-start | bytes 147464 | tf_op jit(solution)/shard_map/ppermute | solution.py:175
  167.1 2.3 %collective-permute-done.2 = bf16[96,256]{1,0:T(8,128)(2,1)S(1)} collective-permute-done((bf16[96,256]{1,0:T(8,128)(2,1)S(1)}, bf16[96,256]{1,0:T(8,128)(2,1)S(1)}, u32[]{:S(2)}, u32[]{:S(2)}) %collective-permute-start.2) | collective-permute-done | bytes 49184 | tf_op jit(solution)/shard_map/ppermute | solution.py:175
  169.4 7.4 %all-gather.6.cloned.1.call-done = bf16[6144,256]{1,0:T(8,128)(2,1)} async-done(((bf16[768,256]{1,0:T(8,128)(2,1)}), bf16[6144,256]{1,0:T(8,128)(2,1)}) %all-gather.6.cloned.1.call-update) | async-done | bytes 3145744 | tf_op jit(solution)/shard_map/all_gather | solution.py:131
  176.8 2.9 %fusion.48 = (f32[4,96]{1,0:T(4,128)S(1)}, f32[1,4,96,6144]{3,2,1,0:T(8,128)S(1)}) fusion(f32[96,6144]{1,0:T(8,128)S(1)} %fusion.19, bf16[6144,256]{1,0:T(8,128)(2,1)} %all-gather.6.cloned.1.call-done, bf16[96,256]{1,0:T(8,128)(2,1)S(1)} %get-tuple-element.33, bf16[96,256]{1,0:T(8,128)(2,1)S(1)} %get-tuple-element.32), kind=kOutput, calls=%fused_computation.107 | convolution fusion | flops 608894592 | bytes 13469184 | tf_op jit(solution)/shard_map/tkgd,skd->kgts/dot_general | solution.py:181
  179.7 1.7 fusion
  181.6 1.6 abs_reduce_fusion.3
  183.2 0.7 broadcast_in_dim.133
  183.9 10.9 %all-to-all-start.8 = ((f32[64,1,512]{2,1,0:T(1,128)}), f32[64,1,512]{2,1,0:T(1,128)S(1)}, u32[]{:S(2)}, u32[]{:S(2)}) async-start(f32[64,1,512]{2,1,0:T(1,128)} %broadcast_in_dim.133), calls=%async_computation.8 | async-start | bytes 262144 | tf_op jit(solution)/shard_map/all_to_all | solution.py:19
  194.9 0.9 copy.54
  197.1 0.7 copy.73
  197.8 9.6 %all-to-all-done.8 = f32[64,1,512]{2,1,0:T(1,128)S(1)} async-done(((f32[64,1,512]{2,1,0:T(1,128)}), f32[64,1,512]{2,1,0:T(1,128)S(1)}, u32[]{:S(2)}, u32[]{:S(2)}) %all-to-all-start.8) | async-done | bytes 131104 | tf_op jit(solution)/shard_map/all_to_all | solution.py:19
  207.4 0.7 reduce_max.109
  (99 shorter events, 11.3 us)
Async XLA Ops:
  7.2 25.0 %copy-start.2 = (bf16[96,8192]{1,0:T(8,128)(2,1)S(1)}, bf16[96,8192]{1,0:T(8,128)(2,1)}, u32[]{:S(2)}) copy-start(bf16[96,8192]{1,0:T(8,128)(2,1)} %param.6) | copy-start | bytes 4718596
  7.2 26.4 %copy-start.9 = (s32[96]{0:T(128)S(1)}, s32[96]{0:T(128)}, u32[]{:S(2)}) copy-start(s32[96]{0:T(128)} %param.11) | copy-start | bytes 1156
  7.2 26.5 %copy-start.4 = (bf16[128,512]{1,0:T(8,128)(2,1)S(1)}, bf16[128,512]{1,0:T(8,128)(2,1)}, u32[]{:S(2)}) copy-start(bf16[128,512]{1,0:T(8,128)(2,1)} %param.8) | copy-start | bytes 393220
  7.2 71.1 %all-gather.4.cloned.1.call-start = ((), (), s32[]{:S(2)}) async-start(), calls=%async_computation.9 | async-start | bytes 2359296 | tf_op jit(solution)/shard_map/all_gather | solution.py:84
  33.5 42.6 %copy-start = (bf16[96,8192]{1,0:T(8,128)(2,1)}, bf16[96,8192]{1,0:T(8,128)(2,1)S(1)}, u32[]{:S(2)}) copy-start(bf16[96,8192]{1,0:T(8,128)(2,1)S(1)} %get-tuple-element.15) | copy-start | bytes 4718596
  33.5 9.7 %copy-start.7 = (bf16[128,128]{1,0:T(8,128)(2,1)S(1)}, bf16[128,128]{1,0:T(8,128)(2,1)}, u32[]{:S(2)}) copy-start(bf16[128,128]{1,0:T(8,128)(2,1)} %param.9) | copy-start | bytes 98308
  33.5 9.7 %copy-start.8 = (bf16[128,128]{1,0:T(8,128)(2,1)S(1)}, bf16[128,128]{1,0:T(8,128)(2,1)}, u32[]{:S(2)}) copy-start(bf16[128,128]{1,0:T(8,128)(2,1)} %param.10) | copy-start | bytes 98308
  34.9 22.3 %all-to-all-start = ((bf16[8,144,256]{2,1,0:T(8,128)(2,1)}), bf16[8,144,256]{2,1,0:T(8,128)(2,1)S(1)}, u32[]{:S(2)}, u32[]{:S(2)}) async-start(bf16[8,144,256]{2,1,0:T(8,128)(2,1)} %maximum_maximum_fusion), calls=%async_computation | async-start | bytes 1179648 | tf_op jit(solution)/shard_map/all_to_all | solution.py:19
  38.4 119.9 %all-gather.8.cloned.1.call-start = ((), (), s32[]{:S(2)}) async-start(), calls=%async_computation.11 | async-start | bytes 4718592 | tf_op jit(solution)/shard_map/all_gather | solution.py:104
  39.5 29.4 %collective-permute-start = (bf16[96,4096]{1,0:T(8,128)(2,1)}, bf16[96,4096]{1,0:T(8,128)(2,1)}, u32[]{:S(2)}, u32[]{:S(2)}) collective-permute-start(bf16[96,4096]{1,0:T(8,128)(2,1)} %constant_dynamic-slice_fusion), channel_id=1, source_target_pairs={{0,8},{8,0},{1,9},{9,1},{2,10},{10,2},{3,11},{11,3},{4,12},{12,4},... | collective-permute-start | bytes 2359304 | tf_op jit(solution)/shard_map/ppermute | solution.py:92
  60.3 22.0 %all-to-all-start.4 = ((bf16[8,2,6208]{2,1,0:T(2,128)(2,1)}), bf16[8,2,6208]{2,1,0:T(2,128)(2,1)S(1)}, u32[]{:S(2)}, u32[]{:S(2)}) async-start(bf16[8,2,6208]{2,1,0:T(2,128)(2,1)} %reshape.310), calls=%async_computation.4 | async-start | bytes 401408 | tf_op jit(solution)/shard_map/all_to_all | solution.py:19
  68.9 5.7 %collective-permute-start.1 = (bf16[96,4096]{1,0:T(8,128)(2,1)}, bf16[96,4096]{1,0:T(8,128)(2,1)}, u32[]{:S(2)}, u32[]{:S(2)}) collective-permute-start(bf16[96,4096]{1,0:T(8,128)(2,1)} %collective-permute-done), channel_id=1, source_target_pairs={{0,1},{1,0},{2,3},{3,2},{4,5},{5,4},{6,7},{7,6},{8,9},{9,8},{10,11... | collective-permute-start | bytes 2359304 | tf_op jit(solution)/shard_map/ppermute | solution.py:114
  76.1 29.4 %copy-start.1 = (bf16[96,4096]{1,0:T(8,128)(2,1)}, bf16[96,4096]{1,0:T(8,128)(2,1)S(1)}, u32[]{:S(2)}) copy-start(bf16[96,4096]{1,0:T(8,128)(2,1)S(1)} %get-tuple-element.21) | copy-start | bytes 2359300
  82.3 15.3 %all-to-all-start.3 = ((bf16[8,2,448]{2,1,0:T(2,128)(2,1)}), bf16[8,2,448]{2,1,0:T(2,128)(2,1)S(1)}, u32[]{:S(2)}, u32[]{:S(2)}) async-start(bf16[8,2,448]{2,1,0:T(2,128)(2,1)} %reshape.308), calls=%async_computation.3 | async-start | bytes 32768 | tf_op jit(solution)/shard_map/all_to_all | solution.py:19
  98.4 19.7 %all-to-all-start.2 = ((bf16[8,192,128]{2,1,0:T(8,128)(2,1)}), bf16[8,192,128]{2,1,0:T(8,128)(2,1)S(1)}, u32[]{:S(2)}, u32[]{:S(2)}) async-start(bf16[8,192,128]{2,1,0:T(8,128)(2,1)} %broadcast_in_dim.124), calls=%async_computation.2 | async-start | bytes 786432 | tf_op jit(solution)/shard_map/all_to_all | solution.py:19
  104.1 72.7 %all-gather.6.cloned.1.call-start = ((), (), s32[]{:S(2)}) async-start(), calls=%async_computation.10 | async-start | bytes 3538944 | tf_op jit(solution)/shard_map/all_gather | solution.py:131
  120.7 11.2 %all-to-all-start.5 = ((f32[8,1,768]{2,1,0:T(1,128)}), f32[8,1,768]{2,1,0:T(1,128)S(1)}, u32[]{:S(2)}, u32[]{:S(2)}) async-start(f32[8,1,768]{2,1,0:T(1,128)} %broadcast_in_dim.128), calls=%async_computation.5 | async-start | bytes 49152 | tf_op jit(solution)/shard_map/all_to_all | solution.py:19
  132.6 11.2 %all-to-all-start.6 = ((f32[8,1,768]{2,1,0:T(1,128)}), f32[8,1,768]{2,1,0:T(1,128)S(1)}, u32[]{:S(2)}, u32[]{:S(2)}) async-start(f32[8,1,768]{2,1,0:T(1,128)} %broadcast_in_dim.129), calls=%async_computation.6 | async-start | bytes 49152 | tf_op jit(solution)/shard_map/all_to_all | solution.py:19
  144.5 8.8 %all-to-all-start.7 = ((f32[8,1,768]{2,1,0:T(1,128)}), f32[8,1,768]{2,1,0:T(1,128)S(1)}, u32[]{:S(2)}, u32[]{:S(2)}) async-start(f32[8,1,768]{2,1,0:T(1,128)} %broadcast_in_dim.130), calls=%async_computation.7 | async-start | bytes 49152 | tf_op jit(solution)/shard_map/all_to_all | solution.py:19
  158.3 4.4 %copy-start.5 = (f32[192,64]{1,0:T(8,128)S(1)}, f32[192,64]{1,0:T(8,128)}, u32[]{:S(2)}) copy-start(f32[192,64]{1,0:T(8,128)} %get-tuple-element.36) | copy-start | bytes 147460
  158.3 4.4 %copy-start.6 = (f32[192,64]{1,0:T(8,128)S(1)}, f32[192,64]{1,0:T(8,128)}, u32[]{:S(2)}) copy-start(f32[192,64]{1,0:T(8,128)} %get-tuple-element.37) | copy-start | bytes 147460
  163.4 6.0 %collective-permute-start.2 = (bf16[96,256]{1,0:T(8,128)(2,1)S(1)}, bf16[96,256]{1,0:T(8,128)(2,1)S(1)}, u32[]{:S(2)}, u32[]{:S(2)}) collective-permute-start(bf16[96,256]{1,0:T(8,128)(2,1)S(1)} %bitcast.141), channel_id=1, source_target_pairs={{0,8},{8,0},{1,9},{9,1},{2,10},{10,2},{3,11},{11,3},{4,12},{12,4},... | collective-permute-start | bytes 147464 | tf_op jit(solution)/shard_map/ppermute | solution.py:175
  179.7 1.9 copy-start.3
  183.9 23.5 %all-to-all-start.8 = ((f32[64,1,512]{2,1,0:T(1,128)}), f32[64,1,512]{2,1,0:T(1,128)S(1)}, u32[]{:S(2)}, u32[]{:S(2)}) async-start(f32[64,1,512]{2,1,0:T(1,128)} %broadcast_in_dim.133), calls=%async_computation.8 | async-start | bytes 262144 | tf_op jit(solution)/shard_map/all_to_all | solution.py:19
Sparse Core Ops, SparseCore 0:
  30.5 39.6 all-gather.3
  72.2 55.8 all-gather.7
  130.2 46.5 all-gather.5
